TPU v7x, 32 devices: a whole 2x2x4 slice. The times are simulated.
32 devices in a mesh: gz: 8 (over z, x), gx: 4 (over y, core).
Axes of the slice: x: 2, y: 2, z: 4, core: 2. Of those that a mesh axis runs over, the one named last changes fastest.
Arguments:
- noisy_volume: float32 [32, 512, 512], P('gz', 'gx'), may hold values from -3 to 3, as said below
- tv_weight: float32 [32, 512, 512], P('gz', 'gx'), may hold values from 0.05 to 0.5
Outputs:
- denoised: float32 [32, 512, 512], P('gz', 'gx')
- gap_values: float32 [4], replicated
- step_values: float32 [4], replicated
Inputs may be any that keep to these rules, and one draw needn't show every extreme that they name: `noisy_volume`: voxel intensities.
All inputs are finite; a program needn't handle non-finite values.
Results may differ from a plain program's by a relative error of at most 0.0001.
Values sent between devices are 32-bit elements; how exact they have to be, the bound alone decides.
No kernel may reach another device: no remote copies, remote signals or barrier semaphores. Data moves between devices by JAX's collectives and lax.ppermute only.
A program may use at most 64 MiB of HBM per device.

v0:
```python
import jax
import jax.numpy as jnp
from jax import lax
from jax.sharding import PartitionSpec as P

ITERS = 4


primal_step = 0.28
dual_step = 0.28


def shifted_2(value, axis, steps):
    count = lax.axis_size(axis)
    initial, last = (max(0, -steps), min(count, count - steps))
    return lax.ppermute(value, axis, [(source, source + steps) for source in range(initial, last)])


def gradient(volume, next_plane, next_row, keep_plane, keep_row):
    along_z = (jnp.concatenate([volume[1:], next_plane], axis=0) - volume) * keep_plane
    along_x = (jnp.concatenate([volume[:, 1:], next_row], axis=1) - volume) * keep_row
    along_y = jnp.concatenate(
        [volume[:, :, 1:] - volume[:, :, :-1], jnp.zeros_like(volume[:, :, :1])], axis=2
    )
    return (along_z, along_x, along_y)


def divergence(dual_field, prev_plane, prev_row):
    dual_z, dual_x, dual_y = dual_field
    back_z = dual_z - jnp.concatenate([prev_plane, dual_z[:-1]], axis=0)
    back_x = dual_x - jnp.concatenate([prev_row, dual_x[:, :-1]], axis=1)
    back_y = dual_y - jnp.concatenate([jnp.zeros_like(dual_y[:, :, :1]), dual_y[:, :, :-1]], axis=2)
    return back_z + back_x + back_y


def shards(noisy_volume, tv_weight):
    planes_dev, rows_dev, cols_dev = noisy_volume.shape
    cell_count = planes_dev * rows_dev * cols_dev * lax.axis_size("gz") * lax.axis_size("gx")
    last_slab = lax.axis_index("gz") == lax.axis_size("gz") - 1
    last_block = lax.axis_index("gx") == lax.axis_size("gx") - 1
    plane_ids = lax.iota(jnp.int32, planes_dev)
    row_ids = lax.iota(jnp.int32, rows_dev)
    keep_plane = (
        jnp.where(jnp.logical_or(plane_ids < planes_dev - 1, jnp.logical_not(last_slab)), 1.0, 0.0)
        .astype(jnp.float32)
        .reshape(planes_dev, 1, 1)
    )
    keep_row = (
        jnp.where(jnp.logical_or(row_ids < rows_dev - 1, jnp.logical_not(last_block)), 1.0, 0.0)
        .astype(jnp.float32)
        .reshape(1, rows_dev, 1)
    )
    primal = noisy_volume
    extrapolated = noisy_volume
    zeros_field = jnp.zeros_like(noisy_volume)
    dual_field = (zeros_field, zeros_field, zeros_field)
    grad_primal = None
    gap_list = []
    step_list = []
    for iteration in range(ITERS):
        next_planes = shifted_2((primal[:1], extrapolated[:1]), "gz", -1)
        next_rows = shifted_2((primal[:, :1], extrapolated[:, :1]), "gx", -1)
        grad_primal = gradient(primal, next_planes[0], next_rows[0], keep_plane, keep_row)
        grad_extra = gradient(extrapolated, next_planes[1], next_rows[1], keep_plane, keep_row)
        proposed = tuple(
            (
                dual_part + dual_step * grad_part
                for dual_part, grad_part in zip(dual_field, grad_extra)
            )
        )
        magnitude = jnp.sqrt(
            proposed[0] * proposed[0] + proposed[1] * proposed[1] + proposed[2] * proposed[2]
        )
        shrink = tv_weight / jnp.maximum(tv_weight, magnitude)
        dual_field = tuple((part * shrink for part in proposed))
        prev_plane = shifted_2(dual_field[0][-1:], "gz", 1)
        prev_row = shifted_2(dual_field[1][:, -1:], "gx", 1)
        spread = divergence(dual_field, prev_plane, prev_row)
        updated = (primal + primal_step * (spread + noisy_volume)) / (1.0 + primal_step)
        total_var = jnp.sqrt(
            grad_primal[0] * grad_primal[0]
            + grad_primal[1] * grad_primal[1]
            + grad_primal[2] * grad_primal[2]
        )
        misfit = primal - noisy_volume
        shifted = noisy_volume + spread
        gap_terms = (
            0.5 * misfit * misfit
            + tv_weight * total_var
            - 0.5 * noisy_volume * noisy_volume
            + 0.5 * shifted * shifted
        )
        change = updated - primal
        gap_part = jnp.sum(gap_terms)
        step_part = jnp.sum(change * change)
        gap_list.append(gap_part)
        step_list.append(step_part)
        extrapolated = 2.0 * updated - primal
        primal = updated
    gap_total, step_total = lax.psum((jnp.stack(gap_list), jnp.stack(step_list)), ("gz", "gx"))
    gap_values = gap_total / cell_count
    step_values = jnp.sqrt(step_total / cell_count)
    return (primal, gap_values, step_values)


def solution(mesh):
    placed = (P("gz", "gx", None), P("gz", "gx", None))
    return jax.shard_map(
        shards,
        mesh=mesh,
        in_specs=placed,
        out_specs=(P("gz", "gx", None), P(), P()),
        check_vma=False,
    )
```

profile of v0, /device:TPU:0, one launch (start us, length us, event | category | flops | bytes accessed | tf_op | source)
XLA Modules:
  0.0 154.7 jit_solution(10416529285463513435)
XLA Ops:
  1.6 1.3 collective-permute-start
  3.8 1.4 collective-permute-start.1
  5.2 1.9 %slice_subtract_fusion.6 = f32[4,128,511]{2,1,0:T(8,128)S(1)} fusion(f32[4,128,512]{2,1,0:T(8,128)} %param.2), kind=kLoop, calls=%fused_computation.127 | loop fusion | flops 261632 | bytes 3139584 | tf_op jit(solution)/shard_map/sub | solution.py:23
  7.4 5.4 %collective-permute-done = f32[1,128,512]{2,1,0:T(8,128)S(1)} collective-permute-done((f32[1,128,512]{2,1,0:T(8,128)S(1)}, f32[1,128,512]{2,1,0:T(8,128)S(1)}, u32[]{:S(2)}, u32[]{:S(2)}) %collective-permute-start) | collective-permute-done | bytes 262176 | tf_op jit(solution)/shard_map/ppermute | solution.py:16
  14.3 4.6 %collective-permute-start.2 = (f32[1,128,512]{2,1,0:T(8,128)S(1)}, f32[1,128,512]{2,1,0:T(8,128)S(1)}, u32[]{:S(2)}, u32[]{:S(2)}) collective-permute-start(f32[1,128,512]{2,1,0:T(8,128)S(1)} %slice.254), channel_id=1, source_target_pairs={{0,4},{4,8},{8,12},{12,16},{16,20},{20,24},{24,28},{1,5},{5,9},{9,... | collective-permute-start | bytes 786440 | tf_op jit(solution)/shard_map/ppermute | solution.py:16
  21.0 2.5 %collective-permute-done.2 = f32[1,128,512]{2,1,0:T(8,128)S(1)} collective-permute-done((f32[1,128,512]{2,1,0:T(8,128)S(1)}, f32[1,128,512]{2,1,0:T(8,128)S(1)}, u32[]{:S(2)}, u32[]{:S(2)}) %collective-permute-start.2) | collective-permute-done | bytes 262176 | tf_op jit(solution)/shard_map/ppermute | solution.py:16
  24.5 1.3 collective-permute-start.4
  25.8 1.3 collective-permute-start.5
  28.0 1.3 collective-permute-start.16
  29.3 1.3 collective-permute-start.17
  30.6 3.7 %collective-permute-done.4 = f32[1,128,512]{2,1,0:T(8,128)S(1)} collective-permute-done((f32[1,128,512]{2,1,0:T(8,128)S(1)}, f32[1,128,512]{2,1,0:T(8,128)S(1)}, u32[]{:S(2)}, u32[]{:S(2)}) %collective-permute-start.4) | collective-permute-done | bytes 262176 | tf_op jit(solution)/shard_map/ppermute | solution.py:16
  35.9 4.8 %collective-permute-start.6 = (f32[1,128,512]{2,1,0:T(8,128)S(1)}, f32[1,128,512]{2,1,0:T(8,128)S(1)}, u32[]{:S(2)}, u32[]{:S(2)}) collective-permute-start(f32[1,128,512]{2,1,0:T(8,128)S(1)} %slice.265), channel_id=1, source_target_pairs={{0,4},{4,8},{8,12},{12,16},{16,20},{20,24},{24,28},{1,5},{5,9},{9,... | collective-permute-start | bytes 786440 | tf_op jit(solution)/shard_map/ppermute | solution.py:16
  42.8 3.3 %collective-permute-done.6 = f32[1,128,512]{2,1,0:T(8,128)S(1)} collective-permute-done((f32[1,128,512]{2,1,0:T(8,128)S(1)}, f32[1,128,512]{2,1,0:T(8,128)S(1)}, u32[]{:S(2)}, u32[]{:S(2)}) %collective-permute-start.6) | collective-permute-done | bytes 262176 | tf_op jit(solution)/shard_map/ppermute | solution.py:16
  46.2 5.0 %fusion.3 = (f32[]{:T(128)}, f32[]{:T(128)}, f32[]{:T(128)}, f32[]{:T(128)}, f32[4,128,512]{2,1,0:T(8,128)S(1)}, /*index=5*/f32[4,128,512]{2,1,0:T(8,128)S(1)}) fusion(f32[4,128,512]{2,1,0:T(8,128)S(1)} %get-tuple-element.31, f32[4,128,512]{2,1,0:T(8,128)S(1)} %copy-done.4, f32[4,128,512]{2,1,0:T(8,128)S(1)} %copy-done, ...), kind=kLoop, calls=%fused_computation.16 | loop fusion | flops 15728636 | bytes 18868768 | tf_op jit(solution)/shard_map/reduce_sum | solution.py:94
  51.5 1.3 collective-permute-start.8
  52.8 1.3 collective-permute-start.9
  55.8 5.6 %collective-permute-done.8 = f32[1,128,512]{2,1,0:T(8,128)S(1)} collective-permute-done((f32[1,128,512]{2,1,0:T(8,128)S(1)}, f32[1,128,512]{2,1,0:T(8,128)S(1)}, u32[]{:S(2)}, u32[]{:S(2)}) %collective-permute-start.8) | collective-permute-done | bytes 262176 | tf_op jit(solution)/shard_map/ppermute | solution.py:16
  63.1 5.0 %collective-permute-start.10 = (f32[1,128,512]{2,1,0:T(8,128)S(1)}, f32[1,128,512]{2,1,0:T(8,128)S(1)}, u32[]{:S(2)}, u32[]{:S(2)}) collective-permute-start(f32[1,128,512]{2,1,0:T(8,128)S(1)} %slice.276), channel_id=1, source_target_pairs={{0,4},{4,8},{8,12},{12,16},{16,20},{20,24},{24,28},{1,5},{5,9},{9,... | collective-permute-start | bytes 786440 | tf_op jit(solution)/shard_map/ppermute | solution.py:16
  68.1 1.5 collective-permute-start.11
  70.2 1.3 collective-permute-start.18
  71.5 1.3 collective-permute-start.19
  74.0 1.3 collective-permute-start.12
  75.3 1.3 collective-permute-start.13
  77.4 1.3 collective-permute-start.20
  78.7 2.2 %collective-permute-done.13 = f32[4,1,512]{2,1,0:T(1,128)S(1)} collective-permute-done((f32[4,1,512]{2,1,0:T(1,128)S(1)}, f32[4,1,512]{2,1,0:T(1,128)S(1)}, u32[]{:S(2)}, u32[]{:S(2)}) %collective-permute-start.13) | collective-permute-done | bytes 8224 | tf_op jit(solution)/shard_map/ppermute | solution.py:16
  82.2 4.0 %collective-permute-done.12 = f32[1,128,512]{2,1,0:T(8,128)S(1)} collective-permute-done((f32[1,128,512]{2,1,0:T(8,128)S(1)}, f32[1,128,512]{2,1,0:T(8,128)S(1)}, u32[]{:S(2)}, u32[]{:S(2)}) %collective-permute-start.12) | collective-permute-done | bytes 262176 | tf_op jit(solution)/shard_map/ppermute | solution.py:16
  87.7 4.8 %collective-permute-start.14 = (f32[1,128,512]{2,1,0:T(8,128)S(1)}, f32[1,128,512]{2,1,0:T(8,128)S(1)}, u32[]{:S(2)}, u32[]{:S(2)}) collective-permute-start(f32[1,128,512]{2,1,0:T(8,128)S(1)} %slice.287), channel_id=1, source_target_pairs={{0,4},{4,8},{8,12},{12,16},{16,20},{20,24},{24,28},{1,5},{5,9},{9,... | collective-permute-start | bytes 786440 | tf_op jit(solution)/shard_map/ppermute | solution.py:16
  92.6 4.1 %collective-permute-start.15 = (f32[4,1,512]{2,1,0:T(1,128)S(1)}, f32[4,1,512]{2,1,0:T(1,128)S(1)}, u32[]{:S(2)}, u32[]{:S(2)}) collective-permute-start(f32[4,1,512]{2,1,0:T(1,128)S(1)} %slice.289), channel_id=1, source_target_pairs={{0,1},{1,2},{2,3},{4,5},{5,6},{6,7},{8,9},{9,10},{10,11},{12,13},{... | collective-permute-start | bytes 24584 | tf_op jit(solution)/shard_map/ppermute | solution.py:16
  98.4 5.7 %fusion.11 = (f32[]{:T(128)}, f32[]{:T(128)}, f32[]{:T(128)}, f32[]{:T(128)}, f32[4,128,512]{2,1,0:T(8,128)}) fusion(f32[4,128,512]{2,1,0:T(8,128)S(1)} %get-tuple-element.21, f32[4,128,512]{2,1,0:T(8,128)S(1)} %copy-done.4, f32[4,128,512]{2,1,0:T(8,128)S(1)} %get-tuple-element.13, f32[1,128,512]{2,1,0:T(8,128)S(1)} %collective-permute-done.18, ...), kind=kLoop, calls=%fused_computation.24 | loop fusion | flops 15990780 | bytes 18868768 | tf_op jit(solution)/shard_map/reduce_sum | solution.py:94
  104.1 2.7 %pad_maximum_fusion.1 = f32[4]{0:T(128)S(1)} fusion(f32[1]{0:T(128)} %bitcast.7, f32[1]{0:T(128)} %bitcast.6, f32[1]{0:T(128)} %bitcast.5, f32[1]{0:T(128)} %bitcast.4), kind=kLoop, calls=%fused_computation.140 | loop fusion | flops 12 | bytes 32 | tf_op jit(solution)/shard_map/stack | solution.py:100
  106.8 2.6 %pad_maximum_fusion = f32[4]{0:T(128)S(1)} fusion(f32[1]{0:T(128)} %bitcast.3, f32[1]{0:T(128)} %bitcast.2, f32[1]{0:T(128)} %bitcast.1, f32[1]{0:T(128)} %bitcast), kind=kLoop, calls=%fused_computation.139 | loop fusion | flops 12 | bytes 32 | tf_op jit(solution)/shard_map/stack | solution.py:100
  109.3 44.9 %all-reduce.11 = (f32[4]{0:T(128)S(1)}, f32[4]{0:T(128)S(1)}) all-reduce(f32[4]{0:T(128)S(1)} %pad_maximum_fusion, f32[4]{0:T(128)S(1)} %pad_maximum_fusion.1), channel_id=1, replica_groups=mesh['gz'=8,'gx'=4] {'gz','gx'}, use_global_device_ids=true, to_apply=%region_4.5 | all-reduce | flops 8 | bytes 64 | tf_op jit(solution)/shard_map/psum | solution.py:100
  (92 shorter events, 22.1 us)
Async XLA Ops:
  1.6 11.2 %collective-permute-start = (f32[1,128,512]{2,1,0:T(8,128)S(1)}, f32[1,128,512]{2,1,0:T(8,128)S(1)}, u32[]{:S(2)}, u32[]{:S(2)}) collective-permute-start(f32[1,128,512]{2,1,0:T(8,128)S(1)} %slice.193), channel_id=1, source_target_pairs={{4,0},{8,4},{12,8},{16,12},{20,16},{24,20},{28,24},{5,1},{9,5},{13... | collective-permute-start | bytes 786440 | tf_op jit(solution)/shard_map/ppermute | solution.py:16
  3.8 3.4 %copy-start = (f32[4,128,512]{2,1,0:T(8,128)S(1)}, f32[4,128,512]{2,1,0:T(8,128)}, u32[]{:S(2)}) copy-start(f32[4,128,512]{2,1,0:T(8,128)} %param.2) | copy-start | bytes 3145732
  3.8 3.6 %collective-permute-start.1 = (f32[4,1,512]{2,1,0:T(1,128)S(1)}, f32[4,1,512]{2,1,0:T(1,128)S(1)}, u32[]{:S(2)}, u32[]{:S(2)}) collective-permute-start(f32[4,1,512]{2,1,0:T(1,128)S(1)} %slice.195), channel_id=1, source_target_pairs={{1,0},{2,1},{3,2},{5,4},{6,5},{7,6},{9,8},{10,9},{11,10},{13,12},{... | collective-permute-start | bytes 24584 | tf_op jit(solution)/shard_map/ppermute | solution.py:16
  7.3 5.5 %copy-start.4 = (f32[4,128,512]{2,1,0:T(8,128)S(1)}, f32[4,128,512]{2,1,0:T(8,128)}, u32[]{:S(2)}) copy-start(f32[4,128,512]{2,1,0:T(8,128)} %param.3) | copy-start | bytes 3145732
  14.3 9.2 %collective-permute-start.2 = (f32[1,128,512]{2,1,0:T(8,128)S(1)}, f32[1,128,512]{2,1,0:T(8,128)S(1)}, u32[]{:S(2)}, u32[]{:S(2)}) collective-permute-start(f32[1,128,512]{2,1,0:T(8,128)S(1)} %slice.254), channel_id=1, source_target_pairs={{0,4},{4,8},{8,12},{12,16},{16,20},{20,24},{24,28},{1,5},{5,9},{9,... | collective-permute-start | bytes 786440 | tf_op jit(solution)/shard_map/ppermute | solution.py:16
  18.9 2.1 %collective-permute-start.3 = (f32[4,1,512]{2,1,0:T(1,128)S(1)}, f32[4,1,512]{2,1,0:T(1,128)S(1)}, u32[]{:S(2)}, u32[]{:S(2)}) collective-permute-start(f32[4,1,512]{2,1,0:T(1,128)S(1)} %slice.256), channel_id=1, source_target_pairs={{0,1},{1,2},{2,3},{4,5},{5,6},{6,7},{8,9},{9,10},{10,11},{12,13},{... | collective-permute-start | bytes 24584 | tf_op jit(solution)/shard_map/ppermute | solution.py:16
  24.5 9.8 %collective-permute-start.4 = (f32[1,128,512]{2,1,0:T(8,128)S(1)}, f32[1,128,512]{2,1,0:T(8,128)S(1)}, u32[]{:S(2)}, u32[]{:S(2)}) collective-permute-start(f32[1,128,512]{2,1,0:T(8,128)S(1)} %slice.260), channel_id=1, source_target_pairs={{4,0},{8,4},{12,8},{16,12},{20,16},{24,20},{28,24},{5,1},{9,5},{13... | collective-permute-start | bytes 786440 | tf_op jit(solution)/shard_map/ppermute | solution.py:16
  25.8 4.8 %collective-permute-start.5 = (f32[4,1,512]{2,1,0:T(1,128)S(1)}, f32[4,1,512]{2,1,0:T(1,128)S(1)}, u32[]{:S(2)}, u32[]{:S(2)}) collective-permute-start(f32[4,1,512]{2,1,0:T(1,128)S(1)} %slice.262), channel_id=1, source_target_pairs={{1,0},{2,1},{3,2},{5,4},{6,5},{7,6},{9,8},{10,9},{11,10},{13,12},{... | collective-permute-start | bytes 24584 | tf_op jit(solution)/shard_map/ppermute | solution.py:16
  27.3 15.2 %copy-start.1 = (f32[4,128,512]{2,1,0:T(8,128)}, f32[4,128,512]{2,1,0:T(8,128)S(1)}, u32[]{:S(2)}) copy-start(f32[4,128,512]{2,1,0:T(8,128)S(1)} %fusion.72) | copy-start | bytes 3145732
  28.0 14.7 %collective-permute-start.16 = (f32[1,128,512]{2,1,0:T(8,128)S(1)}, f32[1,128,512]{2,1,0:T(8,128)S(1)}, u32[]{:S(2)}, u32[]{:S(2)}) collective-permute-start(f32[1,128,512]{2,1,0:T(8,128)S(1)} %slice.293), channel_id=1, source_target_pairs={{4,0},{8,4},{12,8},{16,12},{20,16},{24,20},{28,24},{5,1},{9,5},{13... | collective-permute-start | bytes 786440 | tf_op jit(solution)/shard_map/ppermute | solution.py:16
  29.3 13.4 %collective-permute-start.17 = (f32[4,1,512]{2,1,0:T(1,128)S(1)}, f32[4,1,512]{2,1,0:T(1,128)S(1)}, u32[]{:S(2)}, u32[]{:S(2)}) collective-permute-start(f32[4,1,512]{2,1,0:T(1,128)S(1)} %slice.295), channel_id=1, source_target_pairs={{1,0},{2,1},{3,2},{5,4},{6,5},{7,6},{9,8},{10,9},{11,10},{13,12},{... | collective-permute-start | bytes 24584 | tf_op jit(solution)/shard_map/ppermute | solution.py:16
  35.9 10.3 %collective-permute-start.6 = (f32[1,128,512]{2,1,0:T(8,128)S(1)}, f32[1,128,512]{2,1,0:T(8,128)S(1)}, u32[]{:S(2)}, u32[]{:S(2)}) collective-permute-start(f32[1,128,512]{2,1,0:T(8,128)S(1)} %slice.265), channel_id=1, source_target_pairs={{0,4},{4,8},{8,12},{12,16},{16,20},{20,24},{24,28},{1,5},{5,9},{9,... | collective-permute-start | bytes 786440 | tf_op jit(solution)/shard_map/ppermute | solution.py:16
  40.7 2.1 %collective-permute-start.7 = (f32[4,1,512]{2,1,0:T(1,128)S(1)}, f32[4,1,512]{2,1,0:T(1,128)S(1)}, u32[]{:S(2)}, u32[]{:S(2)}) collective-permute-start(f32[4,1,512]{2,1,0:T(1,128)S(1)} %slice.267), channel_id=1, source_target_pairs={{0,1},{1,2},{2,3},{4,5},{5,6},{6,7},{8,9},{9,10},{10,11},{12,13},{... | collective-permute-start | bytes 24584 | tf_op jit(solution)/shard_map/ppermute | solution.py:16
  42.5 3.6 %slice-start = ((f32[4,128,512]{2,1,0:T(8,128)}), f32[3,128,512]{2,1,0:T(8,128)S(1)}, s32[]{:S(2)}) async-start(f32[4,128,512]{2,1,0:T(8,128)} %copy-done.1), calls=%async_computation | async-start | bytes 1572864 | tf_op jit(solution)/shard_map/slice | solution.py:20
  46.2 5.0 %copy-start.2 = (f32[4,128,512]{2,1,0:T(8,128)S(1)}, f32[4,128,512]{2,1,0:T(8,128)}, u32[]{:S(2)}) copy-start(f32[4,128,512]{2,1,0:T(8,128)} %copy-done.1) | copy-start | bytes 3145732
  51.5 10.0 %collective-permute-start.8 = (f32[1,128,512]{2,1,0:T(8,128)S(1)}, f32[1,128,512]{2,1,0:T(8,128)S(1)}, u32[]{:S(2)}, u32[]{:S(2)}) collective-permute-start(f32[1,128,512]{2,1,0:T(8,128)S(1)} %slice.271), channel_id=1, source_target_pairs={{4,0},{8,4},{12,8},{16,12},{20,16},{24,20},{28,24},{5,1},{9,5},{13... | collective-permute-start | bytes 786440 | tf_op jit(solution)/shard_map/ppermute | solution.py:16
  52.8 3.1 %collective-permute-start.9 = (f32[4,1,512]{2,1,0:T(1,128)S(1)}, f32[4,1,512]{2,1,0:T(1,128)S(1)}, u32[]{:S(2)}, u32[]{:S(2)}) collective-permute-start(f32[4,1,512]{2,1,0:T(1,128)S(1)} %slice.273), channel_id=1, source_target_pairs={{1,0},{2,1},{3,2},{5,4},{6,5},{7,6},{9,8},{10,9},{11,10},{13,12},{... | collective-permute-start | bytes 24584 | tf_op jit(solution)/shard_map/ppermute | solution.py:16
  63.1 9.8 %collective-permute-start.10 = (f32[1,128,512]{2,1,0:T(8,128)S(1)}, f32[1,128,512]{2,1,0:T(8,128)S(1)}, u32[]{:S(2)}, u32[]{:S(2)}) collective-permute-start(f32[1,128,512]{2,1,0:T(8,128)S(1)} %slice.276), channel_id=1, source_target_pairs={{0,4},{4,8},{8,12},{12,16},{16,20},{20,24},{24,28},{1,5},{5,9},{9,... | collective-permute-start | bytes 786440 | tf_op jit(solution)/shard_map/ppermute | solution.py:16
  68.1 4.7 %collective-permute-start.11 = (f32[4,1,512]{2,1,0:T(1,128)S(1)}, f32[4,1,512]{2,1,0:T(1,128)S(1)}, u32[]{:S(2)}, u32[]{:S(2)}) collective-permute-start(f32[4,1,512]{2,1,0:T(1,128)S(1)} %slice.278), channel_id=1, source_target_pairs={{0,1},{1,2},{2,3},{4,5},{5,6},{6,7},{8,9},{9,10},{10,11},{12,13},{... | collective-permute-start | bytes 24584 | tf_op jit(solution)/shard_map/ppermute | solution.py:16
  70.2 27.2 %collective-permute-start.18 = (f32[1,128,512]{2,1,0:T(8,128)S(1)}, f32[1,128,512]{2,1,0:T(8,128)S(1)}, u32[]{:S(2)}, u32[]{:S(2)}) collective-permute-start(f32[1,128,512]{2,1,0:T(8,128)S(1)} %slice.299), channel_id=1, source_target_pairs={{4,0},{8,4},{12,8},{16,12},{20,16},{24,20},{28,24},{5,1},{9,5},{13... | collective-permute-start | bytes 786440 | tf_op jit(solution)/shard_map/ppermute | solution.py:16
  71.5 21.1 %collective-permute-start.19 = (f32[4,1,512]{2,1,0:T(1,128)S(1)}, f32[4,1,512]{2,1,0:T(1,128)S(1)}, u32[]{:S(2)}, u32[]{:S(2)}) collective-permute-start(f32[4,1,512]{2,1,0:T(1,128)S(1)} %slice.301), channel_id=1, source_target_pairs={{1,0},{2,1},{3,2},{5,4},{6,5},{7,6},{9,8},{10,9},{11,10},{13,12},{... | collective-permute-start | bytes 24584 | tf_op jit(solution)/shard_map/ppermute | solution.py:16
  74.0 12.2 %collective-permute-start.12 = (f32[1,128,512]{2,1,0:T(8,128)S(1)}, f32[1,128,512]{2,1,0:T(8,128)S(1)}, u32[]{:S(2)}, u32[]{:S(2)}) collective-permute-start(f32[1,128,512]{2,1,0:T(8,128)S(1)} %slice.282), channel_id=1, source_target_pairs={{4,0},{8,4},{12,8},{16,12},{20,16},{24,20},{28,24},{5,1},{9,5},{13... | collective-permute-start | bytes 786440 | tf_op jit(solution)/shard_map/ppermute | solution.py:16
  75.3 5.6 %collective-permute-start.13 = (f32[4,1,512]{2,1,0:T(1,128)S(1)}, f32[4,1,512]{2,1,0:T(1,128)S(1)}, u32[]{:S(2)}, u32[]{:S(2)}) collective-permute-start(f32[4,1,512]{2,1,0:T(1,128)S(1)} %slice.284), channel_id=1, source_target_pairs={{1,0},{2,1},{3,2},{5,4},{6,5},{7,6},{9,8},{10,9},{11,10},{13,12},{... | collective-permute-start | bytes 24584 | tf_op jit(solution)/shard_map/ppermute | solution.py:16
  76.8 20.4 %copy-start.3 = (f32[4,128,512]{2,1,0:T(8,128)}, f32[4,128,512]{2,1,0:T(8,128)S(1)}, u32[]{:S(2)}) copy-start(f32[4,128,512]{2,1,0:T(8,128)S(1)} %fusion.74) | copy-start | bytes 3145732
  77.4 19.9 %collective-permute-start.20 = (f32[1,128,512]{2,1,0:T(8,128)S(1)}, f32[1,128,512]{2,1,0:T(8,128)S(1)}, u32[]{:S(2)}, u32[]{:S(2)}) collective-permute-start(f32[1,128,512]{2,1,0:T(8,128)S(1)} %slice.305), channel_id=1, source_target_pairs={{4,0},{8,4},{12,8},{16,12},{20,16},{24,20},{28,24},{5,1},{9,5},{13... | collective-permute-start | bytes 786440 | tf_op jit(solution)/shard_map/ppermute | solution.py:16
  80.9 16.5 %collective-permute-start.21 = (f32[4,1,512]{2,1,0:T(1,128)S(1)}, f32[4,1,512]{2,1,0:T(1,128)S(1)}, u32[]{:S(2)}, u32[]{:S(2)}) collective-permute-start(f32[4,1,512]{2,1,0:T(1,128)S(1)} %slice.307), channel_id=1, source_target_pairs={{1,0},{2,1},{3,2},{5,4},{6,5},{7,6},{9,8},{10,9},{11,10},{13,12},{... | collective-permute-start | bytes 24584 | tf_op jit(solution)/shard_map/ppermute | solution.py:16
  87.7 9.9 %collective-permute-start.14 = (f32[1,128,512]{2,1,0:T(8,128)S(1)}, f32[1,128,512]{2,1,0:T(8,128)S(1)}, u32[]{:S(2)}, u32[]{:S(2)}) collective-permute-start(f32[1,128,512]{2,1,0:T(8,128)S(1)} %slice.287), channel_id=1, source_target_pairs={{0,4},{4,8},{8,12},{12,16},{16,20},{20,24},{24,28},{1,5},{5,9},{9,... | collective-permute-start | bytes 786440 | tf_op jit(solution)/shard_map/ppermute | solution.py:16
  92.6 5.0 %collective-permute-start.15 = (f32[4,1,512]{2,1,0:T(1,128)S(1)}, f32[4,1,512]{2,1,0:T(1,128)S(1)}, u32[]{:S(2)}, u32[]{:S(2)}) collective-permute-start(f32[4,1,512]{2,1,0:T(1,128)S(1)} %slice.289), channel_id=1, source_target_pairs={{0,1},{1,2},{2,3},{4,5},{5,6},{6,7},{8,9},{9,10},{10,11},{12,13},{... | collective-permute-start | bytes 24584 | tf_op jit(solution)/shard_map/ppermute | solution.py:16
  97.3 1.1 slice-start.1
where the time goes:
time: 156 us; the launch traced here: 155 us
  starting transfers between devices  45.6 us (29%)
  blocking collectives  44.9 us (29%)
  other arithmetic  29.3 us (19%)
  waiting for transfers between devices  29.3 us (19%)
  local copies, waits for them, and re-layouts  4.3 us (3%)
    ppermute x22, starting transfers between devices, shifted_2(): lax.ppermute(value, axis, [(source, source + steps) for source in range(i...  45.6 us
    psum x1, blocking collectives, shards(): lax.psum((jnp.stack(gap_list), jnp.stack(step_list)), ('gz', 'gx'))  44.9 us
    ppermute x22, waiting for transfers between devices, shifted_2(): lax.ppermute(value, axis, [(source, source + steps) for source in range(i...  29.3 us
    reduce_sum x2, other arithmetic, shards(): gap_part = jnp.sum(gap_terms)  10.7 us
    mul x8, other arithmetic, shards(): dual_field = tuple((part * shrink for part in proposed))  6.13 us
    sub x7, other arithmetic, gradient(): volume[:, :, 1:] - volume[:, :, :-1]  3.94 us
  transfers between devices with their start and end apart: 22, of which 12 were waited for; matrix products, arithmetic and copies ran while one was open for 7% of the time, Pallas kernels for 0%

commit v1 on v0

v1 whole, which is shorter than its diff:
```python
import functools

import jax
import jax.numpy as jnp
from jax import lax
from jax.experimental import pallas as pl
from jax.experimental.pallas import tpu as pltpu
from jax.sharding import PartitionSpec as P

ITERS = 4
primal_step = 0.28
dual_step = 0.28

SUB = 8
LANE = 128
HALO = ITERS
VMEM = pltpu.VMEM


def vmem_call(body, shapes, count, scratch=(), flops=1 << 20, limit=None, name=None):
    whole = pl.BlockSpec(memory_space=VMEM)
    return pl.pallas_call(
        body,
        out_shape=[jax.ShapeDtypeStruct(s, jnp.float32) for s in shapes],
        in_specs=[pl.BlockSpec(memory_space=pltpu.SMEM)] + [whole] * count,
        out_specs=[whole] * len(shapes),
        scratch_shapes=list(scratch),
        compiler_params=pltpu.CompilerParams(vmem_limit_bytes=limit),
        cost_estimate=pl.CostEstimate(flops=flops, bytes_accessed=1 << 20, transcendentals=0),
        name=name,
    )


def pack_send(half, info, noisy, weight, send_n, send_w, edge_one, edge_two):
    odd = info[0] == 1
    planes, rows, _ = noisy.shape

    def edges(to, start):
        for a, ref in enumerate((noisy, weight)):
            for j in range(planes // 2):
                to[a, j, 0:HALO] = ref[2 * j, start : start + HALO]
                to[a, j, HALO:] = ref[2 * j + 1, start : start + HALO]

    @pl.when(odd)
    def _():
        send_n[...] = noisy[:, 0 : half + SUB]
        send_w[...] = weight[:, 0 : half + SUB]
        edges(edge_one, 0)
        edges(edge_two, rows - HALO)

    @pl.when(jnp.logical_not(odd))
    def _():
        send_n[...] = noisy[:, rows - half - SUB :]
        send_w[...] = weight[:, rows - half - SUB :]
        edges(edge_one, rows - HALO)
        edges(edge_two, 0)


def put_rows(odd, to, body, body_even, body_odd, edge, a):
    planes, ext, _ = to.shape
    count = ext - HALO

    def edge_rows(z):
        half = HALO * (z % 2)
        return edge[a, z // 2, half : half + HALO]

    @pl.when(odd)
    def _():
        to[:, 0:count] = body[:, body_odd : body_odd + count]
        for z in range(planes):
            to[z, count:] = edge_rows(z)

    @pl.when(jnp.logical_not(odd))
    def _():
        to[:, HALO:] = body[:, body_even : body_even + count]
        for z in range(planes):
            to[z, 0:HALO] = edge_rows(z)


def pack_own(half, info, noisy, weight, edge, out_n, out_w):
    odd = info[0] == 1
    for a, (ref, to) in enumerate(((noisy, out_n), (weight, out_w))):
        put_rows(odd, to, ref, 0, half - HALO, edge, a)


def pack_partner(a, info, got, edge, out):
    put_rows(info[0] == 1, out, got, 0, SUB - HALO, edge, a)


def iterate(info, *refs):
    (own_n, own_w, par_n, par_w, one_n, one_w, two_n, two_w) = refs[:8]
    keep, send, stats = refs[8:11]
    noisy, weight, u, bar, p_z, p_x, p_y, cx_ref, acc = refs[11:]
    odd = info[0] == 1
    first_plane, first_row, all_planes, all_rows = info[1], info[2], info[3], info[4]
    planes, ext, cols = own_n.shape
    total = 4 * planes
    strips = ext // SUB
    chunks = cols // LANE
    half = ext - 2 * HALO

    lane = lax.broadcasted_iota(jnp.int32, (SUB, LANE), 1)
    sub = lax.broadcasted_iota(jnp.int32, (SUB, LANE), 0)
    first_sub, last_sub = sub == 0, sub == SUB - 1
    first_lane, last_lane = lane == 0, lane == LANE - 1

    for s in range(strips):
        row = first_row + s * SUB + sub
        inside = jnp.logical_and(row >= 0, row < all_rows - 1)
        cx_ref[s * SUB : (s + 1) * SUB] = jnp.where(inside, dual_step, 0.0).astype(jnp.float32)

    row_block = first_row + lax.broadcasted_iota(jnp.int32, (ext, cols), 0)
    row_in = jnp.logical_and(row_block >= 0, row_block < all_rows)

    def place(base, n_ref, w_ref):
        def one(z, _):
            value = n_ref[z]
            noisy[base + z] = value
            u[base + z] = value
            bar[base + z] = value
            plane = first_plane + base + z
            plane_in = jnp.logical_and(plane >= 0, plane < all_planes)
            weight[base + z] = jnp.where(jnp.logical_and(row_in, plane_in), w_ref[z], 1.0)
            zero = jnp.zeros_like(value)
            p_z[base + z] = zero
            p_x[base + z] = zero
            p_y[base + z] = zero
            return 0

        lax.fori_loop(0, planes, one, 0)

    @pl.when(odd)
    def _():
        place(0, one_n, one_w)
        place(planes, par_n, par_w)
        place(2 * planes, own_n, own_w)
        place(3 * planes, two_n, two_w)

    @pl.when(jnp.logical_not(odd))
    def _():
        place(0, two_n, two_w)
        place(planes, own_n, own_w)
        place(2 * planes, par_n, par_w)
        place(3 * planes, one_n, one_w)

    acc[...] = jnp.zeros_like(acc)

    def load(ref, i, s):
        return [ref[i, s * SUB : (s + 1) * SUB, c * LANE : (c + 1) * LANE] for c in range(chunks)]

    def save(ref, i, s, values):
        for c in range(chunks):
            ref[i, s * SUB : (s + 1) * SUB, c * LANE : (c + 1) * LANE] = values[c]

    def next_col(x):
        rolled = [pltpu.roll(v, LANE - 1, 1) for v in x]
        return [
            jnp.where(last_lane, rolled[c + 1], rolled[c]) if c + 1 < chunks else rolled[c]
            for c in range(chunks)
        ]

    def gradient(x, above, rolled, rolled_next, cz, cx):
        y_next = next_col(x)
        out = []
        for c in range(chunks):
            d_z = (above[c] - x[c]) * cz
            down = jnp.where(last_sub, rolled_next[c], rolled[c])
            d_x = (down - x[c]) * cx
            d_y = (y_next[c] - x[c]) * dual_step
            if c + 1 == chunks:
                d_y = jnp.where(last_lane, 0.0, d_y)
            out.append((d_z, d_x, d_y))
        return out

    def row_up(x):
        return [pltpu.roll(v, SUB - 1, 0) for v in x]

    def row_down(x):
        return [pltpu.roll(v, 1, 0) for v in x]

    def plane_step(k, i, do_u, own):
        plane = first_plane + i
        z_in = jnp.logical_and(plane >= 0, plane < all_planes - 1)
        cz = jnp.where(z_in, dual_step, 0.0).astype(jnp.float32)
        zero = jnp.zeros((SUB, LANE), jnp.float32)
        tv_sum, quad_sum, step_sum = zero, zero, zero
        bar_now = load(bar, i, 0)
        bar_roll = row_up(bar_now)
        if own:
            u_now = load(u, i, 0)
            u_roll = row_up(u_now)
        px_roll_before = None
        for s in range(strips):
            cx = cx_ref[s * SUB : (s + 1) * SUB]
            more = s + 1 < strips
            bar_next = load(bar, i, s + 1) if more else bar_now
            bar_roll_next = row_up(bar_next) if more else bar_roll
            g_bar = gradient(bar_now, load(bar, i + 1, s), bar_roll, bar_roll_next, cz, cx)
            w = load(weight, i, s)
            if own:
                u_next = load(u, i, s + 1) if more else u_now
                u_roll_next = row_up(u_next) if more else u_roll
                g_u = gradient(u_now, load(u, i + 1, s), u_roll, u_roll_next, cz, cx)
                part = zero
                for c in range(chunks):
                    a, b, d = g_u[c]
                    part = part + w[c] * jnp.sqrt(a * a + b * b + d * d)
            pz, px, py = load(p_z, i, s), load(p_x, i, s), load(p_y, i, s)
            for c in range(chunks):
                a, b, d = (q + g for q, g in zip((pz[c], px[c], py[c]), g_bar[c]))
                shrink = jnp.minimum(1.0, w[c] * lax.rsqrt(a * a + b * b + d * d))
                pz[c], px[c], py[c] = a * shrink, b * shrink, d * shrink
            save(p_z, i, s, pz)
            save(p_x, i, s, px)
            save(p_y, i, s, py)
            if do_u:
                pz_below = load(p_z, i - 1, s)
                px_roll = row_down(px)
                before = px_roll_before if s else px_roll
                py_roll = [pltpu.roll(v, 1, 1) for v in py]
                n = load(noisy, i, s)
                old = u_now if own else load(u, i, s)
                new, new_bar = [], []
                quad, step = zero, zero
                for c in range(chunks):
                    x_before = jnp.where(first_sub, before[c], px_roll[c])
                    y_before = jnp.where(first_lane, py_roll[c - 1] if c else 0.0, py_roll[c])
                    spread = (pz[c] - pz_below[c]) + (px[c] - x_before) + (py[c] - y_before)
                    shifted = n[c] + spread
                    updated = (old[c] + primal_step * shifted) * (1.0 / (1.0 + primal_step))
                    change = updated - old[c]
                    new.append(updated)
                    new_bar.append(updated + change)
                    if own:
                        quad = quad + (old[c] * (0.5 * old[c] - n[c]) + 0.5 * (shifted * shifted))
                        step = step + change * change
                save(u, i, s, new)
                save(bar, i, s, new_bar)
                px_roll_before = px_roll
            if own:
                if s == 0:
                    part, quad, step = (jnp.where(sub >= HALO, v, 0.0) for v in (part, quad, step))
                if s + 1 == strips:
                    part, quad, step = (jnp.where(sub < HALO, v, 0.0) for v in (part, quad, step))
                tv_sum, quad_sum, step_sum = tv_sum + part, quad_sum + quad, step_sum + step
                u_now, u_roll = u_next, u_roll_next
            bar_now, bar_roll = bar_next, bar_roll_next
        if own:
            acc[0, k] += tv_sum
            acc[1, k] += quad_sum
            acc[2, k] += step_sum

    def sweep(k, _):
        plane_step(k, k, False, False)

        def ghost(i, _):
            plane_step(k, i, True, False)
            return 0

        def own(i, _):
            plane_step(k, i, True, True)
            return 0

        lax.fori_loop(k + 1, planes, ghost, 0)
        lax.fori_loop(planes, 3 * planes, own, 0)
        lax.fori_loop(3 * planes, total - 1 - k, ghost, 0)
        return 0

    lax.fori_loop(0, ITERS, sweep, 0)

    @pl.when(odd)
    def _():
        keep[...] = u[2 * planes : 3 * planes, HALO : HALO + half]
        send[...] = u[planes : 2 * planes, HALO : HALO + half]

    @pl.when(jnp.logical_not(odd))
    def _():
        keep[...] = u[planes : 2 * planes, HALO : HALO + half]
        send[...] = u[2 * planes : 3 * planes, HALO : HALO + half]

    for k in range(ITERS):
        gap = acc[0, k] * (1.0 / dual_step) + acc[1, k]
        stats[k : k + 1] = jnp.sum(gap, axis=0, keepdims=True)
        stats[ITERS + k : ITERS + k + 1] = jnp.sum(acc[2, k], axis=0, keepdims=True)


def pack_out(info, keep, got, out):
    odd = info[0] == 1
    half = keep.shape[1]

    @pl.when(odd)
    def _():
        out[:, 0:half] = got[...]
        out[:, half:] = keep[...]

    @pl.when(jnp.logical_not(odd))
    def _():
        out[:, 0:half] = keep[...]
        out[:, half:] = got[...]


def shards(noisy_volume, tv_weight):
    planes, rows, cols = noisy_volume.shape
    count_z, count_x = lax.axis_size("gz"), lax.axis_size("gx")
    if planes < ITERS or planes % 2 or count_z % 2 or rows % (2 * SUB) or cols % LANE:
        raise ValueError("unsupported sizes")
    half = rows // 2
    ext = half + 2 * HALO
    cell_count = planes * rows * cols * count_z * count_x
    both = ("gz", "gx")
    gz, gx = lax.axis_index("gz"), lax.axis_index("gx")
    odd = gz % 2
    pair = gz // 2
    info = jnp.stack(
        [
            odd,
            (2 * pair - 1) * planes,
            gx * rows + odd * half - HALO,
            jnp.int32(planes * count_z),
            jnp.int32(rows * count_x),
        ]
    ).astype(jnp.int32)

    def permute(value, step):
        pairs = []
        for z in range(count_z):
            for x in range(count_x):
                tz, tx = step(z, x)
                if 0 <= tz < count_z and 0 <= tx < count_x:
                    pairs.append((z * count_x + x, tz * count_x + tx))
        return lax.ppermute(value, both, pairs)

    swap = lambda z, x: (z ^ 1, x)
    edge_step_one = lambda z, x: (z, x - 1 if z % 2 else x + 1)
    edge_step_two = lambda z, x: (z ^ 1, x + 1 if z % 2 else x - 1)
    ghost_step_one = lambda z, x: (z + 2 if z % 2 else z - 2, x)
    ghost_step_two = lambda z, x: (z - 2 if z % 2 else z + 2, x)

    block = (planes, ext, cols)
    edge = (2, planes // 2, 2 * HALO, cols)
    send_shape = (planes, half + SUB, cols)
    send_n, send_w, edge_one, edge_two = vmem_call(
        functools.partial(pack_send, half), [send_shape] * 2 + [edge] * 2, 2, name="pack_send"
    )(info, noisy_volume, tv_weight)
    got_n = permute(send_n, swap)
    got_one = permute(edge_one, edge_step_one)
    got_two = permute(edge_two, edge_step_two)
    got_w = permute(send_w, swap)
    own_n, own_w = vmem_call(functools.partial(pack_own, half), [block] * 2, 3, name="pack_own")(
        info, noisy_volume, tv_weight, got_one
    )
    one_n = permute(own_n, ghost_step_one)
    one_w = permute(own_w, ghost_step_one)
    (par_n,) = vmem_call(functools.partial(pack_partner, 0), [block], 2, name="pack_partner")(
        info, got_n, got_two
    )
    two_n = permute(par_n, ghost_step_two)
    (par_w,) = vmem_call(functools.partial(pack_partner, 1), [block], 2, name="pack_partner")(
        info, got_w, got_two
    )
    two_w = permute(par_w, ghost_step_two)

    out_half = (planes, half, cols)
    volume = VMEM((4 * planes, ext, cols), jnp.float32)
    keep, send, stats = vmem_call(
        iterate,
        [out_half, out_half, (2 * ITERS, LANE)],
        8,
        scratch=[volume] * 7
        + [VMEM((ext, LANE), jnp.float32), VMEM((3, ITERS, SUB, LANE), jnp.float32)],
        flops=100 << 20,
        limit=40 << 20,
        name="iterate",
    )(info, own_n, own_w, par_n, par_w, one_n, one_w, two_n, two_w)
    got = permute(send, swap)

    if count_z & (count_z - 1) or count_x & (count_x - 1):
        stats = lax.psum(stats, both)
    else:
        step = 1
        while step < count_x:
            stats = stats + permute(stats, lambda z, x, d=step: (z, x ^ d))
            step *= 2
        step = 1
        while step < count_z:
            stats = stats + permute(stats, lambda z, x, d=step: (z ^ d, x))
            step *= 2
    totals = jnp.sum(stats, axis=1) / cell_count
    (out,) = vmem_call(pack_out, [(planes, rows, cols)], 2, name="pack_out")(info, keep, got)
    return (out, totals[:ITERS], jnp.sqrt(totals[ITERS:]))


def solution(mesh):
    placed = (P("gz", "gx", None), P("gz", "gx", None))
    return jax.shard_map(
        shards,
        mesh=mesh,
        in_specs=placed,
        out_specs=(P("gz", "gx", None), P(), P()),
        check_vma=False,
    )
```

time: 156 us -> 114 us (0.73)
  blocking collectives: 44.9 us -> 0 us
  other arithmetic: 29.3 us -> 0.13 us
  Pallas kernels: 0 us -> 28.2 us
  waiting for transfers between devices: 29.3 us -> 38.3 us
  starting transfers between devices: 45.6 us -> 41.2 us
    psum x1 -> x0, blocking collectives: 44.9 us -> none  [shards(): lax.psum((jnp.stack(gap_list), jnp.stack(step_list)), ('gz', 'gx'))]
    pallas_call x0 -> x6, Pallas kernels: none -> 28.2 us  [the longest x1 16.5 us: shards(): vmem_call(iterate, [out_half, out_half, (2 * ITERS, LANE)], 8, scratch=[v...]
    reduce_sum x2 -> x1, other arithmetic: 10.7 us -> 0.11 us  [shards(): totals = jnp.sum(stats, axis=1) / cell_count]
    ppermute x22 -> x14, waiting for transfers between devices: 29.3 us -> 38.3 us  [permute(): return lax.ppermute(value, both, pairs)]
    sub x10 -> x0, other arithmetic: 6.17 us -> none  [the longest x7 3.94 us: gradient(): volume[:, :, 1:] - volume[:, :, :-1]]
    mul x8 -> x0, other arithmetic: 6.13 us -> none  [shards(): dual_field = tuple((part * shrink for part in proposed))]
    another operation x2 -> x0, other arithmetic: 5.25 us -> none  [the longest x1 2.7 us: shards(): jnp.stack(step_list)]
    ppermute x22 -> x14, starting transfers between devices: 45.6 us -> 41.2 us  [permute(): return lax.ppermute(value, both, pairs)]
  transfers between devices with their start and end apart: 22 -> 14, of which waited for: 12 -> 10; matrix products, arithmetic and copies ran while one was open for 7% -> 1% of each run, Pallas kernels for 0% -> 6%
where the time goes in v1:
time: 114 us
  starting transfers between devices  41.2 us (36%)
  waiting for transfers between devices  38.3 us (34%)
  Pallas kernels  28.2 us (25%)
  local copies, waits for them, and re-layouts  5.39 us (5%)
    ppermute x14, starting transfers between devices, permute(): return lax.ppermute(value, both, pairs)  41.2 us
    ppermute x14, waiting for transfers between devices, permute(): return lax.ppermute(value, both, pairs)  38.3 us
    pallas_call x1, Pallas kernels, shards(): vmem_call(iterate, [out_half, out_half, (2 * ITERS, LANE)], 8, scratch=[v...  16.5 us
    unnamed x20, local copies, waits for them, and re-layouts  4.11 us
    pallas_call x1, Pallas kernels, shards(): vmem_call(functools.partial(pack_own, half), [block] * 2, 3, name='pack_o...  2.71 us
    pallas_call x1, Pallas kernels, shards(): vmem_call(functools.partial(pack_send, half), [send_shape] * 2 + [edge] *...  2.7 us
  transfers between devices with their start and end apart: 14, of which 10 were waited for; matrix products, arithmetic and copies ran while one was open for 1% of the time, Pallas kernels for 6%

profile of v1, /device:TPU:0, one launch (start us, length us, event | category | flops | bytes accessed | tf_op | source)
XLA Modules:
  0.0 114.0 jit_solution(8238364503290909857)
XLA Ops:
  0.7 0.7 stack.15.info
  1.3 2.7 %pack_send.1 = (f32[4,72,512]{2,1,0:T(8,128)}, f32[4,72,512]{2,1,0:T(8,128)}, f32[2,2,8,512]{3,2,1,0:T(8,128)}, f32[2,2,8,512]{3,2,1,0:T(8,128)}) custom-call(s32[5]{0:T(128)} %stack.15.info, f32[4,128,512]{2,1,0:T(8,128)} %noisy.3, f32[4,128,512]{2,1,0:T(8,128)} %weight.3), custom_call_target="tpu_custom_call" | custom-call | flops 1048576 | bytes 1048576 | tf_op jit(solution)/shard_map/pack_send/pallas_call | solution.py:342
  4.0 3.0 %collective-permute-start.1 = (f32[4,72,512]{2,1,0:T(8,128)}, f32[4,72,512]{2,1,0:T(8,128)S(1)}, u32[]{:S(2)}, u32[]{:S(2)}) collective-permute-start(f32[4,72,512]{2,1,0:T(8,128)} %get-tuple-element.15), channel_id=1, source_target_pairs={{0,4},{1,5},{2,6},{3,7},{4,0},{5,1},{6,2},{7,3},{8,12},{9,13},{10,... | collective-permute-start | bytes 1769480 | tf_op jit(solution)/shard_map/ppermute | solution.py:331
  7.0 1.4 %collective-permute-start = (f32[2,2,8,512]{3,2,1,0:T(8,128)}, f32[2,2,8,512]{3,2,1,0:T(8,128)S(1)}, u32[]{:S(2)}, u32[]{:S(2)}) collective-permute-start(f32[2,2,8,512]{3,2,1,0:T(8,128)} %get-tuple-element.12), channel_id=1, source_target_pairs={{0,1},{1,2},{2,3},{5,4},{6,5},{7,6},{8,9},{9,10},{10,11},{13,12},{... | collective-permute-start | bytes 196616 | tf_op jit(solution)/shard_map/ppermute | solution.py:331
  10.2 2.7 %pack_own.1 = (f32[4,72,512]{2,1,0:T(8,128)}, f32[4,72,512]{2,1,0:T(8,128)}) custom-call(s32[5]{0:T(128)} %stack.15.info, f32[4,128,512]{2,1,0:T(8,128)} %noisy.3, f32[4,128,512]{2,1,0:T(8,128)} %weight.3, f32[2,2,8,512]{3,2,1,0:T(8,128)} %copy-done.9), custom_call_target="tpu_custom_call" | custom-call | flops 1048576 | bytes 1048576 | tf_op jit(solution)/shard_map/pack_own/pallas_call | solution.py:349
  12.9 1.3 %collective-permute-start.4 = (f32[4,72,512]{2,1,0:T(8,128)}, f32[4,72,512]{2,1,0:T(8,128)S(1)}, u32[]{:S(2)}, u32[]{:S(2)}) collective-permute-start(f32[4,72,512]{2,1,0:T(8,128)} %get-tuple-element.13.refs_0_), channel_id=1, source_target_pairs={{4,12},{5,13},{6,14},{7,15},{8,0},{9,1},{10,2},{11,3},{12,20},{13,... | collective-permute-start | bytes 1769480 | tf_op jit(solution)/shard_map/ppermute | solution.py:331
  14.2 1.3 %collective-permute-start.5 = (f32[4,72,512]{2,1,0:T(8,128)}, f32[4,72,512]{2,1,0:T(8,128)S(1)}, u32[]{:S(2)}, u32[]{:S(2)}) collective-permute-start(f32[4,72,512]{2,1,0:T(8,128)} %get-tuple-element.14.refs_1_), channel_id=1, source_target_pairs={{4,12},{5,13},{6,14},{7,15},{8,0},{9,1},{10,2},{11,3},{12,20},{13,... | collective-permute-start | bytes 1769480 | tf_op jit(solution)/shard_map/ppermute | solution.py:331
  15.5 5.9 %collective-permute-done.1.got = f32[4,72,512]{2,1,0:T(8,128)S(1)} collective-permute-done((f32[4,72,512]{2,1,0:T(8,128)}, f32[4,72,512]{2,1,0:T(8,128)S(1)}, u32[]{:S(2)}, u32[]{:S(2)}) %collective-permute-start.1) | collective-permute-done | bytes 589856 | tf_op jit(solution)/shard_map/ppermute | solution.py:331
  21.4 0.8 copy-done.6
  22.2 2.0 %pack_partner.2.refs_2_ = f32[4,72,512]{2,1,0:T(8,128)} custom-call(s32[5]{0:T(128)} %stack.15.info, f32[4,72,512]{2,1,0:T(8,128)} %copy-done.6, f32[2,2,8,512]{3,2,1,0:T(8,128)} %copy-done.8), custom_call_target="tpu_custom_call" | custom-call | flops 1048576 | bytes 1048576 | tf_op jit(solution)/shard_map/pack_partner/pallas_call | solution.py:354
  24.2 4.2 %collective-permute-start.6 = (f32[4,72,512]{2,1,0:T(8,128)}, f32[4,72,512]{2,1,0:T(8,128)S(1)}, u32[]{:S(2)}, u32[]{:S(2)}) collective-permute-start(f32[4,72,512]{2,1,0:T(8,128)} %pack_partner.2.refs_2_), channel_id=1, source_target_pairs={{0,8},{1,9},{2,10},{3,11},{8,16},{9,17},{10,18},{11,19},{12,4},{13... | collective-permute-start | bytes 1769480 | tf_op jit(solution)/shard_map/ppermute | solution.py:331
  28.4 5.6 %collective-permute-done.3.got = f32[4,72,512]{2,1,0:T(8,128)} collective-permute-done((f32[4,72,512]{2,1,0:T(8,128)}, f32[4,72,512]{2,1,0:T(8,128)}, u32[]{:S(2)}, u32[]{:S(2)}) %collective-permute-start.3) | collective-permute-done | bytes 589856 | tf_op jit(solution)/shard_map/ppermute | solution.py:331
  34.0 1.9 %pack_partner.3.refs_3_ = f32[4,72,512]{2,1,0:T(8,128)} custom-call(s32[5]{0:T(128)} %stack.15.info, f32[4,72,512]{2,1,0:T(8,128)} %collective-permute-done.3.got, f32[2,2,8,512]{3,2,1,0:T(8,128)} %copy-done.8), custom_call_target="tpu_custom_call" | custom-call | flops 1048576 | bytes 1048576 | tf_op jit(solution)/shard_map/pack_partner/pallas_call | solution.py:358
  35.9 3.8 %collective-permute-start.7 = (f32[4,72,512]{2,1,0:T(8,128)}, f32[4,72,512]{2,1,0:T(8,128)S(1)}, u32[]{:S(2)}, u32[]{:S(2)}) collective-permute-start(f32[4,72,512]{2,1,0:T(8,128)} %pack_partner.3.refs_3_), channel_id=1, source_target_pairs={{0,8},{1,9},{2,10},{3,11},{8,16},{9,17},{10,18},{11,19},{12,4},{13... | collective-permute-start | bytes 1769480 | tf_op jit(solution)/shard_map/ppermute | solution.py:331
  39.7 1.7 %collective-permute-done.5.refs_5_ = f32[4,72,512]{2,1,0:T(8,128)S(1)} collective-permute-done((f32[4,72,512]{2,1,0:T(8,128)}, f32[4,72,512]{2,1,0:T(8,128)S(1)}, u32[]{:S(2)}, u32[]{:S(2)}) %collective-permute-start.5) | collective-permute-done | bytes 589856 | tf_op jit(solution)/shard_map/ppermute | solution.py:331
  41.4 10.9 %collective-permute-done.7.refs_7_ = f32[4,72,512]{2,1,0:T(8,128)S(1)} collective-permute-done((f32[4,72,512]{2,1,0:T(8,128)}, f32[4,72,512]{2,1,0:T(8,128)S(1)}, u32[]{:S(2)}, u32[]{:S(2)}) %collective-permute-start.7) | collective-permute-done | bytes 589856 | tf_op jit(solution)/shard_map/ppermute | solution.py:331
  52.3 1.1 copy-done.1
  53.4 16.5 %iterate.1 = (f32[4,64,512]{2,1,0:T(8,128)S(1)}, f32[4,64,512]{2,1,0:T(8,128)S(1)}, f32[8,128]{1,0:T(8,128)S(1)}) custom-call(s32[5]{0:T(128)S(1)} %copy-done.5, f32[4,72,512]{2,1,0:T(8,128)S(1)} %copy-done.2, f32[4,72,512]{2,1,0:T(8,128)S(1)} %copy-done.3, f32[4,72,512]{2,1,0:T(8,128)S(1)} %copy-done, f32[4,72,512]{2,1,0:T(8,128)S(1)} %copy-done.1, ...), custom_call_target="tpu_custom_call" | custom-call | flops 104857600 | bytes 1048576 | tf_op jit(solution)/shard_map/iterate/pallas_call | solution.py:365
  69.9 0.8 copy-done.4
  70.7 7.8 %collective-permute-start.9 = (f32[8,128]{1,0:T(8,128)S(1)}, f32[8,128]{1,0:T(8,128)S(1)}, u32[]{:S(2)}, u32[]{:S(2)}) collective-permute-start(f32[8,128]{1,0:T(8,128)S(1)} %get-tuple-element.20), channel_id=1, source_target_pairs={{0,1},{1,0},{2,3},{3,2},{4,5},{5,4},{6,7},{7,6},{8,9},{9,8},{10,11... | collective-permute-start | bytes 12296 | tf_op jit(solution)/shard_map/ppermute | solution.py:331
  78.5 0.8 collective-permute-done.9
  79.4 8.8 %collective-permute-start.10 = (f32[8,128]{1,0:T(8,128)S(1)}, f32[8,128]{1,0:T(8,128)S(1)}, u32[]{:S(2)}, u32[]{:S(2)}) collective-permute-start(f32[8,128]{1,0:T(8,128)S(1)} %add.27), channel_id=1, source_target_pairs={{0,2},{1,3},{2,0},{3,1},{4,6},{5,7},{6,4},{7,5},{8,10},{9,11},{10,... | collective-permute-start | bytes 12296 | tf_op jit(solution)/shard_map/ppermute | solution.py:331
  88.1 1.6 %collective-permute-done.10 = f32[8,128]{1,0:T(8,128)S(1)} collective-permute-done((f32[8,128]{1,0:T(8,128)S(1)}, f32[8,128]{1,0:T(8,128)S(1)}, u32[]{:S(2)}, u32[]{:S(2)}) %collective-permute-start.10) | collective-permute-done | bytes 4128 | tf_op jit(solution)/shard_map/ppermute | solution.py:331
  89.7 2.7 %collective-permute-start.11 = (f32[8,128]{1,0:T(8,128)S(1)}, f32[8,128]{1,0:T(8,128)S(1)}, u32[]{:S(2)}, u32[]{:S(2)}) collective-permute-start(f32[8,128]{1,0:T(8,128)S(1)} %add.28), channel_id=1, source_target_pairs={{0,4},{1,5},{2,6},{3,7},{4,0},{5,1},{6,2},{7,3},{8,12},{9,13},{10,... | collective-permute-start | bytes 12296 | tf_op jit(solution)/shard_map/ppermute | solution.py:331
  92.4 1.6 %collective-permute-done.11 = f32[8,128]{1,0:T(8,128)S(1)} collective-permute-done((f32[8,128]{1,0:T(8,128)S(1)}, f32[8,128]{1,0:T(8,128)S(1)}, u32[]{:S(2)}, u32[]{:S(2)}) %collective-permute-start.11) | collective-permute-done | bytes 4128 | tf_op jit(solution)/shard_map/ppermute | solution.py:331
  94.0 1.7 %collective-permute-start.12 = (f32[8,128]{1,0:T(8,128)S(1)}, f32[8,128]{1,0:T(8,128)S(1)}, u32[]{:S(2)}, u32[]{:S(2)}) collective-permute-start(f32[8,128]{1,0:T(8,128)S(1)} %add.29), channel_id=1, source_target_pairs={{0,8},{1,9},{2,10},{3,11},{4,12},{5,13},{6,14},{7,15},{8,0},{9,1},... | collective-permute-start | bytes 12296 | tf_op jit(solution)/shard_map/ppermute | solution.py:331
  95.7 1.9 %collective-permute-done.12 = f32[8,128]{1,0:T(8,128)S(1)} collective-permute-done((f32[8,128]{1,0:T(8,128)S(1)}, f32[8,128]{1,0:T(8,128)S(1)}, u32[]{:S(2)}, u32[]{:S(2)}) %collective-permute-start.12) | collective-permute-done | bytes 4128 | tf_op jit(solution)/shard_map/ppermute | solution.py:331
  97.6 2.7 %collective-permute-start.13 = (f32[8,128]{1,0:T(8,128)S(1)}, f32[8,128]{1,0:T(8,128)S(1)}, u32[]{:S(2)}, u32[]{:S(2)}) collective-permute-start(f32[8,128]{1,0:T(8,128)S(1)} %add.30), channel_id=1, source_target_pairs={{0,16},{1,17},{2,18},{3,19},{4,20},{5,21},{6,22},{7,23},{8,24},{9,... | collective-permute-start | bytes 12296 | tf_op jit(solution)/shard_map/ppermute | solution.py:331
  100.3 1.9 %collective-permute-start.8 = (f32[4,64,512]{2,1,0:T(8,128)S(1)}, f32[4,64,512]{2,1,0:T(8,128)S(1)}, u32[]{:S(2)}, u32[]{:S(2)}) collective-permute-start(f32[4,64,512]{2,1,0:T(8,128)S(1)} %get-tuple-element.19), channel_id=1, source_target_pairs={{0,4},{1,5},{2,6},{3,7},{4,0},{5,1},{6,2},{7,3},{8,12},{9,13},{10,... | collective-permute-start | bytes 1572872 | tf_op jit(solution)/shard_map/ppermute | solution.py:331
  103.0 8.0 %collective-permute-done.8.got = f32[4,64,512]{2,1,0:T(8,128)S(1)} collective-permute-done((f32[4,64,512]{2,1,0:T(8,128)S(1)}, f32[4,64,512]{2,1,0:T(8,128)S(1)}, u32[]{:S(2)}, u32[]{:S(2)}) %collective-permute-start.8) | collective-permute-done | bytes 524320 | tf_op jit(solution)/shard_map/ppermute | solution.py:331
  110.9 0.8 copy-done.7
  111.7 2.3 %pack_out.1 = f32[4,128,512]{2,1,0:T(8,128)} custom-call(s32[5]{0:T(128)} %stack.15.info, f32[4,64,512]{2,1,0:T(8,128)} %copy-done.4, f32[4,64,512]{2,1,0:T(8,128)} %copy-done.7), custom_call_target="tpu_custom_call" | custom-call | flops 1048576 | bytes 1048576 | tf_op jit(solution)/shard_map/pack_out/pallas_call | solution.py:389
  (30 shorter events, 2.5 us)
Async XLA Ops:
  4.0 17.4 %collective-permute-start.1 = (f32[4,72,512]{2,1,0:T(8,128)}, f32[4,72,512]{2,1,0:T(8,128)S(1)}, u32[]{:S(2)}, u32[]{:S(2)}) collective-permute-start(f32[4,72,512]{2,1,0:T(8,128)} %get-tuple-element.15), channel_id=1, source_target_pairs={{0,4},{1,5},{2,6},{3,7},{4,0},{5,1},{6,2},{7,3},{8,12},{9,13},{10,... | collective-permute-start | bytes 1769480 | tf_op jit(solution)/shard_map/ppermute | solution.py:331
  7.0 27.0 %collective-permute-start.3 = (f32[4,72,512]{2,1,0:T(8,128)}, f32[4,72,512]{2,1,0:T(8,128)}, u32[]{:S(2)}, u32[]{:S(2)}) collective-permute-start(f32[4,72,512]{2,1,0:T(8,128)} %get-tuple-element.17), channel_id=1, source_target_pairs={{0,4},{1,5},{2,6},{3,7},{4,0},{5,1},{6,2},{7,3},{8,12},{9,13},{10,... | collective-permute-start | bytes 1769480 | tf_op jit(solution)/shard_map/ppermute | solution.py:331
  7.0 2.5 %collective-permute-start = (f32[2,2,8,512]{3,2,1,0:T(8,128)}, f32[2,2,8,512]{3,2,1,0:T(8,128)S(1)}, u32[]{:S(2)}, u32[]{:S(2)}) collective-permute-start(f32[2,2,8,512]{3,2,1,0:T(8,128)} %get-tuple-element.12), channel_id=1, source_target_pairs={{0,1},{1,2},{2,3},{5,4},{6,5},{7,6},{8,9},{9,10},{10,11},{13,12},{... | collective-permute-start | bytes 196616 | tf_op jit(solution)/shard_map/ppermute | solution.py:331
  8.5 7.0 %collective-permute-start.2 = (f32[2,2,8,512]{3,2,1,0:T(8,128)}, f32[2,2,8,512]{3,2,1,0:T(8,128)S(1)}, u32[]{:S(2)}, u32[]{:S(2)}) collective-permute-start(f32[2,2,8,512]{3,2,1,0:T(8,128)} %get-tuple-element.16), channel_id=1, source_target_pairs={{1,4},{2,5},{3,6},{4,1},{5,2},{6,3},{9,12},{10,13},{11,14},{12,9},... | collective-permute-start | bytes 196616 | tf_op jit(solution)/shard_map/ppermute | solution.py:331
  9.6 0.6 copy-start.9
  12.9 26.8 %collective-permute-start.4 = (f32[4,72,512]{2,1,0:T(8,128)}, f32[4,72,512]{2,1,0:T(8,128)S(1)}, u32[]{:S(2)}, u32[]{:S(2)}) collective-permute-start(f32[4,72,512]{2,1,0:T(8,128)} %get-tuple-element.13.refs_0_), channel_id=1, source_target_pairs={{4,12},{5,13},{6,14},{7,15},{8,0},{9,1},{10,2},{11,3},{12,20},{13,... | collective-permute-start | bytes 1769480 | tf_op jit(solution)/shard_map/ppermute | solution.py:331
  14.2 27.2 %collective-permute-start.5 = (f32[4,72,512]{2,1,0:T(8,128)}, f32[4,72,512]{2,1,0:T(8,128)S(1)}, u32[]{:S(2)}, u32[]{:S(2)}) collective-permute-start(f32[4,72,512]{2,1,0:T(8,128)} %get-tuple-element.14.refs_1_), channel_id=1, source_target_pairs={{4,12},{5,13},{6,14},{7,15},{8,0},{9,1},{10,2},{11,3},{12,20},{13,... | collective-permute-start | bytes 1769480 | tf_op jit(solution)/shard_map/ppermute | solution.py:331
  15.5 5.9 %copy-start.8 = (f32[2,2,8,512]{3,2,1,0:T(8,128)}, f32[2,2,8,512]{3,2,1,0:T(8,128)S(1)}, u32[]{:S(2)}) copy-start(f32[2,2,8,512]{3,2,1,0:T(8,128)S(1)} %collective-permute-done.2.edge) | copy-start | bytes 196612
  21.4 0.8 copy-start.6
  22.2 30.1 %copy-start.3 = (f32[4,72,512]{2,1,0:T(8,128)S(1)}, f32[4,72,512]{2,1,0:T(8,128)}, u32[]{:S(2)}) copy-start(f32[4,72,512]{2,1,0:T(8,128)} %get-tuple-element.14.refs_1_) | copy-start | bytes 1769476
  24.2 28.1 %copy-start = (f32[4,72,512]{2,1,0:T(8,128)S(1)}, f32[4,72,512]{2,1,0:T(8,128)}, u32[]{:S(2)}) copy-start(f32[4,72,512]{2,1,0:T(8,128)} %pack_partner.2.refs_2_) | copy-start | bytes 1769476
  24.2 28.1 %copy-start.2 = (f32[4,72,512]{2,1,0:T(8,128)S(1)}, f32[4,72,512]{2,1,0:T(8,128)}, u32[]{:S(2)}) copy-start(f32[4,72,512]{2,1,0:T(8,128)} %get-tuple-element.13.refs_0_) | copy-start | bytes 1769476
  24.2 28.1 %copy-start.5 = (s32[5]{0:T(128)S(1)}, s32[5]{0:T(128)}, u32[]{:S(2)}) copy-start(s32[5]{0:T(128)} %stack.15.info) | copy-start | bytes 64
  24.2 17.2 %collective-permute-start.6 = (f32[4,72,512]{2,1,0:T(8,128)}, f32[4,72,512]{2,1,0:T(8,128)S(1)}, u32[]{:S(2)}, u32[]{:S(2)}) collective-permute-start(f32[4,72,512]{2,1,0:T(8,128)} %pack_partner.2.refs_2_), channel_id=1, source_target_pairs={{0,8},{1,9},{2,10},{3,11},{8,16},{9,17},{10,18},{11,19},{12,4},{13... | collective-permute-start | bytes 1769480 | tf_op jit(solution)/shard_map/ppermute | solution.py:331
  35.9 16.3 %collective-permute-start.7 = (f32[4,72,512]{2,1,0:T(8,128)}, f32[4,72,512]{2,1,0:T(8,128)S(1)}, u32[]{:S(2)}, u32[]{:S(2)}) collective-permute-start(f32[4,72,512]{2,1,0:T(8,128)} %pack_partner.3.refs_3_), channel_id=1, source_target_pairs={{0,8},{1,9},{2,10},{3,11},{8,16},{9,17},{10,18},{11,19},{12,4},{13... | collective-permute-start | bytes 1769480 | tf_op jit(solution)/shard_map/ppermute | solution.py:331
  52.3 1.1 copy-start.1
  69.9 0.8 copy-start.4
  70.7 8.7 %collective-permute-start.9 = (f32[8,128]{1,0:T(8,128)S(1)}, f32[8,128]{1,0:T(8,128)S(1)}, u32[]{:S(2)}, u32[]{:S(2)}) collective-permute-start(f32[8,128]{1,0:T(8,128)S(1)} %get-tuple-element.20), channel_id=1, source_target_pairs={{0,1},{1,0},{2,3},{3,2},{4,5},{5,4},{6,7},{7,6},{8,9},{9,8},{10,11... | collective-permute-start | bytes 12296 | tf_op jit(solution)/shard_map/ppermute | solution.py:331
  79.4 10.3 %collective-permute-start.10 = (f32[8,128]{1,0:T(8,128)S(1)}, f32[8,128]{1,0:T(8,128)S(1)}, u32[]{:S(2)}, u32[]{:S(2)}) collective-permute-start(f32[8,128]{1,0:T(8,128)S(1)} %add.27), channel_id=1, source_target_pairs={{0,2},{1,3},{2,0},{3,1},{4,6},{5,7},{6,4},{7,5},{8,10},{9,11},{10,... | collective-permute-start | bytes 12296 | tf_op jit(solution)/shard_map/ppermute | solution.py:331
  89.7 4.3 %collective-permute-start.11 = (f32[8,128]{1,0:T(8,128)S(1)}, f32[8,128]{1,0:T(8,128)S(1)}, u32[]{:S(2)}, u32[]{:S(2)}) collective-permute-start(f32[8,128]{1,0:T(8,128)S(1)} %add.28), channel_id=1, source_target_pairs={{0,4},{1,5},{2,6},{3,7},{4,0},{5,1},{6,2},{7,3},{8,12},{9,13},{10,... | collective-permute-start | bytes 12296 | tf_op jit(solution)/shard_map/ppermute | solution.py:331
  94.0 3.6 %collective-permute-start.12 = (f32[8,128]{1,0:T(8,128)S(1)}, f32[8,128]{1,0:T(8,128)S(1)}, u32[]{:S(2)}, u32[]{:S(2)}) collective-permute-start(f32[8,128]{1,0:T(8,128)S(1)} %add.29), channel_id=1, source_target_pairs={{0,8},{1,9},{2,10},{3,11},{4,12},{5,13},{6,14},{7,15},{8,0},{9,1},... | collective-permute-start | bytes 12296 | tf_op jit(solution)/shard_map/ppermute | solution.py:331
  97.6 4.6 %collective-permute-start.13 = (f32[8,128]{1,0:T(8,128)S(1)}, f32[8,128]{1,0:T(8,128)S(1)}, u32[]{:S(2)}, u32[]{:S(2)}) collective-permute-start(f32[8,128]{1,0:T(8,128)S(1)} %add.30), channel_id=1, source_target_pairs={{0,16},{1,17},{2,18},{3,19},{4,20},{5,21},{6,22},{7,23},{8,24},{9,... | collective-permute-start | bytes 12296 | tf_op jit(solution)/shard_map/ppermute | solution.py:331
  100.3 10.6 %collective-permute-start.8 = (f32[4,64,512]{2,1,0:T(8,128)S(1)}, f32[4,64,512]{2,1,0:T(8,128)S(1)}, u32[]{:S(2)}, u32[]{:S(2)}) collective-permute-start(f32[4,64,512]{2,1,0:T(8,128)S(1)} %get-tuple-element.19), channel_id=1, source_target_pairs={{0,4},{1,5},{2,6},{3,7},{4,0},{5,1},{6,2},{7,3},{8,12},{9,13},{10,... | collective-permute-start | bytes 1572872 | tf_op jit(solution)/shard_map/ppermute | solution.py:331
  110.9 0.8 copy-start.7

commit v2 on v0

v2 whole, which is shorter than its diff:
```python
import functools

import jax
import jax.numpy as jnp
from jax import lax
from jax.experimental import pallas as pl
from jax.experimental.pallas import tpu as pltpu
from jax.sharding import PartitionSpec as P

ITERS = 4
primal_step = 0.28
dual_step = 0.28

SUB = 8
LANE = 128
HALO = ITERS
VMEM = pltpu.VMEM


def vmem_call(body, shapes, spaces, scratch=(), flops=1 << 20, limit=16, name=None):
    return pl.pallas_call(
        body,
        out_shape=[jax.ShapeDtypeStruct(s, jnp.float32) for s in shapes],
        in_specs=[pl.BlockSpec(memory_space=s) for s in spaces],
        out_specs=[pl.BlockSpec(memory_space=VMEM)] * len(shapes),
        scratch_shapes=list(scratch),
        compiler_params=pltpu.CompilerParams(vmem_limit_bytes=limit << 20),
        cost_estimate=pl.CostEstimate(flops=flops, bytes_accessed=1 << 20, transcendentals=0),
        name=name,
    )


def is_odd():
    return lax.rem(lax.axis_index("gz"), 2) == 1


def by_parity(odd, when_odd, when_even):
    pl.when(odd)(when_odd)
    pl.when(jnp.logical_not(odd))(when_even)


def pack_edges(noisy, weight, edge_one, edge_two, low, high, sems):
    planes, rows, _ = noisy.shape
    copies = []
    for a, ref in enumerate((noisy, weight)):
        copies.append(pltpu.make_async_copy(ref.at[:, 0:SUB], low.at[a], sems.at[2 * a]))
        copies.append(
            pltpu.make_async_copy(ref.at[:, rows - SUB : rows], high.at[a], sems.at[2 * a + 1])
        )
    for copy in copies:
        copy.start()
    for copy in copies:
        copy.wait()

    def fill(to, ref, start):
        for a in range(2):
            for j in range(planes // 2):
                to[a, j, 0:HALO] = ref[a, 2 * j, start : start + HALO]
                to[a, j, HALO:] = ref[a, 2 * j + 1, start : start + HALO]

    def when_odd():
        fill(edge_one, low, 0)
        fill(edge_two, high, SUB - HALO)

    def when_even():
        fill(edge_one, high, SUB - HALO)
        fill(edge_two, low, 0)

    by_parity(is_odd(), when_odd, when_even)


def pack_block(parts, *refs):
    count = len(parts)
    bodies, edge, outs = refs[:count], refs[count], refs[count + 1 :]

    def fill(odd):
        for (a, body_even, body_odd), body, to in zip(parts, bodies, outs):
            planes, ext, _ = to.shape
            used = ext - HALO
            start = body_odd if odd else body_even
            if odd:
                to[:, 0:used] = body[:, start : start + used]
            else:
                to[:, HALO:] = body[:, start : start + used]
            for z in range(planes):
                half = HALO * (z % 2)
                rows = edge[a, z // 2, half : half + HALO]
                if odd:
                    to[z, used:] = rows
                else:
                    to[z, 0:HALO] = rows

    by_parity(is_odd(), lambda: fill(True), lambda: fill(False))


class Sweep:
    def __init__(self, state, weight, noisy, cx_ref, acc, offset, first_plane, all_planes):
        self.u, self.bar, self.p_z, self.p_x, self.p_y = state
        self.weight, self.noisy, self.cx_ref, self.acc = weight, noisy, cx_ref, acc
        self.offset, self.first_plane, self.all_planes = offset, first_plane, all_planes
        _, self.ext, cols = weight.shape
        self.strips, self.chunks = self.ext // SUB, cols // LANE
        lane = lax.broadcasted_iota(jnp.int32, (SUB, LANE), 1)
        self.sub = lax.broadcasted_iota(jnp.int32, (SUB, LANE), 0)
        self.first_sub, self.last_sub = self.sub == 0, self.sub == SUB - 1
        self.first_lane, self.last_lane = lane == 0, lane == LANE - 1

    def load(self, ref, m, s):
        return [
            ref[m, s * SUB : (s + 1) * SUB, c * LANE : (c + 1) * LANE] for c in range(self.chunks)
        ]

    def save(self, ref, m, s, values):
        for c in range(self.chunks):
            ref[m, s * SUB : (s + 1) * SUB, c * LANE : (c + 1) * LANE] = values[c]

    def gradient(self, x, above, rolled, rolled_next, cz, cx):
        side = [pltpu.roll(v, LANE - 1, 1) for v in x]
        out = []
        for c in range(self.chunks):
            last = c + 1 == self.chunks
            y_next = side[c] if last else jnp.where(self.last_lane, side[c + 1], side[c])
            d_z = (above[c] - x[c]) * cz
            down = jnp.where(self.last_sub, rolled_next[c], rolled[c])
            d_x = (down - x[c]) * cx
            d_y = (y_next - x[c]) * dual_step
            if last:
                d_y = jnp.where(self.last_lane, 0.0, d_y)
            out.append((d_z, d_x, d_y))
        return out

    def step(self, k, i, do_p, do_u, own):
        m = i - self.offset
        plane = self.first_plane + i
        z_in = jnp.logical_and(plane >= 0, plane < self.all_planes - 1)
        cz = jnp.where(z_in, dual_step, 0.0).astype(jnp.float32)
        zero = jnp.zeros((SUB, LANE), jnp.float32)
        tv_sum, quad_sum, step_sum = zero, zero, zero
        load, save, strips, chunks = self.load, self.save, self.strips, self.chunks
        row_up = lambda x: [pltpu.roll(v, SUB - 1, 0) for v in x]
        if do_p:
            bar_now = load(self.bar, m, 0)
            bar_roll = row_up(bar_now)
            if own:
                u_now = load(self.u, m, 0)
                u_roll = row_up(u_now)
        px_roll_before = None
        for s in range(strips):
            more = s + 1 < strips
            part, quad, step = zero, zero, zero
            if do_p:
                cx = self.cx_ref[s * SUB : (s + 1) * SUB]
                bar_next = load(self.bar, m, s + 1) if more else bar_now
                bar_roll_next = row_up(bar_next) if more else bar_roll
                above = load(self.bar, m + 1, s)
                g_bar = self.gradient(bar_now, above, bar_roll, bar_roll_next, cz, cx)
                w = load(self.weight, m, s)
                if own:
                    u_next = load(self.u, m, s + 1) if more else u_now
                    u_roll_next = row_up(u_next) if more else u_roll
                    above = load(self.u, m + 1, s)
                    g_u = self.gradient(u_now, above, u_roll, u_roll_next, cz, cx)
                    for c in range(chunks):
                        a, b, d = g_u[c]
                        part = part + w[c] * jnp.sqrt(a * a + b * b + d * d)
            pz, px, py = load(self.p_z, m, s), load(self.p_x, m, s), load(self.p_y, m, s)
            if do_p:
                for c in range(chunks):
                    a, b, d = (q + g for q, g in zip((pz[c], px[c], py[c]), g_bar[c]))
                    shrink = jnp.minimum(1.0, w[c] * lax.rsqrt(a * a + b * b + d * d))
                    pz[c], px[c], py[c] = a * shrink, b * shrink, d * shrink
                save(self.p_z, m, s, pz)
                save(self.p_x, m, s, px)
                save(self.p_y, m, s, py)
            if do_u:
                pz_below = load(self.p_z, m - 1, s)
                px_roll = [pltpu.roll(v, 1, 0) for v in px]
                before = px_roll_before if s else px_roll
                py_roll = [pltpu.roll(v, 1, 1) for v in py]
                n = load(self.noisy, m, s)
                old = u_now if own and do_p else load(self.u, m, s)
                new, new_bar = [], []
                for c in range(chunks):
                    x_before = jnp.where(self.first_sub, before[c], px_roll[c])
                    y_before = jnp.where(self.first_lane, py_roll[c - 1] if c else 0.0, py_roll[c])
                    spread = (pz[c] - pz_below[c]) + (px[c] - x_before) + (py[c] - y_before)
                    shifted = n[c] + spread
                    updated = (old[c] + primal_step * shifted) * (1.0 / (1.0 + primal_step))
                    change = updated - old[c]
                    new.append(updated)
                    new_bar.append(updated + change)
                    if own:
                        quad = quad + (old[c] * (0.5 * old[c] - n[c]) + 0.5 * (shifted * shifted))
                        step = step + change * change
                save(self.u, m, s, new)
                save(self.bar, m, s, new_bar)
                px_roll_before = px_roll
            if own:
                if s == 0:
                    part, quad, step = (
                        jnp.where(self.sub >= HALO, v, 0.0) for v in (part, quad, step)
                    )
                if not more:
                    part, quad, step = (
                        jnp.where(self.sub < HALO, v, 0.0) for v in (part, quad, step)
                    )
                tv_sum, quad_sum, step_sum = tv_sum + part, quad_sum + quad, step_sum + step
            if do_p:
                bar_now, bar_roll = bar_next, bar_roll_next
                if own:
                    u_now, u_roll = u_next, u_roll_next
        if own:
            if do_p:
                self.acc[0, k] += tv_sum
            if do_u:
                self.acc[1, k] += quad_sum
                self.acc[2, k] += step_sum

    def loop(self, k, low, high, own):
        def body(i, _):
            self.step(k, i, True, True, own)
            return 0

        lax.fori_loop(low, high, body, 0)


def place_rows(cx_ref, first_row, all_rows):
    sub = lax.broadcasted_iota(jnp.int32, (SUB, LANE), 0)
    for s in range(cx_ref.shape[0] // SUB):
        row = first_row + s * SUB + sub
        inside = jnp.logical_and(row >= 0, row < all_rows - 1)
        cx_ref[s * SUB : (s + 1) * SUB] = jnp.where(inside, dual_step, 0.0).astype(jnp.float32)


def place_weight(to, m, value, plane, first_row, all_planes, all_rows):
    row = first_row + lax.broadcasted_iota(jnp.int32, value.shape, 0)
    row_in = jnp.logical_and(row >= 0, row < all_rows)
    plane_in = jnp.logical_and(plane >= 0, plane < all_planes)
    to[m] = jnp.where(jnp.logical_and(row_in, plane_in), value, 1.0)


def geometry(planes, half, count_z, count_x):
    gz, gx = lax.axis_index("gz"), lax.axis_index("gx")
    odd = lax.rem(gz, 2)
    first_plane = (gz - odd - 1) * planes
    first_row = (2 * gx + odd) * half - HALO
    return odd == 1, first_plane, first_row, planes * count_z, 2 * half * count_x


def early(counts, own_n, own_w, par_n, par_w, one_n, one_w, send, carry, stats, *scratch):
    noisy, weight, cx_ref, acc = scratch[:4]
    state = scratch[4:]
    planes, ext, cols = own_n.shape
    half = ext - 2 * HALO
    odd, first_plane, first_row, all_planes, all_rows = geometry(planes, half, *counts)
    offset = jnp.where(odd, 0, planes)
    place_rows(cx_ref, first_row, all_rows)

    def place(base, n_ref, w_ref):
        def one(z, _):
            m = base + z
            value = n_ref[z]
            noisy[m] = value
            state[0][m] = value
            state[1][m] = value
            plane = first_plane + offset + m
            place_weight(weight, m, w_ref[z], plane, first_row, all_planes, all_rows)
            for ref in state[2:]:
                ref[m] = jnp.zeros_like(value)
            return 0

        lax.fori_loop(0, planes, one, 0)

    place(planes, par_n, par_w)

    def when_odd():
        place(0, one_n, one_w)
        place(2 * planes, own_n, own_w)

    def when_even():
        place(0, own_n, own_w)
        place(2 * planes, one_n, one_w)

    by_parity(odd, when_odd, when_even)
    acc[...] = jnp.zeros_like(acc)
    sweep = Sweep(state, weight, noisy, cx_ref, acc, offset, first_plane, all_planes)

    def iteration(k, _):
        by_parity(
            odd,
            lambda: sweep.step(k, k, True, False, False),
            lambda: sweep.step(k, planes + k, True, False, True),
        )
        sweep.loop(k, k + 1, jnp.where(odd, planes, 0), False)
        sweep.loop(
            k,
            jnp.where(odd, planes, planes + 1 + k),
            jnp.where(odd, 3 * planes - 1 - k, 3 * planes),
            True,
        )
        sweep.loop(k, 3 * planes, jnp.where(odd, 0, 4 * planes - 1 - k), False)
        return 0

    lax.fori_loop(0, ITERS, iteration, 0)
    rows = slice(HALO, HALO + half)

    def finish(first_carry, first_send):
        for a, ref in enumerate(state):
            carry[a] = ref[first_carry : first_carry + planes + 1]
        send[...] = state[0][first_send : first_send + planes, rows]

    by_parity(odd, lambda: finish(2 * planes - 1, planes), lambda: finish(0, planes))
    write_stats(stats, acc)


def write_stats(stats, acc, before=None):
    for k in range(ITERS):
        gap = acc[0, k] * (1.0 / dual_step) + acc[1, k]
        for row, value in ((k, gap), (ITERS + k, acc[2, k])):
            total = jnp.sum(value, axis=0, keepdims=True)
            if before is not None:
                total = total + before[row : row + 1]
            stats[row : row + 1] = total


def late(counts, own_n, own_w, two_n, two_w, carry, stats_in, keep, stats, *scratch):
    noisy, weight, cx_ref, acc = scratch[:4]
    state = scratch[4:]
    planes, ext, cols = own_n.shape
    half = ext - 2 * HALO
    odd, first_plane, first_row, all_planes, all_rows = geometry(planes, half, *counts)
    offset = jnp.where(odd, 2 * planes - 1, 0)
    place_rows(cx_ref, first_row, all_rows)

    def place(base, n_ref, w_ref, fresh):
        def one(z, _):
            m = base + z
            value = n_ref[z]
            noisy[m] = value
            plane = first_plane + offset + m
            place_weight(weight, m, w_ref[z], plane, first_row, all_planes, all_rows)
            if fresh:
                state[0][m] = value
                state[1][m] = value
                for ref in state[2:]:
                    ref[m] = jnp.zeros_like(value)
            return 0

        lax.fori_loop(0, planes, one, 0)

    def restore(base):
        def one(z, _):
            for a, ref in enumerate(state):
                ref[base + z] = carry[a, z]
            return 0

        lax.fori_loop(0, planes + 1, one, 0)

    def when_odd():
        restore(0)
        place(1, own_n, own_w, False)
        place(planes + 1, two_n, two_w, True)

    def when_even():
        place(0, two_n, two_w, True)
        place(planes, own_n, own_w, False)
        restore(planes)

    by_parity(odd, when_odd, when_even)
    acc[...] = jnp.zeros_like(acc)
    sweep = Sweep(state, weight, noisy, cx_ref, acc, offset, first_plane, all_planes)
    even = jnp.logical_not(odd)

    def iteration(k, _):
        @pl.when(even)
        def _():
            sweep.step(k, k, True, False, False)

        sweep.loop(k, k + 1, jnp.where(odd, 0, planes), False)
        sweep.loop(
            k,
            jnp.where(odd, 3 * planes - 1 - k, planes),
            jnp.where(odd, 3 * planes, planes + k),
            True,
        )
        sweep.loop(k, 3 * planes, jnp.where(odd, 4 * planes - 1 - k, 0), False)

        @pl.when(even)
        def _():
            sweep.step(k, planes + k, False, True, True)

        return 0

    lax.fori_loop(0, ITERS, iteration, 0)
    rows = slice(HALO, HALO + half)

    def finish(first):
        keep[...] = state[0][first : first + planes, rows]

    by_parity(odd, lambda: finish(1), lambda: finish(planes))
    write_stats(stats, acc, stats_in)


def pack_out(keep, got, out):
    half = keep.shape[1]

    def when_odd():
        out[:, 0:half] = got[...]
        out[:, half:] = keep[...]

    def when_even():
        out[:, 0:half] = keep[...]
        out[:, half:] = got[...]

    by_parity(is_odd(), when_odd, when_even)


def shards(noisy_volume, tv_weight):
    planes, rows, cols = noisy_volume.shape
    count_z, count_x = lax.axis_size("gz"), lax.axis_size("gx")
    if planes != ITERS or count_z % 2 or rows % (2 * SUB) or cols % LANE:
        raise ValueError("unsupported sizes")
    half = rows // 2
    ext = half + 2 * HALO
    cell_count = planes * rows * cols * count_z * count_x
    both = ("gz", "gx")
    odd = lax.rem(lax.axis_index("gz"), 2)

    def permute(value, step):
        pairs = []
        for z in range(count_z):
            for x in range(count_x):
                tz, tx = step(z, x)
                if 0 <= tz < count_z and 0 <= tx < count_x:
                    pairs.append((z * count_x + x, tz * count_x + tx))
        return lax.ppermute(value, both, pairs)

    swap = lambda z, x: (z ^ 1, x)
    edge_step_one = lambda z, x: (z, x - 1 if z % 2 else x + 1)
    edge_step_two = lambda z, x: (z ^ 1, x + 1 if z % 2 else x - 1)
    ghost_step_one = lambda z, x: (z + 2 if z % 2 else z - 2, x)
    ghost_step_two = lambda z, x: (z - 2 if z % 2 else z + 2, x)

    block = (planes, ext, cols)
    edge = (2, planes // 2, 2 * HALO, cols)
    near = (2, planes, SUB, cols)
    sent = (planes, half + SUB, cols)
    start = (1 - odd) * (rows - half - SUB)
    zero = jnp.zeros_like(start)
    send_n = lax.dynamic_slice(noisy_volume, (zero, start, zero), sent)
    got_n = permute(send_n, swap)
    edge_one, edge_two = vmem_call(
        pack_edges,
        [edge] * 2,
        [pl.ANY] * 2,
        scratch=[VMEM(near, jnp.float32)] * 2 + [pltpu.SemaphoreType.DMA((4,))],
        name="pack_edges",
    )(noisy_volume, tv_weight)
    got_one = permute(edge_one, edge_step_one)
    got_two = permute(edge_two, edge_step_two)
    send_w = lax.dynamic_slice(tv_weight, (zero, start, zero), sent)
    got_w = permute(send_w, swap)

    def pack(parts, bodies, got_edge, name):
        return vmem_call(
            functools.partial(pack_block, parts),
            [block] * len(parts),
            [VMEM] * (len(parts) + 1),
            name=name,
        )(*bodies, got_edge)

    own_n, own_w = pack(
        [(0, 0, half - HALO), (1, 0, half - HALO)], [noisy_volume, tv_weight], got_one, "pack_own"
    )
    one_n = permute(own_n, ghost_step_one)
    one_w = permute(own_w, ghost_step_one)
    (par_n,) = pack([(0, 0, SUB - HALO)], [got_n], got_two, "pack_partner_n")
    two_n = permute(par_n, ghost_step_two)
    (par_w,) = pack([(1, 0, SUB - HALO)], [got_w], got_two, "pack_partner_w")
    two_w = permute(par_w, ghost_step_two)

    out_half = (planes, half, cols)
    stats_shape = (2 * ITERS, LANE)
    counts = (count_z, count_x)
    small = [VMEM((ext, LANE), jnp.float32), VMEM((3, ITERS, SUB, LANE), jnp.float32)]

    def volumes(depth):
        one = VMEM((depth, ext, cols), jnp.float32)
        return [one] * 2 + small + [one] * 5

    send, carry, stats_early = vmem_call(
        functools.partial(early, counts),
        [out_half, (5, planes + 1, ext, cols), stats_shape],
        [VMEM] * 6,
        scratch=volumes(3 * planes),
        flops=100 << 20,
        limit=32,
        name="early",
    )(own_n, own_w, par_n, par_w, one_n, one_w)
    got = permute(send, swap)
    keep, stats = vmem_call(
        functools.partial(late, counts),
        [out_half, stats_shape],
        [VMEM] * 6,
        scratch=volumes(2 * planes + 1),
        flops=50 << 20,
        limit=32,
        name="late",
    )(own_n, own_w, two_n, two_w, carry, stats_early)

    if count_z & (count_z - 1) or count_x & (count_x - 1):
        stats = lax.psum(stats, both)
    else:
        step = 1
        while step < count_x:
            stats = stats + permute(stats, lambda z, x, d=step: (z, x ^ d))
            step *= 2
        step = 1
        while step < count_z:
            stats = stats + permute(stats, lambda z, x, d=step: (z ^ d, x))
            step *= 2
    totals = jnp.sum(stats, axis=1) / cell_count
    (out,) = vmem_call(pack_out, [(planes, rows, cols)], [VMEM] * 2, name="pack_out")(keep, got)
    return (out, totals[:ITERS], jnp.sqrt(totals[ITERS:]))


def solution(mesh):
    placed = (P("gz", "gx", None), P("gz", "gx", None))
    return jax.shard_map(
        shards,
        mesh=mesh,
        in_specs=placed,
        out_specs=(P("gz", "gx", None), P(), P()),
        check_vma=False,
    )
```

time: 156 us -> 85 us (0.54)
  blocking collectives: 44.9 us -> 0 us
  other arithmetic: 29.3 us -> 0.13 us
  Pallas kernels: 0 us -> 19 us
  starting transfers between devices: 45.6 us -> 34.2 us
  waiting for transfers between devices: 29.3 us -> 25.2 us
    psum x1 -> x0, blocking collectives: 44.9 us -> none  [shards(): lax.psum((jnp.stack(gap_list), jnp.stack(step_list)), ('gz', 'gx'))]
    pallas_call x0 -> x7, Pallas kernels: none -> 19 us  [the longest x1 11.9 us: shards(): vmem_call(functools.partial(early, counts), [out_half, (5, planes + 1, ex...]
    ppermute x22 -> x14, starting transfers between devices: 45.6 us -> 34.2 us  [permute(): return lax.ppermute(value, both, pairs)]
    reduce_sum x2 -> x1, other arithmetic: 10.7 us -> 0.11 us  [shards(): totals = jnp.sum(stats, axis=1) / cell_count]
    sub x10 -> x0, other arithmetic: 6.17 us -> none  [the longest x7 3.94 us: gradient(): volume[:, :, 1:] - volume[:, :, :-1]]
    mul x8 -> x0, other arithmetic: 6.13 us -> none  [shards(): dual_field = tuple((part * shrink for part in proposed))]
    another operation x2 -> x0, other arithmetic: 5.25 us -> none  [the longest x1 2.7 us: shards(): jnp.stack(step_list)]
    slice x42 -> x0, local copies, waits for them, and re-layouts: 4.28 us -> none  [the longest x7 1.08 us: shards(): next_planes = shifted_2((primal[:1], extrapolated[:1]), 'gz', -1)]
  transfers between devices with their start and end apart: 22 -> 14, of which waited for: 12 -> 9; matrix products, arithmetic and copies ran while one was open for 7% -> 1% of each run, Pallas kernels for 0% -> 22%
where the time goes in v2:
time: 85 us; the launch traced here: 84.6 us
  starting transfers between devices  34.2 us (40%)
  waiting for transfers between devices  25.2 us (30%)
  Pallas kernels  19 us (22%)
  local copies, waits for them, and re-layouts  5.26 us (6%)
    ppermute x14, starting transfers between devices, permute(): return lax.ppermute(value, both, pairs)  34.2 us
    ppermute x14, waiting for transfers between devices, permute(): return lax.ppermute(value, both, pairs)  25.2 us
    pallas_call x1, Pallas kernels, shards(): vmem_call(functools.partial(early, counts), [out_half, (5, planes + 1, ex...  11.9 us
    pallas_call x1, Pallas kernels, shards(): vmem_call(functools.partial(late, counts), [out_half, stats_shape], [VMEM...  5.68 us
    unnamed x4, local copies, waits for them, and re-layouts  2.45 us
  transfers between devices with their start and end apart: 14, of which 9 were waited for; matrix products, arithmetic and copies ran while one was open for 1% of the time, Pallas kernels for 22%

profile of v2, /device:TPU:0, one launch (start us, length us, event | category | flops | bytes accessed | tf_op | source)
XLA Modules:
  0.0 84.6 jit_solution(12167409030349613828)
XLA Ops:
  0.6 1.1 %constant_dynamic-slice_fusion.1 = f32[4,72,512]{2,1,0:T(8,128)S(1)} fusion(f32[4,128,512]{2,1,0:T(8,128)} %refs_0_.1, s32[]{:T(128)S(6)} %select_n.4), kind=kLoop, calls=%fused_computation.3 | loop fusion | bytes 1179652 | tf_op jit(solution)/shard_map/dynamic_slice | solution.py:450
  1.8 3.0 %collective-permute-start.1 = (f32[4,72,512]{2,1,0:T(8,128)S(1)}, f32[4,72,512]{2,1,0:T(8,128)S(1)}, u32[]{:S(2)}, u32[]{:S(2)}) collective-permute-start(f32[4,72,512]{2,1,0:T(8,128)S(1)} %constant_dynamic-slice_fusion.1), channel_id=1, source_target_pairs={{0,4},{1,5},{2,6},{3,7},{4,0},{5,1},{6,2},{7,3},{8,12},{9,13},{10,... | collective-permute-start | bytes 1769480 | tf_op jit(solution)/shard_map/ppermute | solution.py:436
  4.8 1.1 %constant_dynamic-slice_fusion = f32[4,72,512]{2,1,0:T(8,128)S(1)} fusion(f32[4,128,512]{2,1,0:T(8,128)} %refs_1_.1, s32[]{:T(128)S(6)} %select_n.4), kind=kLoop, calls=%fused_computation.2 | loop fusion | bytes 1179652 | tf_op jit(solution)/shard_map/dynamic_slice | solution.py:461
  6.0 1.2 %copy-done = f32[4,128,512]{2,1,0:T(8,128)S(1)} copy-done((f32[4,128,512]{2,1,0:T(8,128)S(1)}, f32[4,128,512]{2,1,0:T(8,128)}, u32[]{:S(2)}) %copy-start) | copy-done | bytes 1048600
  7.2 1.2 %copy-done.1 = f32[4,128,512]{2,1,0:T(8,128)S(1)} copy-done((f32[4,128,512]{2,1,0:T(8,128)S(1)}, f32[4,128,512]{2,1,0:T(8,128)}, u32[]{:S(2)}) %copy-start.1) | copy-done | bytes 1048600
  8.4 0.2 pack_edges.1
  8.6 1.5 %collective-permute-start = (f32[2,2,8,512]{3,2,1,0:T(8,128)S(1)}, f32[2,2,8,512]{3,2,1,0:T(8,128)S(1)}, u32[]{:S(2)}, u32[]{:S(2)}) collective-permute-start(f32[2,2,8,512]{3,2,1,0:T(8,128)S(1)} %get-tuple-element.12), channel_id=1, source_target_pairs={{0,1},{1,2},{2,3},{5,4},{6,5},{7,6},{8,9},{9,10},{10,11},{13,12},{... | collective-permute-start | bytes 196616 | tf_op jit(solution)/shard_map/ppermute | solution.py:436
  10.1 0.9 %collective-permute-done.refs_2_ = f32[2,2,8,512]{3,2,1,0:T(8,128)S(1)} collective-permute-done((f32[2,2,8,512]{3,2,1,0:T(8,128)S(1)}, f32[2,2,8,512]{3,2,1,0:T(8,128)S(1)}, u32[]{:S(2)}, u32[]{:S(2)}) %collective-permute-start) | collective-permute-done | bytes 65568 | tf_op jit(solution)/shard_map/ppermute | solution.py:436
  11.0 1.3 %collective-permute-start.6 = (f32[4,72,512]{2,1,0:T(8,128)S(1)}, f32[4,72,512]{2,1,0:T(8,128)S(1)}, u32[]{:S(2)}, u32[]{:S(2)}) collective-permute-start(f32[4,72,512]{2,1,0:T(8,128)S(1)} %get-tuple-element.13.own_n), channel_id=1, source_target_pairs={{4,12},{5,13},{6,14},{7,15},{8,0},{9,1},{10,2},{11,3},{12,20},{13,... | collective-permute-start | bytes 1769480 | tf_op jit(solution)/shard_map/ppermute | solution.py:436
  12.3 1.3 %collective-permute-start.7 = (f32[4,72,512]{2,1,0:T(8,128)S(1)}, f32[4,72,512]{2,1,0:T(8,128)S(1)}, u32[]{:S(2)}, u32[]{:S(2)}) collective-permute-start(f32[4,72,512]{2,1,0:T(8,128)S(1)} %get-tuple-element.14.own_w), channel_id=1, source_target_pairs={{4,12},{5,13},{6,14},{7,15},{8,0},{9,1},{10,2},{11,3},{12,20},{13,... | collective-permute-start | bytes 1769480 | tf_op jit(solution)/shard_map/ppermute | solution.py:436
  13.6 0.7 collective-permute-start.2
  14.3 4.6 %collective-permute-done.1.refs_0_ = f32[4,72,512]{2,1,0:T(8,128)S(1)} collective-permute-done((f32[4,72,512]{2,1,0:T(8,128)S(1)}, f32[4,72,512]{2,1,0:T(8,128)S(1)}, u32[]{:S(2)}, u32[]{:S(2)}) %collective-permute-start.1) | collective-permute-done | bytes 589856 | tf_op jit(solution)/shard_map/ppermute | solution.py:436
  19.0 4.0 %collective-permute-start.3 = (f32[4,72,512]{2,1,0:T(8,128)S(1)}, f32[4,72,512]{2,1,0:T(8,128)S(1)}, u32[]{:S(2)}, u32[]{:S(2)}) collective-permute-start(f32[4,72,512]{2,1,0:T(8,128)S(1)} %pack_partner_n.1.par_n), channel_id=1, source_target_pairs={{0,8},{1,9},{2,10},{3,11},{8,16},{9,17},{10,18},{11,19},{12,4},{13... | collective-permute-start | bytes 1769480 | tf_op jit(solution)/shard_map/ppermute | solution.py:436
  23.1 8.4 %collective-permute-done.4.refs_0_ = f32[4,72,512]{2,1,0:T(8,128)S(1)} collective-permute-done((f32[4,72,512]{2,1,0:T(8,128)S(1)}, f32[4,72,512]{2,1,0:T(8,128)S(1)}, u32[]{:S(2)}, u32[]{:S(2)}) %collective-permute-start.4) | collective-permute-done | bytes 589856 | tf_op jit(solution)/shard_map/ppermute | solution.py:436
  31.5 3.8 %collective-permute-start.5 = (f32[4,72,512]{2,1,0:T(8,128)S(1)}, f32[4,72,512]{2,1,0:T(8,128)S(1)}, u32[]{:S(2)}, u32[]{:S(2)}) collective-permute-start(f32[4,72,512]{2,1,0:T(8,128)S(1)} %pack_partner_w.1.par_w), channel_id=1, source_target_pairs={{0,8},{1,9},{2,10},{3,11},{8,16},{9,17},{10,18},{11,19},{12,4},{13... | collective-permute-start | bytes 1769480 | tf_op jit(solution)/shard_map/ppermute | solution.py:436
  35.3 4.4 %collective-permute-done.7.one_w = f32[4,72,512]{2,1,0:T(8,128)S(1)} collective-permute-done((f32[4,72,512]{2,1,0:T(8,128)S(1)}, f32[4,72,512]{2,1,0:T(8,128)S(1)}, u32[]{:S(2)}, u32[]{:S(2)}) %collective-permute-start.7) | collective-permute-done | bytes 589856 | tf_op jit(solution)/shard_map/ppermute | solution.py:436
  39.7 11.9 %early.1 = (f32[4,64,512]{2,1,0:T(8,128)S(1)}, f32[5,5,72,512]{3,2,1,0:T(8,128)S(1)}, f32[8,128]{1,0:T(8,128)S(1)}) custom-call(f32[4,72,512]{2,1,0:T(8,128)S(1)} %get-tuple-element.13.own_n, f32[4,72,512]{2,1,0:T(8,128)S(1)} %get-tuple-element.14.own_w, f32[4,72,512]{2,1,0:T(8,128)S(1)} %pack_partner_n.1.par_n, f32[4,72,512]{2,1,0:T(8,128)S(1)} %pack_partner_w.1.par_w, ...), custom_call_target="tpu_custom_call" | custom-call | flops 104857600 | bytes 1048576 | tf_op jit(solution)/shard_map/early/pallas_call | solution.py:491
  51.7 1.9 %collective-permute-start.8 = (f32[4,64,512]{2,1,0:T(8,128)S(1)}, f32[4,64,512]{2,1,0:T(8,128)S(1)}, u32[]{:S(2)}, u32[]{:S(2)}) collective-permute-start(f32[4,64,512]{2,1,0:T(8,128)S(1)} %get-tuple-element.19), channel_id=1, source_target_pairs={{0,4},{1,5},{2,6},{3,7},{4,0},{5,1},{6,2},{7,3},{8,12},{9,13},{10,... | collective-permute-start | bytes 1572872 | tf_op jit(solution)/shard_map/ppermute | solution.py:436
  53.6 5.7 %late.1 = (f32[4,64,512]{2,1,0:T(8,128)S(1)}, f32[8,128]{1,0:T(8,128)S(1)}) custom-call(f32[4,72,512]{2,1,0:T(8,128)S(1)} %get-tuple-element.13.own_n, f32[4,72,512]{2,1,0:T(8,128)S(1)} %get-tuple-element.14.own_w, f32[4,72,512]{2,1,0:T(8,128)S(1)} %collective-permute-done.3.two_n, f32[4,72,512]{2,1,0:T(8,128)S(1)} %collective-permute-done.5.two_w, ...), custom_call_target="tpu_custom_call" | custom-call | flops 52428800 | bytes 1048576 | tf_op jit(solution)/shard_map/late/pallas_call | solution.py:501
  59.3 1.7 %collective-permute-start.9 = (f32[8,128]{1,0:T(8,128)S(1)}, f32[8,128]{1,0:T(8,128)S(1)}, u32[]{:S(2)}, u32[]{:S(2)}) collective-permute-start(f32[8,128]{1,0:T(8,128)S(1)} %get-tuple-element.20), channel_id=1, source_target_pairs={{0,1},{1,0},{2,3},{3,2},{4,5},{5,4},{6,7},{7,6},{8,9},{9,8},{10,11... | collective-permute-start | bytes 12296 | tf_op jit(solution)/shard_map/ppermute | solution.py:436
  61.0 0.8 collective-permute-done.9
  61.8 7.4 %collective-permute-start.10 = (f32[8,128]{1,0:T(8,128)S(1)}, f32[8,128]{1,0:T(8,128)S(1)}, u32[]{:S(2)}, u32[]{:S(2)}) collective-permute-start(f32[8,128]{1,0:T(8,128)S(1)} %add.20), channel_id=1, source_target_pairs={{0,2},{1,3},{2,0},{3,1},{4,6},{5,7},{6,4},{7,5},{8,10},{9,11},{10,... | collective-permute-start | bytes 12296 | tf_op jit(solution)/shard_map/ppermute | solution.py:436
  69.2 1.6 %collective-permute-done.10 = f32[8,128]{1,0:T(8,128)S(1)} collective-permute-done((f32[8,128]{1,0:T(8,128)S(1)}, f32[8,128]{1,0:T(8,128)S(1)}, u32[]{:S(2)}, u32[]{:S(2)}) %collective-permute-start.10) | collective-permute-done | bytes 4128 | tf_op jit(solution)/shard_map/ppermute | solution.py:436
  70.8 3.4 %collective-permute-start.11 = (f32[8,128]{1,0:T(8,128)S(1)}, f32[8,128]{1,0:T(8,128)S(1)}, u32[]{:S(2)}, u32[]{:S(2)}) collective-permute-start(f32[8,128]{1,0:T(8,128)S(1)} %add.21), channel_id=1, source_target_pairs={{0,4},{1,5},{2,6},{3,7},{4,0},{5,1},{6,2},{7,3},{8,12},{9,13},{10,... | collective-permute-start | bytes 12296 | tf_op jit(solution)/shard_map/ppermute | solution.py:436
  74.1 1.6 %collective-permute-done.11 = f32[8,128]{1,0:T(8,128)S(1)} collective-permute-done((f32[8,128]{1,0:T(8,128)S(1)}, f32[8,128]{1,0:T(8,128)S(1)}, u32[]{:S(2)}, u32[]{:S(2)}) %collective-permute-start.11) | collective-permute-done | bytes 4128 | tf_op jit(solution)/shard_map/ppermute | solution.py:436
  75.7 1.6 %collective-permute-start.12 = (f32[8,128]{1,0:T(8,128)S(1)}, f32[8,128]{1,0:T(8,128)S(1)}, u32[]{:S(2)}, u32[]{:S(2)}) collective-permute-start(f32[8,128]{1,0:T(8,128)S(1)} %add.22), channel_id=1, source_target_pairs={{0,8},{1,9},{2,10},{3,11},{4,12},{5,13},{6,14},{7,15},{8,0},{9,1},... | collective-permute-start | bytes 12296 | tf_op jit(solution)/shard_map/ppermute | solution.py:436
  77.3 2.0 %collective-permute-done.12 = f32[8,128]{1,0:T(8,128)S(1)} collective-permute-done((f32[8,128]{1,0:T(8,128)S(1)}, f32[8,128]{1,0:T(8,128)S(1)}, u32[]{:S(2)}, u32[]{:S(2)}) %collective-permute-start.12) | collective-permute-done | bytes 4128 | tf_op jit(solution)/shard_map/ppermute | solution.py:436
  79.3 2.6 %collective-permute-start.13 = (f32[8,128]{1,0:T(8,128)S(1)}, f32[8,128]{1,0:T(8,128)S(1)}, u32[]{:S(2)}, u32[]{:S(2)}) collective-permute-start(f32[8,128]{1,0:T(8,128)S(1)} %add.23), channel_id=1, source_target_pairs={{0,16},{1,17},{2,18},{3,19},{4,20},{5,21},{6,22},{7,23},{8,24},{9,... | collective-permute-start | bytes 12296 | tf_op jit(solution)/shard_map/ppermute | solution.py:436
  81.9 1.0 %pack_out.1 = f32[4,128,512]{2,1,0:T(8,128)} custom-call(f32[4,64,512]{2,1,0:T(8,128)S(1)} %get-tuple-element.18.keep, f32[4,64,512]{2,1,0:T(8,128)S(1)} %collective-permute-done.8.got), custom_call_target="tpu_custom_call" | custom-call | flops 1048576 | bytes 1048576 | tf_op jit(solution)/shard_map/pack_out/pallas_call | solution.py:523
  83.0 0.9 %collective-permute-done.13 = f32[8,128]{1,0:T(8,128)S(1)} collective-permute-done((f32[8,128]{1,0:T(8,128)S(1)}, f32[8,128]{1,0:T(8,128)S(1)}, u32[]{:S(2)}, u32[]{:S(2)}) %collective-permute-start.13) | collective-permute-done | bytes 4128 | tf_op jit(solution)/shard_map/ppermute | solution.py:436
  83.8 0.1 add_reduce_fusion
  84.0 0.6 slice_sqrt_fusion
  (16 shorter events, 0.3 us)
Async XLA Ops:
  1.8 17.2 %collective-permute-start.1 = (f32[4,72,512]{2,1,0:T(8,128)S(1)}, f32[4,72,512]{2,1,0:T(8,128)S(1)}, u32[]{:S(2)}, u32[]{:S(2)}) collective-permute-start(f32[4,72,512]{2,1,0:T(8,128)S(1)} %constant_dynamic-slice_fusion.1), channel_id=1, source_target_pairs={{0,4},{1,5},{2,6},{3,7},{4,0},{5,1},{6,2},{7,3},{8,12},{9,13},{10,... | collective-permute-start | bytes 1769480 | tf_op jit(solution)/shard_map/ppermute | solution.py:436
  5.9 25.6 %collective-permute-start.4 = (f32[4,72,512]{2,1,0:T(8,128)S(1)}, f32[4,72,512]{2,1,0:T(8,128)S(1)}, u32[]{:S(2)}, u32[]{:S(2)}) collective-permute-start(f32[4,72,512]{2,1,0:T(8,128)S(1)} %constant_dynamic-slice_fusion), channel_id=1, source_target_pairs={{0,4},{1,5},{2,6},{3,7},{4,0},{5,1},{6,2},{7,3},{8,12},{9,13},{10,... | collective-permute-start | bytes 1769480 | tf_op jit(solution)/shard_map/ppermute | solution.py:436
  6.0 1.2 %copy-start = (f32[4,128,512]{2,1,0:T(8,128)S(1)}, f32[4,128,512]{2,1,0:T(8,128)}, u32[]{:S(2)}) copy-start(f32[4,128,512]{2,1,0:T(8,128)} %refs_0_.1) | copy-start | bytes 3145732
  7.2 1.2 %copy-start.1 = (f32[4,128,512]{2,1,0:T(8,128)S(1)}, f32[4,128,512]{2,1,0:T(8,128)}, u32[]{:S(2)}) copy-start(f32[4,128,512]{2,1,0:T(8,128)} %refs_1_.1) | copy-start | bytes 3145732
  8.6 2.4 %collective-permute-start = (f32[2,2,8,512]{3,2,1,0:T(8,128)S(1)}, f32[2,2,8,512]{3,2,1,0:T(8,128)S(1)}, u32[]{:S(2)}, u32[]{:S(2)}) collective-permute-start(f32[2,2,8,512]{3,2,1,0:T(8,128)S(1)} %get-tuple-element.12), channel_id=1, source_target_pairs={{0,1},{1,2},{2,3},{5,4},{6,5},{7,6},{8,9},{9,10},{10,11},{13,12},{... | collective-permute-start | bytes 196616 | tf_op jit(solution)/shard_map/ppermute | solution.py:436
  11.0 24.2 %collective-permute-start.6 = (f32[4,72,512]{2,1,0:T(8,128)S(1)}, f32[4,72,512]{2,1,0:T(8,128)S(1)}, u32[]{:S(2)}, u32[]{:S(2)}) collective-permute-start(f32[4,72,512]{2,1,0:T(8,128)S(1)} %get-tuple-element.13.own_n), channel_id=1, source_target_pairs={{4,12},{5,13},{6,14},{7,15},{8,0},{9,1},{10,2},{11,3},{12,20},{13,... | collective-permute-start | bytes 1769480 | tf_op jit(solution)/shard_map/ppermute | solution.py:436
  12.3 27.4 %collective-permute-start.7 = (f32[4,72,512]{2,1,0:T(8,128)S(1)}, f32[4,72,512]{2,1,0:T(8,128)S(1)}, u32[]{:S(2)}, u32[]{:S(2)}) collective-permute-start(f32[4,72,512]{2,1,0:T(8,128)S(1)} %get-tuple-element.14.own_w), channel_id=1, source_target_pairs={{4,12},{5,13},{6,14},{7,15},{8,0},{9,1},{10,2},{11,3},{12,20},{13,... | collective-permute-start | bytes 1769480 | tf_op jit(solution)/shard_map/ppermute | solution.py:436
  13.6 0.7 collective-permute-start.2
  19.0 34.6 %collective-permute-start.3 = (f32[4,72,512]{2,1,0:T(8,128)S(1)}, f32[4,72,512]{2,1,0:T(8,128)S(1)}, u32[]{:S(2)}, u32[]{:S(2)}) collective-permute-start(f32[4,72,512]{2,1,0:T(8,128)S(1)} %pack_partner_n.1.par_n), channel_id=1, source_target_pairs={{0,8},{1,9},{2,10},{3,11},{8,16},{9,17},{10,18},{11,19},{12,4},{13... | collective-permute-start | bytes 1769480 | tf_op jit(solution)/shard_map/ppermute | solution.py:436
  31.5 22.1 %collective-permute-start.5 = (f32[4,72,512]{2,1,0:T(8,128)S(1)}, f32[4,72,512]{2,1,0:T(8,128)S(1)}, u32[]{:S(2)}, u32[]{:S(2)}) collective-permute-start(f32[4,72,512]{2,1,0:T(8,128)S(1)} %pack_partner_w.1.par_w), channel_id=1, source_target_pairs={{0,8},{1,9},{2,10},{3,11},{8,16},{9,17},{10,18},{11,19},{12,4},{13... | collective-permute-start | bytes 1769480 | tf_op jit(solution)/shard_map/ppermute | solution.py:436
  51.7 30.3 %collective-permute-start.8 = (f32[4,64,512]{2,1,0:T(8,128)S(1)}, f32[4,64,512]{2,1,0:T(8,128)S(1)}, u32[]{:S(2)}, u32[]{:S(2)}) collective-permute-start(f32[4,64,512]{2,1,0:T(8,128)S(1)} %get-tuple-element.19), channel_id=1, source_target_pairs={{0,4},{1,5},{2,6},{3,7},{4,0},{5,1},{6,2},{7,3},{8,12},{9,13},{10,... | collective-permute-start | bytes 1572872 | tf_op jit(solution)/shard_map/ppermute | solution.py:436
  59.3 2.5 %collective-permute-start.9 = (f32[8,128]{1,0:T(8,128)S(1)}, f32[8,128]{1,0:T(8,128)S(1)}, u32[]{:S(2)}, u32[]{:S(2)}) collective-permute-start(f32[8,128]{1,0:T(8,128)S(1)} %get-tuple-element.20), channel_id=1, source_target_pairs={{0,1},{1,0},{2,3},{3,2},{4,5},{5,4},{6,7},{7,6},{8,9},{9,8},{10,11... | collective-permute-start | bytes 12296 | tf_op jit(solution)/shard_map/ppermute | solution.py:436
  61.8 8.9 %collective-permute-start.10 = (f32[8,128]{1,0:T(8,128)S(1)}, f32[8,128]{1,0:T(8,128)S(1)}, u32[]{:S(2)}, u32[]{:S(2)}) collective-permute-start(f32[8,128]{1,0:T(8,128)S(1)} %add.20), channel_id=1, source_target_pairs={{0,2},{1,3},{2,0},{3,1},{4,6},{5,7},{6,4},{7,5},{8,10},{9,11},{10,... | collective-permute-start | bytes 12296 | tf_op jit(solution)/shard_map/ppermute | solution.py:436
  70.8 5.0 %collective-permute-start.11 = (f32[8,128]{1,0:T(8,128)S(1)}, f32[8,128]{1,0:T(8,128)S(1)}, u32[]{:S(2)}, u32[]{:S(2)}) collective-permute-start(f32[8,128]{1,0:T(8,128)S(1)} %add.21), channel_id=1, source_target_pairs={{0,4},{1,5},{2,6},{3,7},{4,0},{5,1},{6,2},{7,3},{8,12},{9,13},{10,... | collective-permute-start | bytes 12296 | tf_op jit(solution)/shard_map/ppermute | solution.py:436
  75.7 3.6 %collective-permute-start.12 = (f32[8,128]{1,0:T(8,128)S(1)}, f32[8,128]{1,0:T(8,128)S(1)}, u32[]{:S(2)}, u32[]{:S(2)}) collective-permute-start(f32[8,128]{1,0:T(8,128)S(1)} %add.22), channel_id=1, source_target_pairs={{0,8},{1,9},{2,10},{3,11},{4,12},{5,13},{6,14},{7,15},{8,0},{9,1},... | collective-permute-start | bytes 12296 | tf_op jit(solution)/shard_map/ppermute | solution.py:436
  79.3 4.5 %collective-permute-start.13 = (f32[8,128]{1,0:T(8,128)S(1)}, f32[8,128]{1,0:T(8,128)S(1)}, u32[]{:S(2)}, u32[]{:S(2)}) collective-permute-start(f32[8,128]{1,0:T(8,128)S(1)} %add.23), channel_id=1, source_target_pairs={{0,16},{1,17},{2,18},{3,19},{4,20},{5,21},{6,22},{7,23},{8,24},{9,... | collective-permute-start | bytes 12296 | tf_op jit(solution)/shard_map/ppermute | solution.py:436

commit v3 on v2

v3 whole, which is shorter than its diff:
```python
import functools

import jax
import jax.numpy as jnp
from jax import lax
from jax.experimental import pallas as pl
from jax.experimental.pallas import tpu as pltpu
from jax.sharding import PartitionSpec as P


ITERS = 4
primal_step = 0.28
dual_step = 0.28

SUB = 8
LANE = 128
HALO = ITERS
VMEM = pltpu.VMEM


def vmem_call(body, shapes, spaces, scratch=(), flops=1 << 20, limit=16, aliases=None):
    return pl.pallas_call(
        body,
        out_shape=[jax.ShapeDtypeStruct(s, jnp.float32) for s in shapes],
        in_specs=[pl.BlockSpec(memory_space=s) for s in spaces],
        out_specs=[pl.BlockSpec(memory_space=VMEM)] * len(shapes),
        scratch_shapes=list(scratch),
        input_output_aliases=aliases or {},
        compiler_params=pltpu.CompilerParams(vmem_limit_bytes=limit << 20),
        cost_estimate=pl.CostEstimate(flops=flops, bytes_accessed=1 << 20, transcendentals=0),
    )


def is_odd():
    return lax.rem(lax.axis_index("gz"), 2) == 1


def by_parity(odd, when_odd, when_even):
    pl.when(odd)(when_odd)
    pl.when(jnp.logical_not(odd))(when_even)


def move_rows(planes, rows, half, odd, whole, send, own):
    used = half + HALO
    for z in range(planes):
        base = used * (z % 2)
        low, high = whole[z, 0:used], whole[z, rows - used : rows]
        send[z // 2][z // 2 if len(set(map(id, send))) == 1 else 0, base : base + used] = (
            low if odd else high
        )
        own[z // 2, base : base + used] = high if odd else low


def pack_first(noisy, weight, send_n, own_n, edge_one, edge_two, whole, low, high, sems):
    planes, rows, _ = noisy.shape
    half = rows // 2
    copies = [
        pltpu.make_async_copy(noisy, whole, sems.at[0]),
        pltpu.make_async_copy(weight.at[:, 0:SUB], low, sems.at[1]),
        pltpu.make_async_copy(weight.at[:, rows - SUB : rows], high, sems.at[2]),
    ]
    for copy in copies:
        copy.start()
    for copy in copies:
        copy.wait()

    def fill(to, at_low):
        for j in range(planes // 2):
            for b in range(2):
                rows_to = slice(HALO * b, HALO * (b + 1))
                z = 2 * j + b
                to[0, j, rows_to] = whole[z, 0:HALO] if at_low else whole[z, rows - HALO : rows]
                to[1, j, rows_to] = low[z, 0:HALO] if at_low else high[z, SUB - HALO : SUB]

    def run(odd):
        fill(edge_one, odd)
        fill(edge_two, not odd)
        move_rows(planes, rows, half, odd, whole, [send_n] * (planes // 2), own_n)

    by_parity(is_odd(), lambda: run(True), lambda: run(False))


def pack_second(weight, *refs):
    send, own_w, whole, sem = refs[:-3], refs[-3], refs[-2], refs[-1]
    planes, rows, _ = weight.shape
    copy = pltpu.make_async_copy(weight, whole, sem)
    copy.start()
    copy.wait()
    run = lambda odd: move_rows(planes, rows, rows // 2, odd, whole, send, own_w)
    by_parity(is_odd(), lambda: run(True), lambda: run(False))


class Sweep:
    def __init__(self, state, cx_ref, acc, first_plane, all_planes):
        self.noisy, self.weight, self.u, self.bar, self.p_z, self.p_x, self.p_y = state
        self.cx_ref, self.acc = cx_ref, acc
        self.first_plane, self.all_planes = first_plane, all_planes
        _, self.ext, cols = self.weight.shape
        self.strips, self.chunks = self.ext // SUB, cols // LANE
        lane = lax.broadcasted_iota(jnp.int32, (SUB, LANE), 1)
        self.sub = lax.broadcasted_iota(jnp.int32, (SUB, LANE), 0)
        self.first_sub, self.last_sub = self.sub == 0, self.sub == SUB - 1
        self.first_lane, self.last_lane = lane == 0, lane == LANE - 1

    def load(self, ref, m, s):
        return [
            ref[m, s * SUB : (s + 1) * SUB, c * LANE : (c + 1) * LANE] for c in range(self.chunks)
        ]

    def save(self, ref, m, s, values):
        for c in range(self.chunks):
            ref[m, s * SUB : (s + 1) * SUB, c * LANE : (c + 1) * LANE] = values[c]

    def gradient(self, x, above, rolled, rolled_next, cz, cx):
        side = [pltpu.roll(v, LANE - 1, 1) for v in x]
        out = []
        for c in range(self.chunks):
            last = c + 1 == self.chunks
            y_next = side[c] if last else jnp.where(self.last_lane, side[c + 1], side[c])
            d_z = (above[c] - x[c]) * cz
            down = jnp.where(self.last_sub, rolled_next[c], rolled[c])
            d_x = (down - x[c]) * cx
            d_y = (y_next - x[c]) * dual_step
            if last:
                d_y = jnp.where(self.last_lane, 0.0, d_y)
            out.append((d_z, d_x, d_y))
        return out

    def step(self, k, m, do_p, do_u, own, first):
        u_ref, bar_ref = (self.noisy, self.noisy) if first else (self.u, self.bar)
        plane = self.first_plane + m
        z_in = jnp.logical_and(plane >= 0, plane < self.all_planes - 1)
        cz = jnp.where(z_in, dual_step, 0.0).astype(jnp.float32)
        zero = jnp.zeros((SUB, LANE), jnp.float32)
        tv_sum, quad_sum, step_sum = zero, zero, zero
        load, save, strips, chunks = self.load, self.save, self.strips, self.chunks
        row_up = lambda x: [pltpu.roll(v, SUB - 1, 0) for v in x]
        if do_p:
            bar_now = load(bar_ref, m, 0)
            bar_roll = row_up(bar_now)
            if own and not first:
                u_now = load(u_ref, m, 0)
                u_roll = row_up(u_now)
        px_roll_before = None
        for s in range(strips):
            more = s + 1 < strips
            part, quad, step = zero, zero, zero
            if do_p:
                cx = self.cx_ref[s * SUB : (s + 1) * SUB]
                bar_next = load(bar_ref, m, s + 1) if more else bar_now
                bar_roll_next = row_up(bar_next) if more else bar_roll
                above = load(bar_ref, m + 1, s)
                g_bar = self.gradient(bar_now, above, bar_roll, bar_roll_next, cz, cx)
                w = load(self.weight, m, s)
                g_u = g_bar
                if own and not first:
                    u_next = load(u_ref, m, s + 1) if more else u_now
                    u_roll_next = row_up(u_next) if more else u_roll
                    above = load(u_ref, m + 1, s)
                    g_u = self.gradient(u_now, above, u_roll, u_roll_next, cz, cx)
                if own:
                    for c in range(chunks):
                        a, b, d = g_u[c]
                        part = part + w[c] * jnp.sqrt(a * a + b * b + d * d)
            if first and do_p:
                pz, px, py = ([None] * chunks for _ in range(3))
            else:
                pz, px, py = load(self.p_z, m, s), load(self.p_x, m, s), load(self.p_y, m, s)
            if do_p:
                for c in range(chunks):
                    a, b, d = g_bar[c]
                    if not first:
                        a, b, d = pz[c] + a, px[c] + b, py[c] + d
                    shrink = jnp.minimum(1.0, w[c] * lax.rsqrt(a * a + b * b + d * d))
                    pz[c], px[c], py[c] = a * shrink, b * shrink, d * shrink
                save(self.p_z, m, s, pz)
                save(self.p_x, m, s, px)
                save(self.p_y, m, s, py)
            if do_u:
                pz_below = load(self.p_z, m - 1, s)
                px_roll = [pltpu.roll(v, 1, 0) for v in px]
                before = px_roll_before if s else px_roll
                py_roll = [pltpu.roll(v, 1, 1) for v in py]
                n = load(self.noisy, m, s)
                old = u_now if own and do_p and not first else load(u_ref, m, s)
                new, new_bar = [], []
                for c in range(chunks):
                    x_before = jnp.where(self.first_sub, before[c], px_roll[c])
                    y_before = jnp.where(self.first_lane, py_roll[c - 1] if c else 0.0, py_roll[c])
                    spread = (pz[c] - pz_below[c]) + (px[c] - x_before) + (py[c] - y_before)
                    shifted = n[c] + spread
                    updated = (old[c] + primal_step * shifted) * (1.0 / (1.0 + primal_step))
                    change = updated - old[c]
                    new.append(updated)
                    new_bar.append(updated + change)
                    if own:
                        quad = quad + (old[c] * (0.5 * old[c] - n[c]) + 0.5 * (shifted * shifted))
                        step = step + change * change
                save(self.u, m, s, new)
                save(self.bar, m, s, new_bar)
                px_roll_before = px_roll
            if own:
                if s == 0:
                    part, quad, step = (
                        jnp.where(self.sub >= HALO, v, 0.0) for v in (part, quad, step)
                    )
                if not more:
                    part, quad, step = (
                        jnp.where(self.sub < HALO, v, 0.0) for v in (part, quad, step)
                    )
                tv_sum, quad_sum, step_sum = tv_sum + part, quad_sum + quad, step_sum + step
            if do_p:
                bar_now, bar_roll = bar_next, bar_roll_next
                if own and not first:
                    u_now, u_roll = u_next, u_roll_next
        if own:
            if do_p:
                self.acc[0, k] += tv_sum
            if do_u:
                self.acc[1, k] += quad_sum
                self.acc[2, k] += step_sum

    def loop(self, k, low, high, own, first):
        def body(i, _):
            self.step(k, i, True, True, own, first)
            return 0

        lax.fori_loop(low, high, body, 0)


def place_rows(cx_ref, first_row, all_rows):
    sub = lax.broadcasted_iota(jnp.int32, (SUB, LANE), 0)
    for s in range(cx_ref.shape[0] // SUB):
        row = first_row + s * SUB + sub
        inside = jnp.logical_and(row >= 0, row < all_rows - 1)
        cx_ref[s * SUB : (s + 1) * SUB] = jnp.where(inside, dual_step, 0.0).astype(jnp.float32)


def place(odd, base, raw_n, raw_w, edge, state, edge_in, block_in):
    noisy, weight = state[:2]
    planes = 2 * edge.shape[1]
    ext = noisy.shape[1]
    used = ext - HALO
    body = slice(0, used) if odd else slice(HALO, ext)
    rim = slice(used, ext) if odd else slice(0, HALO)
    for z in range(planes):
        j, b = z // 2, z % 2
        rows, edge_rows = slice(used * b, used * (b + 1)), slice(HALO * b, HALO * (b + 1))
        value = raw_w[j][rows]
        if block_in is not None:
            value = jnp.where(block_in, value, 1.0)
            in_rim = jnp.logical_and(edge_in, block_in)
        else:
            in_rim = edge_in
        noisy[base + z, body] = raw_n[j][rows]
        noisy[base + z, rim] = edge[0, j, edge_rows]
        weight[base + z, body] = value
        weight[base + z, rim] = jnp.where(in_rim, edge[1, j, edge_rows], 1.0)


def geometry(planes, half, count_z, count_x):
    gz, gx = lax.axis_index("gz"), lax.axis_index("gx")
    odd = lax.rem(gz, 2)
    first_plane = (gz - odd - 1) * planes
    first_row = (2 * gx + odd) * half - HALO
    below, above = gz >= 2, gz < count_z - 2
    edge_in = (gx < count_x - 1, gx > 0)
    return odd == 1, first_plane, first_row, planes * count_z, 2 * half * count_x, edge_in, below, above


def split(ref):
    return [ref.at[j] for j in range(ref.shape[0])]


def early(counts, *refs):
    own_n, own_w, par_n, par_w0, par_w1, one_n, one_w, edge_own, edge_par, edge_far = refs[:10]
    send, stats = refs[10:12]
    state, (cx_ref, acc) = refs[12:19], refs[19:]
    planes, half = send.shape[0], send.shape[1]
    odd, first_plane, first_row, all_planes, all_rows, edge_in, below, above = geometry(
        planes, half, *counts
    )
    place_rows(cx_ref, first_row, all_rows)
    par_w = [par_w0.at[0], par_w1.at[0]]

    def when_odd():
        place(True, 0, split(one_n), split(one_w), edge_far, state, edge_in[0], below)
        place(True, planes, split(par_n), par_w, edge_par, state, edge_in[0], None)
        place(True, 2 * planes, split(own_n), split(own_w), edge_own, state, edge_in[0], None)

    def when_even():
        place(False, planes, split(own_n), split(own_w), edge_own, state, edge_in[1], None)
        place(False, 2 * planes, split(par_n), par_w, edge_par, state, edge_in[1], None)
        place(False, 3 * planes, split(one_n), split(one_w), edge_far, state, edge_in[1], above)

    by_parity(odd, when_odd, when_even)
    acc[...] = jnp.zeros_like(acc)
    sweep = Sweep(state, cx_ref, acc, first_plane, all_planes)

    def iteration(k, first):
        by_parity(
            odd,
            lambda: sweep.step(k, k, True, False, False, first),
            lambda: sweep.step(k, planes + k, True, False, True, first),
        )
        sweep.loop(k, k + 1, jnp.where(odd, planes, 0), False, first)
        sweep.loop(
            k,
            jnp.where(odd, planes, planes + 1 + k),
            jnp.where(odd, 3 * planes - 1 - k, 3 * planes),
            True,
            first,
        )
        sweep.loop(k, 3 * planes, jnp.where(odd, 0, 4 * planes - 1 - k), False, first)

    iterations(iteration)

    def finish(first_send):
        send[...] = state[2][first_send : first_send + planes, HALO : HALO + half]

    by_parity(odd, lambda: finish(planes), lambda: finish(2 * planes))
    write_stats(stats, acc)


def iterations(iteration):
    iteration(0, True)

    def body(k, _):
        iteration(k, False)
        return 0

    lax.fori_loop(1, ITERS, body, 0)


def write_stats(stats, acc, before=None):
    for k in range(ITERS):
        gap = acc[0, k] * (1.0 / dual_step) + acc[1, k]
        for row, value in ((k, gap), (ITERS + k, acc[2, k])):
            total = jnp.sum(value, axis=0, keepdims=True)
            if before is not None:
                total = total + before[row : row + 1]
            stats[row : row + 1] = total


def late(counts, *refs):
    two_n, two_w0, two_w1, edge_far, stats_in = refs[:5]
    keep, stats = refs[12:14]
    state, (cx_ref, acc) = refs[14:21], refs[21:]
    planes, half = keep.shape[0], keep.shape[1]
    odd, first_plane, first_row, all_planes, all_rows, edge_in, below, above = geometry(
        planes, half, *counts
    )
    place_rows(cx_ref, first_row, all_rows)
    two_w = [two_w0.at[0], two_w1.at[0]]
    by_parity(
        odd,
        lambda: place(True, 3 * planes, split(two_n), two_w, edge_far, state, edge_in[0], above),
        lambda: place(False, 0, split(two_n), two_w, edge_far, state, edge_in[1], below),
    )
    acc[...] = jnp.zeros_like(acc)
    sweep = Sweep(state, cx_ref, acc, first_plane, all_planes)
    even = jnp.logical_not(odd)

    def iteration(k, first):
        pl.when(even)(lambda: sweep.step(k, k, True, False, False, first))
        sweep.loop(k, k + 1, jnp.where(odd, 0, planes), False, first)
        sweep.loop(
            k,
            jnp.where(odd, 3 * planes - 1 - k, planes),
            jnp.where(odd, 3 * planes, planes + k),
            True,
            first,
        )
        sweep.loop(k, 3 * planes, jnp.where(odd, 4 * planes - 1 - k, 0), False, first)
        pl.when(even)(lambda: sweep.step(k, planes + k, False, True, True, first))

    iterations(iteration)

    def finish(first):
        keep[...] = state[2][first : first + planes, HALO : HALO + half]

    by_parity(odd, lambda: finish(2 * planes), lambda: finish(planes))
    write_stats(stats, acc, stats_in)


def pack_out(keep, got, out):
    half = keep.shape[1]

    def when_odd():
        out[:, 0:half] = got[...]
        out[:, half:] = keep[...]

    def when_even():
        out[:, 0:half] = keep[...]
        out[:, half:] = got[...]

    by_parity(is_odd(), when_odd, when_even)


def shards(noisy_volume, tv_weight):
    planes, rows, cols = noisy_volume.shape
    count_z, count_x = lax.axis_size("gz"), lax.axis_size("gx")
    if planes != ITERS or count_z % 2 or rows % (2 * SUB) or cols % LANE:
        raise ValueError("unsupported sizes")
    half = rows // 2
    ext = half + 2 * HALO
    cell_count = planes * rows * cols * count_z * count_x
    both = ("gz", "gx")

    def permute(value, step):
        pairs = []
        for z in range(count_z):
            for x in range(count_x):
                tz, tx = step(z, x)
                if 0 <= tz < count_z and 0 <= tx < count_x:
                    pairs.append((z * count_x + x, tz * count_x + tx))
        return lax.ppermute(value, both, pairs)

    swap = lambda z, x: (z ^ 1, x)
    edge_step_one = lambda z, x: (z, x - 1 if z % 2 else x + 1)
    edge_step_two = lambda z, x: (z ^ 1, x + 1 if z % 2 else x - 1)
    ghost_step_one = lambda z, x: (z + 2 if z % 2 else z - 2, x)
    ghost_step_two = lambda z, x: (z - 2 if z % 2 else z + 2, x)

    edge = (2, planes // 2, 2 * HALO, cols)
    raw = (planes // 2, 2 * (half + HALO), cols)
    chunk = (1,) + raw[1:]
    near = VMEM((planes, SUB, cols), jnp.float32)
    whole = VMEM((planes, rows, cols), jnp.float32)
    send_n, own_n, edge_one, edge_two = vmem_call(
        pack_first,
        [raw, raw, edge, edge],
        [pltpu.HBM] * 2,
        scratch=[whole, near, near, pltpu.SemaphoreType.DMA((3,))],
    )(*(pltpu.with_memory_space_constraint(v, pltpu.HBM) for v in (noisy_volume, tv_weight)))
    edge_par = permute(edge_two, edge_step_two)
    par_n = permute(send_n, swap)
    one_n = permute(own_n, ghost_step_one)
    *send_w, own_w = vmem_call(
        pack_second,
        [chunk] * (planes // 2) + [raw],
        [pltpu.HBM],
        scratch=[whole, pltpu.SemaphoreType.DMA],
    )(pltpu.with_memory_space_constraint(tv_weight, pltpu.HBM))
    par_w = [permute(value, swap) for value in send_w]
    edge_own = permute(edge_one, edge_step_one)
    one_w = permute(own_w, ghost_step_one)
    edge_one_far = permute(edge_own, ghost_step_one)
    edge_two_far = permute(edge_par, ghost_step_two)
    two_n = permute(par_n, ghost_step_two)
    two_w = [permute(value, ghost_step_two) for value in par_w]

    out_half = (planes, half, cols)
    stats_shape = (2 * ITERS, LANE)
    counts = (count_z, count_x)
    small = [VMEM((ext, LANE), jnp.float32), VMEM((3, ITERS, SUB, LANE), jnp.float32)]
    states = [(4 * planes, ext, cols)] * 7
    send, stats, *state = vmem_call(
        functools.partial(early, counts),
        [out_half, stats_shape] + states,
        [VMEM] * 10,
        scratch=small,
        flops=100 << 20,
        limit=24,
    )(own_n, own_w, par_n, *par_w, one_n, one_w, edge_own, edge_par, edge_one_far)
    got = permute(send, swap)
    keep, stats, *_ = vmem_call(
        functools.partial(late, counts),
        [out_half, stats_shape] + states,
        [VMEM] * 12,
        scratch=small,
        flops=50 << 20,
        limit=24,
        aliases={5 + a: 2 + a for a in range(7)},
    )(two_n, *two_w, edge_two_far, stats, *state)

    if count_z & (count_z - 1) or count_x & (count_x - 1):
        stats = lax.psum(stats, both)
    else:
        step = 1
        while step < count_x:
            stats = stats + permute(stats, lambda z, x, d=step: (z, x ^ d))
            step *= 2
        step = 1
        while step < count_z:
            stats = stats + permute(stats, lambda z, x, d=step: (z ^ d, x))
            step *= 2
    totals = jnp.sum(stats, axis=1) / cell_count
    (out,) = vmem_call(pack_out, [(planes, rows, cols)], [VMEM] * 2)(keep, got)
    return (out, totals[:ITERS], jnp.sqrt(totals[ITERS:]))


def solution(mesh):
    placed = (P("gz", "gx", None), P("gz", "gx", None))

    return jax.shard_map(
        shards,
        mesh=mesh,
        in_specs=placed,
        out_specs=(P("gz", "gx", None), P(), P()),
        check_vma=False,
    )
```

time: 85 us -> 92 us (1.082)
  starting transfers between devices: 34.2 us -> 41.2 us
  local copies, waits for them, and re-layouts: 5.26 us -> 0.6 us
  waiting for transfers between devices: 25.2 us -> 29.6 us
    ppermute x14 -> x18, starting transfers between devices: 34.2 us -> 41.2 us  [permute(): return lax.ppermute(value, both, pairs)]
    ppermute x14 -> x18, waiting for transfers between devices: 25.2 us -> 29.6 us  [permute(): return lax.ppermute(value, both, pairs)]
    unnamed x4 -> x0, local copies, waits for them, and re-layouts: 2.45 us -> none
    dynamic_slice x2 -> x0, local copies, waits for them, and re-layouts: 2.21 us -> none  [the longest x1 1.11 us: shards(): send_n = lax.dynamic_slice(noisy_volume, (zero, start, zero), sent)]
    pallas_call x7 -> x5, Pallas kernels: 19 us -> 19.4 us  [the longest x1 10.6 us: shards(): vmem_call(functools.partial(early, counts), [out_half, stats_shape] + sta...]
  transfers between devices with their start and end apart: 14 -> 18, of which waited for: 9 -> 9; matrix products, arithmetic and copies ran while one was open for 1% -> 0% of each run, Pallas kernels for 22% -> 20%
where the time goes in v3:
time: 92 us; the launch traced here: 91.6 us
  starting transfers between devices  41.2 us (45%)
  waiting for transfers between devices  29.6 us (32%)
  Pallas kernels  19.4 us (21%)
    ppermute x18, starting transfers between devices, permute(): return lax.ppermute(value, both, pairs)  41.2 us
    ppermute x18, waiting for transfers between devices, permute(): return lax.ppermute(value, both, pairs)  29.6 us
    pallas_call x1, Pallas kernels, shards(): vmem_call(functools.partial(early, counts), [out_half, stats_shape] + sta...  10.6 us
    pallas_call x1, Pallas kernels, shards(): vmem_call(functools.partial(late, counts), [out_half, stats_shape] + stat...  5.1 us
  transfers between devices with their start and end apart: 18, of which 9 were waited for; matrix products, arithmetic and copies ran while one was open for 0% of the time, Pallas kernels for 20%

profile of v3, /device:TPU:0, one launch (start us, length us, event | category | flops | bytes accessed | tf_op | source)
XLA Modules:
  0.0 91.6 jit_solution(8937976462502011012)
XLA Ops:
  0.6 1.4 %shard_map.49 = (f32[2,136,512]{2,1,0:T(8,128)S(1)}, f32[2,136,512]{2,1,0:T(8,128)S(1)}, f32[2,2,8,512]{3,2,1,0:T(8,128)S(1)}, f32[2,2,8,512]{3,2,1,0:T(8,128)S(1)}) custom-call(f32[4,128,512]{2,1,0:T(8,128)} %noisy.1, f32[4,128,512]{2,1,0:T(8,128)} %weight.3), custom_call_target="tpu_custom_call" | custom-call | flops 1048576 | bytes 1048576 | tf_op jit(solution)/shard_map/pallas_call | solution.py:430
  2.0 3.0 %collective-permute-start = (f32[2,136,512]{2,1,0:T(8,128)S(1)}, f32[2,136,512]{2,1,0:T(8,128)S(1)}, u32[]{:S(2)}, u32[]{:S(2)}) collective-permute-start(f32[2,136,512]{2,1,0:T(8,128)S(1)} %get-tuple-element.21), channel_id=1, source_target_pairs={{0,4},{1,5},{2,6},{3,7},{4,0},{5,1},{6,2},{7,3},{8,12},{9,13},{10,... | collective-permute-start | bytes 1671176 | tf_op jit(solution)/shard_map/ppermute | solution.py:417
  5.0 1.3 %shard_map.50 = (f32[1,136,512]{2,1,0:T(8,128)S(1)}, f32[1,136,512]{2,1,0:T(8,128)S(1)}, f32[2,136,512]{2,1,0:T(8,128)S(1)}) custom-call(f32[4,128,512]{2,1,0:T(8,128)} %weight.3), custom_call_target="tpu_custom_call" | custom-call | flops 1048576 | bytes 1048576 | tf_op jit(solution)/shard_map/pallas_call | solution.py:439
  6.4 1.3 %collective-permute-start.9 = (f32[2,136,512]{2,1,0:T(8,128)S(1)}, f32[2,136,512]{2,1,0:T(8,128)S(1)}, u32[]{:S(2)}, u32[]{:S(2)}) collective-permute-start(f32[2,136,512]{2,1,0:T(8,128)S(1)} %get-tuple-element.26.refs_1_), channel_id=1, source_target_pairs={{4,12},{5,13},{6,14},{7,15},{8,0},{9,1},{10,2},{11,3},{12,20},{13,... | collective-permute-start | bytes 1671176 | tf_op jit(solution)/shard_map/ppermute | solution.py:417
  7.7 1.3 %collective-permute-start.8 = (f32[2,136,512]{2,1,0:T(8,128)S(1)}, f32[2,136,512]{2,1,0:T(8,128)S(1)}, u32[]{:S(2)}, u32[]{:S(2)}) collective-permute-start(f32[2,136,512]{2,1,0:T(8,128)S(1)} %get-tuple-element.25.refs_0_), channel_id=1, source_target_pairs={{4,12},{5,13},{6,14},{7,15},{8,0},{9,1},{10,2},{11,3},{12,20},{13,... | collective-permute-start | bytes 1671176 | tf_op jit(solution)/shard_map/ppermute | solution.py:417
  9.0 1.5 %collective-permute-start.10 = (f32[2,2,8,512]{3,2,1,0:T(8,128)S(1)}, f32[2,2,8,512]{3,2,1,0:T(8,128)S(1)}, u32[]{:S(2)}, u32[]{:S(2)}) collective-permute-start(f32[2,2,8,512]{3,2,1,0:T(8,128)S(1)} %get-tuple-element.27), channel_id=1, source_target_pairs={{0,1},{1,2},{2,3},{5,4},{6,5},{7,6},{8,9},{9,10},{10,11},{13,12},{... | collective-permute-start | bytes 196616 | tf_op jit(solution)/shard_map/ppermute | solution.py:417
  10.4 0.7 collective-permute-start.6
  11.1 0.2 collective-permute-done.10.refs_7_
  11.3 1.3 %collective-permute-start.11 = (f32[2,2,8,512]{3,2,1,0:T(8,128)S(1)}, f32[2,2,8,512]{3,2,1,0:T(8,128)S(1)}, u32[]{:S(2)}, u32[]{:S(2)}) collective-permute-start(f32[2,2,8,512]{3,2,1,0:T(8,128)S(1)} %collective-permute-done.10.refs_7_), channel_id=1, source_target_pairs={{4,12},{5,13},{6,14},{7,15},{8,0},{9,1},{10,2},{11,3},{12,20},{13,... | collective-permute-start | bytes 196616 | tf_op jit(solution)/shard_map/ppermute | solution.py:417
  12.6 8.7 %collective-permute-start.2 = (f32[1,136,512]{2,1,0:T(8,128)S(1)}, f32[1,136,512]{2,1,0:T(8,128)S(1)}, u32[]{:S(2)}, u32[]{:S(2)}) collective-permute-start(f32[1,136,512]{2,1,0:T(8,128)S(1)} %get-tuple-element.22), channel_id=1, source_target_pairs={{0,4},{1,5},{2,6},{3,7},{4,0},{5,1},{6,2},{7,3},{8,12},{9,13},{10,... | collective-permute-start | bytes 835592 | tf_op jit(solution)/shard_map/ppermute | solution.py:417
  21.3 14.4 %collective-permute-done.11.refs_9_ = f32[2,2,8,512]{3,2,1,0:T(8,128)S(1)} collective-permute-done((f32[2,2,8,512]{3,2,1,0:T(8,128)S(1)}, f32[2,2,8,512]{3,2,1,0:T(8,128)S(1)}, u32[]{:S(2)}, u32[]{:S(2)}) %collective-permute-start.11) | collective-permute-done | bytes 65568 | tf_op jit(solution)/shard_map/ppermute | solution.py:417
  35.7 4.0 %collective-permute-start.1 = (f32[2,136,512]{2,1,0:T(8,128)S(1)}, f32[2,136,512]{2,1,0:T(8,128)S(1)}, u32[]{:S(2)}, u32[]{:S(2)}) collective-permute-start(f32[2,136,512]{2,1,0:T(8,128)S(1)} %collective-permute-done.refs_2_), channel_id=1, source_target_pairs={{0,8},{1,9},{2,10},{3,11},{8,16},{9,17},{10,18},{11,19},{12,4},{13... | collective-permute-start | bytes 1671176 | tf_op jit(solution)/shard_map/ppermute | solution.py:417
  39.7 3.2 %collective-permute-done.4.refs_4_ = f32[1,136,512]{2,1,0:T(8,128)S(1)} collective-permute-done((f32[1,136,512]{2,1,0:T(8,128)S(1)}, f32[1,136,512]{2,1,0:T(8,128)S(1)}, u32[]{:S(2)}, u32[]{:S(2)}) %collective-permute-start.4) | collective-permute-done | bytes 278560 | tf_op jit(solution)/shard_map/ppermute | solution.py:417
  42.9 10.6 %shard_map.51 = (f32[4,64,512]{2,1,0:T(8,128)S(1)}, f32[8,128]{1,0:T(8,128)S(1)}, f32[16,72,512]{2,1,0:T(8,128)S(1)}, f32[16,72,512]{2,1,0:T(8,128)S(1)}, f32[16...) custom-call(f32[2,136,512]{2,1,0:T(8,128)S(1)} %get-tuple-element.25, ...), custom_call_target="tpu_custom_call" | custom-call | flops 104857600 | bytes 1048576 | tf_op jit(solution)/shard_map/pallas_call | solution.py:458
  53.5 0.1 collective-permute-start.12
  53.6 3.6 %collective-permute-start.3 = (f32[1,136,512]{2,1,0:T(8,128)S(1)}, f32[1,136,512]{2,1,0:T(8,128)S(1)}, u32[]{:S(2)}, u32[]{:S(2)}) collective-permute-start(f32[1,136,512]{2,1,0:T(8,128)S(1)} %collective-permute-done.2.refs_3_), channel_id=1, source_target_pairs={{0,8},{1,9},{2,10},{3,11},{8,16},{9,17},{10,18},{11,19},{12,4},{13... | collective-permute-start | bytes 835592 | tf_op jit(solution)/shard_map/ppermute | solution.py:417
  57.2 3.5 %collective-permute-start.5 = (f32[1,136,512]{2,1,0:T(8,128)S(1)}, f32[1,136,512]{2,1,0:T(8,128)S(1)}, u32[]{:S(2)}, u32[]{:S(2)}) collective-permute-start(f32[1,136,512]{2,1,0:T(8,128)S(1)} %collective-permute-done.4.refs_4_), channel_id=1, source_target_pairs={{0,8},{1,9},{2,10},{3,11},{8,16},{9,17},{10,18},{11,19},{12,4},{13... | collective-permute-start | bytes 835592 | tf_op jit(solution)/shard_map/ppermute | solution.py:417
  60.7 3.5 %collective-permute-start.7 = (f32[2,2,8,512]{3,2,1,0:T(8,128)S(1)}, f32[2,2,8,512]{3,2,1,0:T(8,128)S(1)}, u32[]{:S(2)}, u32[]{:S(2)}) collective-permute-start(f32[2,2,8,512]{3,2,1,0:T(8,128)S(1)} %collective-permute-done.6.refs_8_), channel_id=1, source_target_pairs={{0,8},{1,9},{2,10},{3,11},{8,16},{9,17},{10,18},{11,19},{12,4},{13... | collective-permute-start | bytes 196616 | tf_op jit(solution)/shard_map/ppermute | solution.py:417
  64.2 4.4 %collective-permute-done.7.refs_3_ = f32[2,2,8,512]{3,2,1,0:T(8,128)S(1)} collective-permute-done((f32[2,2,8,512]{3,2,1,0:T(8,128)S(1)}, f32[2,2,8,512]{3,2,1,0:T(8,128)S(1)}, u32[]{:S(2)}, u32[]{:S(2)}) %collective-permute-start.7) | collective-permute-done | bytes 65568 | tf_op jit(solution)/shard_map/ppermute | solution.py:417
  68.6 5.1 %shard_map.52 = (f32[4,64,512]{2,1,0:T(8,128)S(1)}, f32[8,128]{1,0:T(8,128)S(1)}, f32[16,72,512]{2,1,0:T(8,128)S(1)}, f32[16,72,512]{2,1,0:T(8,128)S(1)}, f32[16...) custom-call(f32[2,136,512]{2,1,0:T(8,128)S(1)} %collective-permute-d, ...), custom_call_target="tpu_custom_call", output_to_operand_aliasing={{2}: (5, {}), {3}: (6, {}), {4}: (7, {}), {5}: (8, {}), {6}... | custom-call | flops 52428800 | bytes 1048576 | tf_op jit(solution)/shard_map/pallas_call | solution.py:467
  73.8 1.2 %collective-permute-done.13 = f32[8,128]{1,0:T(8,128)S(1)} collective-permute-done((f32[8,128]{1,0:T(8,128)S(1)}, f32[8,128]{1,0:T(8,128)S(1)}, u32[]{:S(2)}, u32[]{:S(2)}) %collective-permute-start.13) | collective-permute-done | bytes 4128 | tf_op jit(solution)/shard_map/ppermute | solution.py:417
  74.9 1.5 %collective-permute-start.14 = (f32[8,128]{1,0:T(8,128)S(1)}, f32[8,128]{1,0:T(8,128)S(1)}, u32[]{:S(2)}, u32[]{:S(2)}) collective-permute-start(f32[8,128]{1,0:T(8,128)S(1)} %add.15), channel_id=1, source_target_pairs={{0,2},{1,3},{2,0},{3,1},{4,6},{5,7},{6,4},{7,5},{8,10},{9,11},{10,... | collective-permute-start | bytes 12296 | tf_op jit(solution)/shard_map/ppermute | solution.py:417
  76.5 2.1 %collective-permute-done.14 = f32[8,128]{1,0:T(8,128)S(1)} collective-permute-done((f32[8,128]{1,0:T(8,128)S(1)}, f32[8,128]{1,0:T(8,128)S(1)}, u32[]{:S(2)}, u32[]{:S(2)}) %collective-permute-start.14) | collective-permute-done | bytes 4128 | tf_op jit(solution)/shard_map/ppermute | solution.py:417
  78.6 2.7 %collective-permute-start.15 = (f32[8,128]{1,0:T(8,128)S(1)}, f32[8,128]{1,0:T(8,128)S(1)}, u32[]{:S(2)}, u32[]{:S(2)}) collective-permute-start(f32[8,128]{1,0:T(8,128)S(1)} %add.16), channel_id=1, source_target_pairs={{0,4},{1,5},{2,6},{3,7},{4,0},{5,1},{6,2},{7,3},{8,12},{9,13},{10,... | collective-permute-start | bytes 12296 | tf_op jit(solution)/shard_map/ppermute | solution.py:417
  81.2 1.6 %collective-permute-done.15 = f32[8,128]{1,0:T(8,128)S(1)} collective-permute-done((f32[8,128]{1,0:T(8,128)S(1)}, f32[8,128]{1,0:T(8,128)S(1)}, u32[]{:S(2)}, u32[]{:S(2)}) %collective-permute-start.15) | collective-permute-done | bytes 4128 | tf_op jit(solution)/shard_map/ppermute | solution.py:417
  82.8 1.8 %collective-permute-start.16 = (f32[8,128]{1,0:T(8,128)S(1)}, f32[8,128]{1,0:T(8,128)S(1)}, u32[]{:S(2)}, u32[]{:S(2)}) collective-permute-start(f32[8,128]{1,0:T(8,128)S(1)} %add.17), channel_id=1, source_target_pairs={{0,8},{1,9},{2,10},{3,11},{4,12},{5,13},{6,14},{7,15},{8,0},{9,1},... | collective-permute-start | bytes 12296 | tf_op jit(solution)/shard_map/ppermute | solution.py:417
  84.6 1.8 %collective-permute-done.16 = f32[8,128]{1,0:T(8,128)S(1)} collective-permute-done((f32[8,128]{1,0:T(8,128)S(1)}, f32[8,128]{1,0:T(8,128)S(1)}, u32[]{:S(2)}, u32[]{:S(2)}) %collective-permute-start.16) | collective-permute-done | bytes 4128 | tf_op jit(solution)/shard_map/ppermute | solution.py:417
  86.4 2.7 %collective-permute-start.17 = (f32[8,128]{1,0:T(8,128)S(1)}, f32[8,128]{1,0:T(8,128)S(1)}, u32[]{:S(2)}, u32[]{:S(2)}) collective-permute-start(f32[8,128]{1,0:T(8,128)S(1)} %add.18), channel_id=1, source_target_pairs={{0,16},{1,17},{2,18},{3,19},{4,20},{5,21},{6,22},{7,23},{8,24},{9,... | collective-permute-start | bytes 12296 | tf_op jit(solution)/shard_map/ppermute | solution.py:417
  89.1 1.0 %shard_map.53 = f32[4,128,512]{2,1,0:T(8,128)} custom-call(f32[4,64,512]{2,1,0:T(8,128)S(1)} %get-tuple-element.36.keep, f32[4,64,512]{2,1,0:T(8,128)S(1)} %collective-permute-done.12.got), custom_call_target="tpu_custom_call" | custom-call | flops 1048576 | bytes 1048576 | tf_op jit(solution)/shard_map/pallas_call | solution.py:489
  90.1 0.8 collective-permute-done.17
  90.9 0.1 add_reduce_fusion
  91.0 0.6 slice_sqrt_fusion
  (16 shorter events, 0.1 us)
Async XLA Ops:
  2.0 33.7 %collective-permute-start = (f32[2,136,512]{2,1,0:T(8,128)S(1)}, f32[2,136,512]{2,1,0:T(8,128)S(1)}, u32[]{:S(2)}, u32[]{:S(2)}) collective-permute-start(f32[2,136,512]{2,1,0:T(8,128)S(1)} %get-tuple-element.21), channel_id=1, source_target_pairs={{0,4},{1,5},{2,6},{3,7},{4,0},{5,1},{6,2},{7,3},{8,12},{9,13},{10,... | collective-permute-start | bytes 1671176 | tf_op jit(solution)/shard_map/ppermute | solution.py:417
  6.4 36.6 %collective-permute-start.9 = (f32[2,136,512]{2,1,0:T(8,128)S(1)}, f32[2,136,512]{2,1,0:T(8,128)S(1)}, u32[]{:S(2)}, u32[]{:S(2)}) collective-permute-start(f32[2,136,512]{2,1,0:T(8,128)S(1)} %get-tuple-element.26.refs_1_), channel_id=1, source_target_pairs={{4,12},{5,13},{6,14},{7,15},{8,0},{9,1},{10,2},{11,3},{12,20},{13,... | collective-permute-start | bytes 1671176 | tf_op jit(solution)/shard_map/ppermute | solution.py:417
  7.7 35.3 %collective-permute-start.8 = (f32[2,136,512]{2,1,0:T(8,128)S(1)}, f32[2,136,512]{2,1,0:T(8,128)S(1)}, u32[]{:S(2)}, u32[]{:S(2)}) collective-permute-start(f32[2,136,512]{2,1,0:T(8,128)S(1)} %get-tuple-element.25.refs_0_), channel_id=1, source_target_pairs={{4,12},{5,13},{6,14},{7,15},{8,0},{9,1},{10,2},{11,3},{12,20},{13,... | collective-permute-start | bytes 1671176 | tf_op jit(solution)/shard_map/ppermute | solution.py:417
  9.0 2.4 %collective-permute-start.10 = (f32[2,2,8,512]{3,2,1,0:T(8,128)S(1)}, f32[2,2,8,512]{3,2,1,0:T(8,128)S(1)}, u32[]{:S(2)}, u32[]{:S(2)}) collective-permute-start(f32[2,2,8,512]{3,2,1,0:T(8,128)S(1)} %get-tuple-element.27), channel_id=1, source_target_pairs={{0,1},{1,2},{2,3},{5,4},{6,5},{7,6},{8,9},{9,10},{10,11},{13,12},{... | collective-permute-start | bytes 196616 | tf_op jit(solution)/shard_map/ppermute | solution.py:417
  10.4 2.2 %collective-permute-start.6 = (f32[2,2,8,512]{3,2,1,0:T(8,128)S(1)}, f32[2,2,8,512]{3,2,1,0:T(8,128)S(1)}, u32[]{:S(2)}, u32[]{:S(2)}) collective-permute-start(f32[2,2,8,512]{3,2,1,0:T(8,128)S(1)} %get-tuple-element.24), channel_id=1, source_target_pairs={{1,4},{2,5},{3,6},{4,1},{5,2},{6,3},{9,12},{10,13},{11,14},{12,9},... | collective-permute-start | bytes 196616 | tf_op jit(solution)/shard_map/ppermute | solution.py:417
  11.3 24.4 %collective-permute-start.11 = (f32[2,2,8,512]{3,2,1,0:T(8,128)S(1)}, f32[2,2,8,512]{3,2,1,0:T(8,128)S(1)}, u32[]{:S(2)}, u32[]{:S(2)}) collective-permute-start(f32[2,2,8,512]{3,2,1,0:T(8,128)S(1)} %collective-permute-done.10.refs_7_), channel_id=1, source_target_pairs={{4,12},{5,13},{6,14},{7,15},{8,0},{9,1},{10,2},{11,3},{12,20},{13,... | collective-permute-start | bytes 196616 | tf_op jit(solution)/shard_map/ppermute | solution.py:417
  12.6 27.1 %collective-permute-start.2 = (f32[1,136,512]{2,1,0:T(8,128)S(1)}, f32[1,136,512]{2,1,0:T(8,128)S(1)}, u32[]{:S(2)}, u32[]{:S(2)}) collective-permute-start(f32[1,136,512]{2,1,0:T(8,128)S(1)} %get-tuple-element.22), channel_id=1, source_target_pairs={{0,4},{1,5},{2,6},{3,7},{4,0},{5,1},{6,2},{7,3},{8,12},{9,13},{10,... | collective-permute-start | bytes 835592 | tf_op jit(solution)/shard_map/ppermute | solution.py:417
  35.7 7.3 %collective-permute-start.4 = (f32[1,136,512]{2,1,0:T(8,128)S(1)}, f32[1,136,512]{2,1,0:T(8,128)S(1)}, u32[]{:S(2)}, u32[]{:S(2)}) collective-permute-start(f32[1,136,512]{2,1,0:T(8,128)S(1)} %get-tuple-element.23), channel_id=1, source_target_pairs={{0,4},{1,5},{2,6},{3,7},{4,0},{5,1},{6,2},{7,3},{8,12},{9,13},{10,... | collective-permute-start | bytes 835592 | tf_op jit(solution)/shard_map/ppermute | solution.py:417
  35.7 32.9 %collective-permute-start.1 = (f32[2,136,512]{2,1,0:T(8,128)S(1)}, f32[2,136,512]{2,1,0:T(8,128)S(1)}, u32[]{:S(2)}, u32[]{:S(2)}) collective-permute-start(f32[2,136,512]{2,1,0:T(8,128)S(1)} %collective-permute-done.refs_2_), channel_id=1, source_target_pairs={{0,8},{1,9},{2,10},{3,11},{8,16},{9,17},{10,18},{11,19},{12,4},{13... | collective-permute-start | bytes 1671176 | tf_op jit(solution)/shard_map/ppermute | solution.py:417
  53.5 35.6 %collective-permute-start.12 = (f32[4,64,512]{2,1,0:T(8,128)S(1)}, f32[4,64,512]{2,1,0:T(8,128)S(1)}, u32[]{:S(2)}, u32[]{:S(2)}) collective-permute-start(f32[4,64,512]{2,1,0:T(8,128)S(1)} %get-tuple-element.37), channel_id=1, source_target_pairs={{0,4},{1,5},{2,6},{3,7},{4,0},{5,1},{6,2},{7,3},{8,12},{9,13},{10,... | collective-permute-start | bytes 1572872 | tf_op jit(solution)/shard_map/ppermute | solution.py:417
  53.6 15.0 %collective-permute-start.3 = (f32[1,136,512]{2,1,0:T(8,128)S(1)}, f32[1,136,512]{2,1,0:T(8,128)S(1)}, u32[]{:S(2)}, u32[]{:S(2)}) collective-permute-start(f32[1,136,512]{2,1,0:T(8,128)S(1)} %collective-permute-done.2.refs_3_), channel_id=1, source_target_pairs={{0,8},{1,9},{2,10},{3,11},{8,16},{9,17},{10,18},{11,19},{12,4},{13... | collective-permute-start | bytes 835592 | tf_op jit(solution)/shard_map/ppermute | solution.py:417
  57.2 11.4 %collective-permute-start.5 = (f32[1,136,512]{2,1,0:T(8,128)S(1)}, f32[1,136,512]{2,1,0:T(8,128)S(1)}, u32[]{:S(2)}, u32[]{:S(2)}) collective-permute-start(f32[1,136,512]{2,1,0:T(8,128)S(1)} %collective-permute-done.4.refs_4_), channel_id=1, source_target_pairs={{0,8},{1,9},{2,10},{3,11},{8,16},{9,17},{10,18},{11,19},{12,4},{13... | collective-permute-start | bytes 835592 | tf_op jit(solution)/shard_map/ppermute | solution.py:417
  60.7 7.9 %collective-permute-start.7 = (f32[2,2,8,512]{3,2,1,0:T(8,128)S(1)}, f32[2,2,8,512]{3,2,1,0:T(8,128)S(1)}, u32[]{:S(2)}, u32[]{:S(2)}) collective-permute-start(f32[2,2,8,512]{3,2,1,0:T(8,128)S(1)} %collective-permute-done.6.refs_8_), channel_id=1, source_target_pairs={{0,8},{1,9},{2,10},{3,11},{8,16},{9,17},{10,18},{11,19},{12,4},{13... | collective-permute-start | bytes 196616 | tf_op jit(solution)/shard_map/ppermute | solution.py:417
  73.7 1.2 %collective-permute-start.13 = (f32[8,128]{1,0:T(8,128)S(1)}, f32[8,128]{1,0:T(8,128)S(1)}, u32[]{:S(2)}, u32[]{:S(2)}) collective-permute-start(f32[8,128]{1,0:T(8,128)S(1)} %get-tuple-element.38), channel_id=1, source_target_pairs={{0,1},{1,0},{2,3},{3,2},{4,5},{5,4},{6,7},{7,6},{8,9},{9,8},{10,11... | collective-permute-start | bytes 12296 | tf_op jit(solution)/shard_map/ppermute | solution.py:417
  74.9 3.6 %collective-permute-start.14 = (f32[8,128]{1,0:T(8,128)S(1)}, f32[8,128]{1,0:T(8,128)S(1)}, u32[]{:S(2)}, u32[]{:S(2)}) collective-permute-start(f32[8,128]{1,0:T(8,128)S(1)} %add.15), channel_id=1, source_target_pairs={{0,2},{1,3},{2,0},{3,1},{4,6},{5,7},{6,4},{7,5},{8,10},{9,11},{10,... | collective-permute-start | bytes 12296 | tf_op jit(solution)/shard_map/ppermute | solution.py:417
  78.6 4.2 %collective-permute-start.15 = (f32[8,128]{1,0:T(8,128)S(1)}, f32[8,128]{1,0:T(8,128)S(1)}, u32[]{:S(2)}, u32[]{:S(2)}) collective-permute-start(f32[8,128]{1,0:T(8,128)S(1)} %add.16), channel_id=1, source_target_pairs={{0,4},{1,5},{2,6},{3,7},{4,0},{5,1},{6,2},{7,3},{8,12},{9,13},{10,... | collective-permute-start | bytes 12296 | tf_op jit(solution)/shard_map/ppermute | solution.py:417
  82.8 3.6 %collective-permute-start.16 = (f32[8,128]{1,0:T(8,128)S(1)}, f32[8,128]{1,0:T(8,128)S(1)}, u32[]{:S(2)}, u32[]{:S(2)}) collective-permute-start(f32[8,128]{1,0:T(8,128)S(1)} %add.17), channel_id=1, source_target_pairs={{0,8},{1,9},{2,10},{3,11},{4,12},{5,13},{6,14},{7,15},{8,0},{9,1},... | collective-permute-start | bytes 12296 | tf_op jit(solution)/shard_map/ppermute | solution.py:417
  86.4 4.5 %collective-permute-start.17 = (f32[8,128]{1,0:T(8,128)S(1)}, f32[8,128]{1,0:T(8,128)S(1)}, u32[]{:S(2)}, u32[]{:S(2)}) collective-permute-start(f32[8,128]{1,0:T(8,128)S(1)} %add.18), channel_id=1, source_target_pairs={{0,16},{1,17},{2,18},{3,19},{4,20},{5,21},{6,22},{7,23},{8,24},{9,... | collective-permute-start | bytes 12296 | tf_op jit(solution)/shard_map/ppermute | solution.py:417

commit v4 on v3

--- a/solution.py
+++ b/solution.py
@@ -13,8 +13,12 @@
 dual_step = 0.28
 
 SUB = 8
+PIECES = 3
 LANE = 128
 HALO = ITERS
+KEEP_SHARE = 1.0 / (1.0 + primal_step)
+NEW_SHARE = primal_step / (1.0 + primal_step)
+TINY = 2.0**-126
 VMEM = pltpu.VMEM
 
 
@@ -40,53 +44,36 @@
     pl.when(jnp.logical_not(odd))(when_even)
 
 
-def move_rows(planes, rows, half, odd, whole, send, own):
-    used = half + HALO
-    for z in range(planes):
-        base = used * (z % 2)
-        low, high = whole[z, 0:used], whole[z, rows - used : rows]
-        send[z // 2][z // 2 if len(set(map(id, send))) == 1 else 0, base : base + used] = (
-            low if odd else high
-        )
-        own[z // 2, base : base + used] = high if odd else low
-
-
-def pack_first(noisy, weight, send_n, own_n, edge_one, edge_two, whole, low, high, sems):
+def unit_rows(sizes, used):
+    return [(piece, used * j) for piece, size in enumerate(sizes) for j in range(size)]
+
+
+def pack(noisy, weight, *refs):
+    *send, own, edge_one, edge_two, whole, sems = refs
     planes, rows, _ = noisy.shape
-    half = rows // 2
+    used = rows // 2 + HALO
     copies = [
-        pltpu.make_async_copy(noisy, whole, sems.at[0]),
-        pltpu.make_async_copy(weight.at[:, 0:SUB], low, sems.at[1]),
-        pltpu.make_async_copy(weight.at[:, rows - SUB : rows], high, sems.at[2]),
+        pltpu.make_async_copy(ref, whole.at[a], sems.at[a]) for a, ref in enumerate((noisy, weight))
     ]
     for copy in copies:
         copy.start()
     for copy in copies:
         copy.wait()
-
-    def fill(to, at_low):
-        for j in range(planes // 2):
-            for b in range(2):
-                rows_to = slice(HALO * b, HALO * (b + 1))
-                z = 2 * j + b
-                to[0, j, rows_to] = whole[z, 0:HALO] if at_low else whole[z, rows - HALO : rows]
-                to[1, j, rows_to] = low[z, 0:HALO] if at_low else high[z, SUB - HALO : SUB]
+    places = unit_rows([ref.shape[0] // used for ref in send], used)
 
     def run(odd):
-        fill(edge_one, odd)
-        fill(edge_two, not odd)
-        move_rows(planes, rows, half, odd, whole, [send_n] * (planes // 2), own_n)
-
-    by_parity(is_odd(), lambda: run(True), lambda: run(False))
-
-
-def pack_second(weight, *refs):
-    send, own_w, whole, sem = refs[:-3], refs[-3], refs[-2], refs[-1]
-    planes, rows, _ = weight.shape
-    copy = pltpu.make_async_copy(weight, whole, sem)
-    copy.start()
-    copy.wait()
-    run = lambda odd: move_rows(planes, rows, rows // 2, odd, whole, send, own_w)
+        for to, at_low in ((edge_one, odd), (edge_two, not odd)):
+            for unit in range(2 * planes):
+                a, z = unit // planes, unit % planes
+                rows_to = slice(HALO * (z % 2), HALO * (z % 2 + 1))
+                first = 0 if at_low else rows - HALO
+                to[a, z // 2, rows_to] = whole[a, z, first : first + HALO]
+        for unit, (piece, base) in enumerate(places):
+            a, z = unit // planes, unit % planes
+            low, high = slice(0, used), slice(rows - used, rows)
+            send[piece][base : base + used] = whole[a, z, low if odd else high]
+            own[used * unit : used * (unit + 1)] = whole[a, z, high if odd else low]
+
     by_parity(is_odd(), lambda: run(True), lambda: run(False))
 
 
@@ -111,16 +98,17 @@
         for c in range(self.chunks):
             ref[m, s * SUB : (s + 1) * SUB, c * LANE : (c + 1) * LANE] = values[c]
 
-    def gradient(self, x, above, rolled, rolled_next, cz, cx):
+    def gradient(self, x, above, rolled, rolled_next, mask):
         side = [pltpu.roll(v, LANE - 1, 1) for v in x]
         out = []
         for c in range(self.chunks):
             last = c + 1 == self.chunks
             y_next = side[c] if last else jnp.where(self.last_lane, side[c + 1], side[c])
-            d_z = (above[c] - x[c]) * cz
-            down = jnp.where(self.last_sub, rolled_next[c], rolled[c])
-            d_x = (down - x[c]) * cx
-            d_y = (y_next - x[c]) * dual_step
+            d_z = above[c] - x[c]
+            d_x = jnp.where(self.last_sub, rolled_next[c], rolled[c]) - x[c]
+            if mask is not None:
+                d_x = d_x * mask
+            d_y = y_next - x[c]
             if last:
                 d_y = jnp.where(self.last_lane, 0.0, d_y)
             out.append((d_z, d_x, d_y))
@@ -130,7 +118,7 @@
         u_ref, bar_ref = (self.noisy, self.noisy) if first else (self.u, self.bar)
         plane = self.first_plane + m
         z_in = jnp.logical_and(plane >= 0, plane < self.all_planes - 1)
-        cz = jnp.where(z_in, dual_step, 0.0).astype(jnp.float32)
+        up = jnp.where(z_in, m + 1, m)
         zero = jnp.zeros((SUB, LANE), jnp.float32)
         tv_sum, quad_sum, step_sum = zero, zero, zero
         load, save, strips, chunks = self.load, self.save, self.strips, self.chunks
@@ -146,22 +134,24 @@
             more = s + 1 < strips
             part, quad, step = zero, zero, zero
             if do_p:
-                cx = self.cx_ref[s * SUB : (s + 1) * SUB]
+                edge = s == 0 or not more
+                mask = self.cx_ref[0 if s == 0 else 1] if edge else None
                 bar_next = load(bar_ref, m, s + 1) if more else bar_now
                 bar_roll_next = row_up(bar_next) if more else bar_roll
-                above = load(bar_ref, m + 1, s)
-                g_bar = self.gradient(bar_now, above, bar_roll, bar_roll_next, cz, cx)
+                above = load(bar_ref, up, s)
+                g_bar = self.gradient(bar_now, above, bar_roll, bar_roll_next, mask)
                 w = load(self.weight, m, s)
                 g_u = g_bar
                 if own and not first:
                     u_next = load(u_ref, m, s + 1) if more else u_now
                     u_roll_next = row_up(u_next) if more else u_roll
-                    above = load(u_ref, m + 1, s)
-                    g_u = self.gradient(u_now, above, u_roll, u_roll_next, cz, cx)
+                    above = load(u_ref, up, s)
+                    g_u = self.gradient(u_now, above, u_roll, u_roll_next, mask)
                 if own:
                     for c in range(chunks):
                         a, b, d = g_u[c]
-                        part = part + w[c] * jnp.sqrt(a * a + b * b + d * d)
+                        square = a * a + b * b + d * d
+                        part = part + w[c] * (square * lax.rsqrt(jnp.maximum(square, TINY)))
             if first and do_p:
                 pz, px, py = ([None] * chunks for _ in range(3))
             else:
@@ -188,13 +178,13 @@
                     x_before = jnp.where(self.first_sub, before[c], px_roll[c])
                     y_before = jnp.where(self.first_lane, py_roll[c - 1] if c else 0.0, py_roll[c])
                     spread = (pz[c] - pz_below[c]) + (px[c] - x_before) + (py[c] - y_before)
-                    shifted = n[c] + spread
-                    updated = (old[c] + primal_step * shifted) * (1.0 / (1.0 + primal_step))
+                    shifted = n[c] + dual_step * spread
+                    updated = old[c] * KEEP_SHARE + shifted * NEW_SHARE
                     change = updated - old[c]
                     new.append(updated)
                     new_bar.append(updated + change)
                     if own:
-                        quad = quad + (old[c] * (0.5 * old[c] - n[c]) + 0.5 * (shifted * shifted))
+                        quad = quad + (old[c] * (old[c] - (n[c] + n[c])) + shifted * shifted)
                         step = step + change * change
                 save(self.u, m, s, new)
                 save(self.bar, m, s, new_bar)
@@ -228,15 +218,15 @@
         lax.fori_loop(low, high, body, 0)
 
 
-def place_rows(cx_ref, first_row, all_rows):
+def place_rows(cx_ref, first_row, ext, all_rows):
     sub = lax.broadcasted_iota(jnp.int32, (SUB, LANE), 0)
-    for s in range(cx_ref.shape[0] // SUB):
-        row = first_row + s * SUB + sub
+    for a, first in enumerate((0, ext - SUB)):
+        row = first_row + first + sub
         inside = jnp.logical_and(row >= 0, row < all_rows - 1)
-        cx_ref[s * SUB : (s + 1) * SUB] = jnp.where(inside, dual_step, 0.0).astype(jnp.float32)
-
-
-def place(odd, base, raw_n, raw_w, edge, state, edge_in, block_in):
+        cx_ref[a] = jnp.where(inside, 1.0, 0.0).astype(jnp.float32)
+
+
+def place(odd, base, units, edge, state, edge_in, block_in):
     noisy, weight = state[:2]
     planes = 2 * edge.shape[1]
     ext = noisy.shape[1]
@@ -245,17 +235,18 @@
     rim = slice(used, ext) if odd else slice(0, HALO)
     for z in range(planes):
         j, b = z // 2, z % 2
-        rows, edge_rows = slice(used * b, used * (b + 1)), slice(HALO * b, HALO * (b + 1))
-        value = raw_w[j][rows]
+        edge_rows = slice(HALO * b, HALO * (b + 1))
+        n_ref, n_base = units[z]
+        w_ref, w_base = units[planes + z]
+        value = w_ref[w_base : w_base + used] * (1.0 / dual_step)
+        in_rim = edge_in
         if block_in is not None:
             value = jnp.where(block_in, value, 1.0)
             in_rim = jnp.logical_and(edge_in, block_in)
-        else:
-            in_rim = edge_in
-        noisy[base + z, body] = raw_n[j][rows]
+        noisy[base + z, body] = n_ref[n_base : n_base + used]
         noisy[base + z, rim] = edge[0, j, edge_rows]
         weight[base + z, body] = value
-        weight[base + z, rim] = jnp.where(in_rim, edge[1, j, edge_rows], 1.0)
+        weight[base + z, rim] = jnp.where(in_rim, edge[1, j, edge_rows] * (1.0 / dual_step), 1.0)
 
 
 def geometry(planes, half, count_z, count_x):
@@ -268,30 +259,34 @@
     return odd == 1, first_plane, first_row, planes * count_z, 2 * half * count_x, edge_in, below, above
 
 
-def split(ref):
-    return [ref.at[j] for j in range(ref.shape[0])]
+def units_of(refs, used):
+    return [
+        (refs[piece], base)
+        for piece, base in unit_rows([ref.shape[0] // used for ref in refs], used)
+    ]
 
 
 def early(counts, *refs):
-    own_n, own_w, par_n, par_w0, par_w1, one_n, one_w, edge_own, edge_par, edge_far = refs[:10]
-    send, stats = refs[10:12]
-    state, (cx_ref, acc) = refs[12:19], refs[19:]
+    own, one, *par = refs[: 2 + PIECES]
+    edge_own, edge_par, edge_far, send, stats = refs[2 + PIECES : 7 + PIECES]
+    state, (cx_ref, acc) = refs[7 + PIECES : 14 + PIECES], refs[14 + PIECES :]
     planes, half = send.shape[0], send.shape[1]
     odd, first_plane, first_row, all_planes, all_rows, edge_in, below, above = geometry(
         planes, half, *counts
     )
-    place_rows(cx_ref, first_row, all_rows)
-    par_w = [par_w0.at[0], par_w1.at[0]]
+    ext = half + 2 * HALO
+    place_rows(cx_ref, first_row, ext, all_rows)
+    own, one, par = (units_of(v, half + HALO) for v in ([own], [one], par))
 
     def when_odd():
-        place(True, 0, split(one_n), split(one_w), edge_far, state, edge_in[0], below)
-        place(True, planes, split(par_n), par_w, edge_par, state, edge_in[0], None)
-        place(True, 2 * planes, split(own_n), split(own_w), edge_own, state, edge_in[0], None)
+        place(True, 0, one, edge_far, state, edge_in[0], below)
+        place(True, planes, par, edge_par, state, edge_in[0], None)
+        place(True, 2 * planes, own, edge_own, state, edge_in[0], None)
 
     def when_even():
-        place(False, planes, split(own_n), split(own_w), edge_own, state, edge_in[1], None)
-        place(False, 2 * planes, split(par_n), par_w, edge_par, state, edge_in[1], None)
-        place(False, 3 * planes, split(one_n), split(one_w), edge_far, state, edge_in[1], above)
+        place(False, planes, own, edge_own, state, edge_in[1], None)
+        place(False, 2 * planes, par, edge_par, state, edge_in[1], None)
+        place(False, 3 * planes, one, edge_far, state, edge_in[1], above)
 
     by_parity(odd, when_odd, when_even)
     acc[...] = jnp.zeros_like(acc)
@@ -334,7 +329,7 @@
 
 def write_stats(stats, acc, before=None):
     for k in range(ITERS):
-        gap = acc[0, k] * (1.0 / dual_step) + acc[1, k]
+        gap = acc[0, k] * dual_step + acc[1, k] * 0.5
         for row, value in ((k, gap), (ITERS + k, acc[2, k])):
             total = jnp.sum(value, axis=0, keepdims=True)
             if before is not None:
@@ -343,19 +338,20 @@
 
 
 def late(counts, *refs):
-    two_n, two_w0, two_w1, edge_far, stats_in = refs[:5]
-    keep, stats = refs[12:14]
-    state, (cx_ref, acc) = refs[14:21], refs[21:]
+    *two, edge_far, stats_in = refs[: PIECES + 2]
+    keep, stats = refs[PIECES + 9 : PIECES + 11]
+    state, (cx_ref, acc) = refs[PIECES + 11 : PIECES + 18], refs[PIECES + 18 :]
     planes, half = keep.shape[0], keep.shape[1]
     odd, first_plane, first_row, all_planes, all_rows, edge_in, below, above = geometry(
         planes, half, *counts
     )
-    place_rows(cx_ref, first_row, all_rows)
-    two_w = [two_w0.at[0], two_w1.at[0]]
+    ext = half + 2 * HALO
+    place_rows(cx_ref, first_row, ext, all_rows)
+    two = units_of(two, half + HALO)
     by_parity(
         odd,
-        lambda: place(True, 3 * planes, split(two_n), two_w, edge_far, state, edge_in[0], above),
-        lambda: place(False, 0, split(two_n), two_w, edge_far, state, edge_in[1], below),
+        lambda: place(True, 3 * planes, two, edge_far, state, edge_in[0], above),
+        lambda: place(False, 0, two, edge_far, state, edge_in[1], below),
     )
     acc[...] = jnp.zeros_like(acc)
     sweep = Sweep(state, cx_ref, acc, first_plane, all_planes)
@@ -421,58 +417,50 @@
     edge_step_two = lambda z, x: (z ^ 1, x + 1 if z % 2 else x - 1)
     ghost_step_one = lambda z, x: (z + 2 if z % 2 else z - 2, x)
     ghost_step_two = lambda z, x: (z - 2 if z % 2 else z + 2, x)
+    edge_step_one_far = lambda z, x: ghost_step_one(*edge_step_one(z, x))
+    edge_step_two_far = lambda z, x: ghost_step_two(*edge_step_two(z, x))
 
     edge = (2, planes // 2, 2 * HALO, cols)
-    raw = (planes // 2, 2 * (half + HALO), cols)
-    chunk = (1,) + raw[1:]
-    near = VMEM((planes, SUB, cols), jnp.float32)
-    whole = VMEM((planes, rows, cols), jnp.float32)
-    send_n, own_n, edge_one, edge_two = vmem_call(
-        pack_first,
-        [raw, raw, edge, edge],
+    used = half + HALO
+    sizes = [-(-(2 * planes - j) // PIECES) for j in range(PIECES)]
+    outs = [(size * used, cols) for size in sizes] + [(2 * planes * used, cols), edge, edge]
+    *send, own, edge_one, edge_two = vmem_call(
+        pack,
+        outs,
         [pltpu.HBM] * 2,
-        scratch=[whole, near, near, pltpu.SemaphoreType.DMA((3,))],
+        scratch=[VMEM((2, planes, rows, cols), jnp.float32), pltpu.SemaphoreType.DMA((2,))],
     )(*(pltpu.with_memory_space_constraint(v, pltpu.HBM) for v in (noisy_volume, tv_weight)))
     edge_par = permute(edge_two, edge_step_two)
-    par_n = permute(send_n, swap)
-    one_n = permute(own_n, ghost_step_one)
-    *send_w, own_w = vmem_call(
-        pack_second,
-        [chunk] * (planes // 2) + [raw],
-        [pltpu.HBM],
-        scratch=[whole, pltpu.SemaphoreType.DMA],
-    )(pltpu.with_memory_space_constraint(tv_weight, pltpu.HBM))
-    par_w = [permute(value, swap) for value in send_w]
+    par = [permute(value, swap) for value in send]
+    one = permute(own, ghost_step_one)
     edge_own = permute(edge_one, edge_step_one)
-    one_w = permute(own_w, ghost_step_one)
-    edge_one_far = permute(edge_own, ghost_step_one)
-    edge_two_far = permute(edge_par, ghost_step_two)
-    two_n = permute(par_n, ghost_step_two)
-    two_w = [permute(value, ghost_step_two) for value in par_w]
+    edge_one_far = permute(edge_one, edge_step_one_far)
+    edge_two_far = permute(edge_two, edge_step_two_far)
+    two = [permute(value, ghost_step_two) for value in par]
 
     out_half = (planes, half, cols)
     stats_shape = (2 * ITERS, LANE)
     counts = (count_z, count_x)
-    small = [VMEM((ext, LANE), jnp.float32), VMEM((3, ITERS, SUB, LANE), jnp.float32)]
+    small = [VMEM((2, SUB, LANE), jnp.float32), VMEM((3, ITERS, SUB, LANE), jnp.float32)]
     states = [(4 * planes, ext, cols)] * 7
     send, stats, *state = vmem_call(
         functools.partial(early, counts),
         [out_half, stats_shape] + states,
-        [VMEM] * 10,
+        [VMEM] * (5 + PIECES),
         scratch=small,
         flops=100 << 20,
         limit=24,
-    )(own_n, own_w, par_n, *par_w, one_n, one_w, edge_own, edge_par, edge_one_far)
+    )(own, one, *par, edge_own, edge_par, edge_one_far)
     got = permute(send, swap)
     keep, stats, *_ = vmem_call(
         functools.partial(late, counts),
         [out_half, stats_shape] + states,
-        [VMEM] * 12,
+        [VMEM] * (9 + PIECES),
         scratch=small,
         flops=50 << 20,
         limit=24,
-        aliases={5 + a: 2 + a for a in range(7)},
-    )(two_n, *two_w, edge_two_far, stats, *state)
+        aliases={2 + PIECES + a: 2 + a for a in range(7)},
+    )(*two, edge_two_far, stats, *state)
 
     if count_z & (count_z - 1) or count_x & (count_x - 1):
         stats = lax.psum(stats, both)

time: 92 us -> 117 us (1.27)
  Pallas kernels: 19.4 us -> 34.5 us
  starting transfers between devices: 41.2 us -> 49.1 us
  waiting for transfers between devices: 29.6 us -> 31.7 us
    pallas_call x1, Pallas kernels: 10.6 us -> 21.1 us  [shards(): vmem_call(functools.partial(early, counts), [out_half, stats_shape] + sta...]
    ppermute x18 -> x17, starting transfers between devices: 41.2 us -> 49.1 us  [permute(): return lax.ppermute(value, both, pairs)]
    pallas_call x1, Pallas kernels: 5.1 us -> 10.6 us  [shards(): vmem_call(functools.partial(late, counts), [out_half, stats_shape] + stat...]
    ppermute x18 -> x17, waiting for transfers between devices: 29.6 us -> 31.7 us  [permute(): return lax.ppermute(value, both, pairs)]
    pallas_call x2 -> x1, Pallas kernels: 2.67 us -> 1.74 us  [shards(): vmem_call(pack, outs, [pltpu.HBM] * 2, scratch=[VMEM((2, planes, rows, co...]
  transfers between devices with their start and end apart: 18 -> 17, of which waited for: 9 -> 10; matrix products, arithmetic and copies ran while one was open for 0% -> 1% of each run, Pallas kernels for 20% -> 18%
where the time goes in v4:
time: 117 us
  starting transfers between devices  49.1 us (42%)
  Pallas kernels  34.5 us (29%)
  waiting for transfers between devices  31.7 us (27%)
    ppermute x17, starting transfers between devices, permute(): return lax.ppermute(value, both, pairs)  49.1 us
    ppermute x17, waiting for transfers between devices, permute(): return lax.ppermute(value, both, pairs)  31.7 us
    pallas_call x1, Pallas kernels, shards(): vmem_call(functools.partial(early, counts), [out_half, stats_shape] + sta...  21.1 us
    pallas_call x1, Pallas kernels, shards(): vmem_call(functools.partial(late, counts), [out_half, stats_shape] + stat...  10.6 us
  transfers between devices with their start and end apart: 17, of which 10 were waited for; matrix products, arithmetic and copies ran while one was open for 1% of the time, Pallas kernels for 18%

profile of v4, /device:TPU:0, one launch (start us, length us, event | category | flops | bytes accessed | tf_op | source)
XLA Modules:
  0.0 116.8 jit_solution(3777060024356542523)
XLA Ops:
  0.6 1.7 %shard_map.49 = (f32[204,512]{1,0:T(8,128)S(1)}, f32[204,512]{1,0:T(8,128)S(1)}, f32[136,512]{1,0:T(8,128)S(1)}, f32[544,512]{1,0:T(8,128)S(1)}, f32[2,2,8,512]{...) custom-call(f32[4,128,512]{2,1,0:T(8,128)} %noisy.1, f32[4,128,512]{2,1,0:T(8,128)} %weight.1), custom_call_target="tpu_custom_call" | custom-call | flops 1048576 | bytes 1048576 | tf_op jit(solution)/shard_map/pallas_call | solution.py:427
  2.4 1.3 %collective-permute-start.7 = (f32[544,512]{1,0:T(8,128)S(1)}, f32[544,512]{1,0:T(8,128)S(1)}, u32[]{:S(2)}, u32[]{:S(2)}) collective-permute-start(f32[544,512]{1,0:T(8,128)S(1)} %get-tuple-element.24.refs_0_), channel_id=1, source_target_pairs={{4,12},{5,13},{6,14},{7,15},{8,0},{9,1},{10,2},{11,3},{12,20},{13,... | collective-permute-start | bytes 3342344 | tf_op jit(solution)/shard_map/ppermute | solution.py:413
  3.7 5.3 %collective-permute-start = (f32[204,512]{1,0:T(8,128)S(1)}, f32[204,512]{1,0:T(8,128)S(1)}, u32[]{:S(2)}, u32[]{:S(2)}) collective-permute-start(f32[204,512]{1,0:T(8,128)S(1)} %get-tuple-element.20), channel_id=1, source_target_pairs={{0,4},{1,5},{2,6},{3,7},{4,0},{5,1},{6,2},{7,3},{8,12},{9,13},{10,... | collective-permute-start | bytes 1253384 | tf_op jit(solution)/shard_map/ppermute | solution.py:413
  9.0 0.1 collective-permute-start.2
  9.1 1.9 %collective-permute-start.4 = (f32[136,512]{1,0:T(8,128)S(1)}, f32[136,512]{1,0:T(8,128)S(1)}, u32[]{:S(2)}, u32[]{:S(2)}) collective-permute-start(f32[136,512]{1,0:T(8,128)S(1)} %get-tuple-element.22), channel_id=1, source_target_pairs={{0,4},{1,5},{2,6},{3,7},{4,0},{5,1},{6,2},{7,3},{8,12},{9,13},{10,... | collective-permute-start | bytes 835592 | tf_op jit(solution)/shard_map/ppermute | solution.py:413
  11.0 8.6 %collective-permute-done.refs_2_ = f32[204,512]{1,0:T(8,128)S(1)} collective-permute-done((f32[204,512]{1,0:T(8,128)S(1)}, f32[204,512]{1,0:T(8,128)S(1)}, u32[]{:S(2)}, u32[]{:S(2)}) %collective-permute-start) | collective-permute-done | bytes 417824 | tf_op jit(solution)/shard_map/ppermute | solution.py:413
  19.6 3.4 %collective-permute-start.1 = (f32[204,512]{1,0:T(8,128)S(1)}, f32[204,512]{1,0:T(8,128)S(1)}, u32[]{:S(2)}, u32[]{:S(2)}) collective-permute-start(f32[204,512]{1,0:T(8,128)S(1)} %collective-permute-done.refs_2_), channel_id=1, source_target_pairs={{0,8},{1,9},{2,10},{3,11},{8,16},{9,17},{10,18},{11,19},{12,4},{13... | collective-permute-start | bytes 1253384 | tf_op jit(solution)/shard_map/ppermute | solution.py:413
  23.1 5.7 %collective-permute-done.2.refs_3_ = f32[204,512]{1,0:T(8,128)S(1)} collective-permute-done((f32[204,512]{1,0:T(8,128)S(1)}, f32[204,512]{1,0:T(8,128)S(1)}, u32[]{:S(2)}, u32[]{:S(2)}) %collective-permute-start.2) | collective-permute-done | bytes 417824 | tf_op jit(solution)/shard_map/ppermute | solution.py:413
  28.8 3.4 %collective-permute-start.3 = (f32[204,512]{1,0:T(8,128)S(1)}, f32[204,512]{1,0:T(8,128)S(1)}, u32[]{:S(2)}, u32[]{:S(2)}) collective-permute-start(f32[204,512]{1,0:T(8,128)S(1)} %collective-permute-done.2.refs_3_), channel_id=1, source_target_pairs={{0,8},{1,9},{2,10},{3,11},{8,16},{9,17},{10,18},{11,19},{12,4},{13... | collective-permute-start | bytes 1253384 | tf_op jit(solution)/shard_map/ppermute | solution.py:413
  32.2 1.4 %collective-permute-done.4.refs_4_ = f32[136,512]{1,0:T(8,128)S(1)} collective-permute-done((f32[136,512]{1,0:T(8,128)S(1)}, f32[136,512]{1,0:T(8,128)S(1)}, u32[]{:S(2)}, u32[]{:S(2)}) %collective-permute-start.4) | collective-permute-done | bytes 278560 | tf_op jit(solution)/shard_map/ppermute | solution.py:413
  33.6 3.4 %collective-permute-start.5 = (f32[136,512]{1,0:T(8,128)S(1)}, f32[136,512]{1,0:T(8,128)S(1)}, u32[]{:S(2)}, u32[]{:S(2)}) collective-permute-start(f32[136,512]{1,0:T(8,128)S(1)} %collective-permute-done.4.refs_4_), channel_id=1, source_target_pairs={{0,8},{1,9},{2,10},{3,11},{8,16},{9,17},{10,18},{11,19},{12,4},{13... | collective-permute-start | bytes 835592 | tf_op jit(solution)/shard_map/ppermute | solution.py:413
  37.0 0.7 collective-permute-start.9
  37.7 0.7 collective-permute-start.10
  38.4 10.4 %collective-permute-start.8 = (f32[2,2,8,512]{3,2,1,0:T(8,128)S(1)}, f32[2,2,8,512]{3,2,1,0:T(8,128)S(1)}, u32[]{:S(2)}, u32[]{:S(2)}) collective-permute-start(f32[2,2,8,512]{3,2,1,0:T(8,128)S(1)} %get-tuple-element.25), channel_id=1, source_target_pairs={{0,1},{1,2},{2,3},{5,4},{6,5},{7,6},{8,9},{9,10},{10,11},{13,12},{... | collective-permute-start | bytes 196616 | tf_op jit(solution)/shard_map/ppermute | solution.py:413
  48.8 0.9 collective-permute-done.8.refs_5_
  49.7 0.7 collective-permute-start.6
  50.3 21.1 %shard_map.50 = (f32[4,64,512]{2,1,0:T(8,128)S(1)}, f32[8,128]{1,0:T(8,128)S(1)}, f32[16,72,512]{2,1,0:T(8,128)S(1)}, f32[16,72,512]{2,1,0:T(8,128)S(1)}, f32[16...) custom-call(f32[544,512]{1,0:T(8,128)S(1)} %get-tuple-element.24.ref, ...), custom_call_target="tpu_custom_call" | custom-call | flops 104857600 | bytes 1048576 | tf_op jit(solution)/shard_map/pallas_call | solution.py:446
  71.5 10.6 %shard_map.51 = (f32[4,64,512]{2,1,0:T(8,128)S(1)}, f32[8,128]{1,0:T(8,128)S(1)}, f32[16,72,512]{2,1,0:T(8,128)S(1)}, f32[16,72,512]{2,1,0:T(8,128)S(1)}, f32[16...) custom-call(f32[204,512]{1,0:T(8,128)S(1)} %collective-permute-done., ...), custom_call_target="tpu_custom_call", output_to_operand_aliasing={{2}: (5, {}), {3}: (6, {}), {4}: (7, {}), {5}: (8, {}), {6}... | custom-call | flops 52428800 | bytes 1048576 | tf_op jit(solution)/shard_map/pallas_call | solution.py:455
  82.1 5.2 %collective-permute-start.12 = (f32[8,128]{1,0:T(8,128)S(1)}, f32[8,128]{1,0:T(8,128)S(1)}, u32[]{:S(2)}, u32[]{:S(2)}) collective-permute-start(f32[8,128]{1,0:T(8,128)S(1)} %get-tuple-element.36), channel_id=1, source_target_pairs={{0,1},{1,0},{2,3},{3,2},{4,5},{5,4},{6,7},{7,6},{8,9},{9,8},{10,11... | collective-permute-start | bytes 12296 | tf_op jit(solution)/shard_map/ppermute | solution.py:413
  87.4 0.8 collective-permute-done.12
  88.2 2.6 %collective-permute-start.13 = (f32[8,128]{1,0:T(8,128)S(1)}, f32[8,128]{1,0:T(8,128)S(1)}, u32[]{:S(2)}, u32[]{:S(2)}) collective-permute-start(f32[8,128]{1,0:T(8,128)S(1)} %add.15), channel_id=1, source_target_pairs={{0,2},{1,3},{2,0},{3,1},{4,6},{5,7},{6,4},{7,5},{8,10},{9,11},{10,... | collective-permute-start | bytes 12296 | tf_op jit(solution)/shard_map/ppermute | solution.py:413
  90.8 1.6 %collective-permute-done.13 = f32[8,128]{1,0:T(8,128)S(1)} collective-permute-done((f32[8,128]{1,0:T(8,128)S(1)}, f32[8,128]{1,0:T(8,128)S(1)}, u32[]{:S(2)}, u32[]{:S(2)}) %collective-permute-start.13) | collective-permute-done | bytes 4128 | tf_op jit(solution)/shard_map/ppermute | solution.py:413
  92.4 7.2 %collective-permute-start.14 = (f32[8,128]{1,0:T(8,128)S(1)}, f32[8,128]{1,0:T(8,128)S(1)}, u32[]{:S(2)}, u32[]{:S(2)}) collective-permute-start(f32[8,128]{1,0:T(8,128)S(1)} %add.16), channel_id=1, source_target_pairs={{0,4},{1,5},{2,6},{3,7},{4,0},{5,1},{6,2},{7,3},{8,12},{9,13},{10,... | collective-permute-start | bytes 12296 | tf_op jit(solution)/shard_map/ppermute | solution.py:413
  99.6 1.6 %collective-permute-done.14 = f32[8,128]{1,0:T(8,128)S(1)} collective-permute-done((f32[8,128]{1,0:T(8,128)S(1)}, f32[8,128]{1,0:T(8,128)S(1)}, u32[]{:S(2)}, u32[]{:S(2)}) %collective-permute-start.14) | collective-permute-done | bytes 4128 | tf_op jit(solution)/shard_map/ppermute | solution.py:413
  101.2 0.8 collective-permute-start.15
  101.9 2.8 %collective-permute-done.15 = f32[8,128]{1,0:T(8,128)S(1)} collective-permute-done((f32[8,128]{1,0:T(8,128)S(1)}, f32[8,128]{1,0:T(8,128)S(1)}, u32[]{:S(2)}, u32[]{:S(2)}) %collective-permute-start.15) | collective-permute-done | bytes 4128 | tf_op jit(solution)/shard_map/ppermute | solution.py:413
  104.8 2.0 %collective-permute-start.11 = (f32[4,64,512]{2,1,0:T(8,128)S(1)}, f32[4,64,512]{2,1,0:T(8,128)S(1)}, u32[]{:S(2)}, u32[]{:S(2)}) collective-permute-start(f32[4,64,512]{2,1,0:T(8,128)S(1)} %get-tuple-element.35), channel_id=1, source_target_pairs={{0,4},{1,5},{2,6},{3,7},{4,0},{5,1},{6,2},{7,3},{8,12},{9,13},{10,... | collective-permute-start | bytes 1572872 | tf_op jit(solution)/shard_map/ppermute | solution.py:413
  106.8 2.5 %collective-permute-done.16 = f32[8,128]{1,0:T(8,128)S(1)} collective-permute-done((f32[8,128]{1,0:T(8,128)S(1)}, f32[8,128]{1,0:T(8,128)S(1)}, u32[]{:S(2)}, u32[]{:S(2)}) %collective-permute-start.16) | collective-permute-done | bytes 4128 | tf_op jit(solution)/shard_map/ppermute | solution.py:413
  109.3 0.1 add_reduce_fusion
  109.4 0.6 slice_sqrt_fusion
  110.0 5.8 %collective-permute-done.11.got = f32[4,64,512]{2,1,0:T(8,128)S(1)} collective-permute-done((f32[4,64,512]{2,1,0:T(8,128)S(1)}, f32[4,64,512]{2,1,0:T(8,128)S(1)}, u32[]{:S(2)}, u32[]{:S(2)}) %collective-permute-start.11) | collective-permute-done | bytes 524320 | tf_op jit(solution)/shard_map/ppermute | solution.py:413
  115.8 1.0 shard_map.52
  (13 shorter events, 0.0 us)
Async XLA Ops:
  2.4 48.0 %collective-permute-start.7 = (f32[544,512]{1,0:T(8,128)S(1)}, f32[544,512]{1,0:T(8,128)S(1)}, u32[]{:S(2)}, u32[]{:S(2)}) collective-permute-start(f32[544,512]{1,0:T(8,128)S(1)} %get-tuple-element.24.refs_0_), channel_id=1, source_target_pairs={{4,12},{5,13},{6,14},{7,15},{8,0},{9,1},{10,2},{11,3},{12,20},{13,... | collective-permute-start | bytes 3342344 | tf_op jit(solution)/shard_map/ppermute | solution.py:413
  3.7 16.0 %collective-permute-start = (f32[204,512]{1,0:T(8,128)S(1)}, f32[204,512]{1,0:T(8,128)S(1)}, u32[]{:S(2)}, u32[]{:S(2)}) collective-permute-start(f32[204,512]{1,0:T(8,128)S(1)} %get-tuple-element.20), channel_id=1, source_target_pairs={{0,4},{1,5},{2,6},{3,7},{4,0},{5,1},{6,2},{7,3},{8,12},{9,13},{10,... | collective-permute-start | bytes 1253384 | tf_op jit(solution)/shard_map/ppermute | solution.py:413
  9.0 19.8 %collective-permute-start.2 = (f32[204,512]{1,0:T(8,128)S(1)}, f32[204,512]{1,0:T(8,128)S(1)}, u32[]{:S(2)}, u32[]{:S(2)}) collective-permute-start(f32[204,512]{1,0:T(8,128)S(1)} %get-tuple-element.21), channel_id=1, source_target_pairs={{0,4},{1,5},{2,6},{3,7},{4,0},{5,1},{6,2},{7,3},{8,12},{9,13},{10,... | collective-permute-start | bytes 1253384 | tf_op jit(solution)/shard_map/ppermute | solution.py:413
  9.1 24.6 %collective-permute-start.4 = (f32[136,512]{1,0:T(8,128)S(1)}, f32[136,512]{1,0:T(8,128)S(1)}, u32[]{:S(2)}, u32[]{:S(2)}) collective-permute-start(f32[136,512]{1,0:T(8,128)S(1)} %get-tuple-element.22), channel_id=1, source_target_pairs={{0,4},{1,5},{2,6},{3,7},{4,0},{5,1},{6,2},{7,3},{8,12},{9,13},{10,... | collective-permute-start | bytes 835592 | tf_op jit(solution)/shard_map/ppermute | solution.py:413
  19.6 51.8 %collective-permute-start.1 = (f32[204,512]{1,0:T(8,128)S(1)}, f32[204,512]{1,0:T(8,128)S(1)}, u32[]{:S(2)}, u32[]{:S(2)}) collective-permute-start(f32[204,512]{1,0:T(8,128)S(1)} %collective-permute-done.refs_2_), channel_id=1, source_target_pairs={{0,8},{1,9},{2,10},{3,11},{8,16},{9,17},{10,18},{11,19},{12,4},{13... | collective-permute-start | bytes 1253384 | tf_op jit(solution)/shard_map/ppermute | solution.py:413
  28.8 42.7 %collective-permute-start.3 = (f32[204,512]{1,0:T(8,128)S(1)}, f32[204,512]{1,0:T(8,128)S(1)}, u32[]{:S(2)}, u32[]{:S(2)}) collective-permute-start(f32[204,512]{1,0:T(8,128)S(1)} %collective-permute-done.2.refs_3_), channel_id=1, source_target_pairs={{0,8},{1,9},{2,10},{3,11},{8,16},{9,17},{10,18},{11,19},{12,4},{13... | collective-permute-start | bytes 1253384 | tf_op jit(solution)/shard_map/ppermute | solution.py:413
  33.6 37.8 %collective-permute-start.5 = (f32[136,512]{1,0:T(8,128)S(1)}, f32[136,512]{1,0:T(8,128)S(1)}, u32[]{:S(2)}, u32[]{:S(2)}) collective-permute-start(f32[136,512]{1,0:T(8,128)S(1)} %collective-permute-done.4.refs_4_), channel_id=1, source_target_pairs={{0,8},{1,9},{2,10},{3,11},{8,16},{9,17},{10,18},{11,19},{12,4},{13... | collective-permute-start | bytes 835592 | tf_op jit(solution)/shard_map/ppermute | solution.py:413
  37.0 0.7 collective-permute-start.9
  37.7 0.7 collective-permute-start.10
  38.4 11.3 %collective-permute-start.8 = (f32[2,2,8,512]{3,2,1,0:T(8,128)S(1)}, f32[2,2,8,512]{3,2,1,0:T(8,128)S(1)}, u32[]{:S(2)}, u32[]{:S(2)}) collective-permute-start(f32[2,2,8,512]{3,2,1,0:T(8,128)S(1)} %get-tuple-element.25), channel_id=1, source_target_pairs={{0,1},{1,2},{2,3},{5,4},{6,5},{7,6},{8,9},{9,10},{10,11},{13,12},{... | collective-permute-start | bytes 196616 | tf_op jit(solution)/shard_map/ppermute | solution.py:413
  49.7 21.8 %collective-permute-start.6 = (f32[2,2,8,512]{3,2,1,0:T(8,128)S(1)}, f32[2,2,8,512]{3,2,1,0:T(8,128)S(1)}, u32[]{:S(2)}, u32[]{:S(2)}) collective-permute-start(f32[2,2,8,512]{3,2,1,0:T(8,128)S(1)} %get-tuple-element.23), channel_id=1, source_target_pairs={{4,9},{5,10},{6,11},{9,4},{10,5},{11,6},{12,17},{13,18},{14,19},{1... | collective-permute-start | bytes 196616 | tf_op jit(solution)/shard_map/ppermute | solution.py:413
  82.1 6.1 %collective-permute-start.12 = (f32[8,128]{1,0:T(8,128)S(1)}, f32[8,128]{1,0:T(8,128)S(1)}, u32[]{:S(2)}, u32[]{:S(2)}) collective-permute-start(f32[8,128]{1,0:T(8,128)S(1)} %get-tuple-element.36), channel_id=1, source_target_pairs={{0,1},{1,0},{2,3},{3,2},{4,5},{5,4},{6,7},{7,6},{8,9},{9,8},{10,11... | collective-permute-start | bytes 12296 | tf_op jit(solution)/shard_map/ppermute | solution.py:413
  88.2 4.2 %collective-permute-start.13 = (f32[8,128]{1,0:T(8,128)S(1)}, f32[8,128]{1,0:T(8,128)S(1)}, u32[]{:S(2)}, u32[]{:S(2)}) collective-permute-start(f32[8,128]{1,0:T(8,128)S(1)} %add.15), channel_id=1, source_target_pairs={{0,2},{1,3},{2,0},{3,1},{4,6},{5,7},{6,4},{7,5},{8,10},{9,11},{10,... | collective-permute-start | bytes 12296 | tf_op jit(solution)/shard_map/ppermute | solution.py:413
  92.4 8.8 %collective-permute-start.14 = (f32[8,128]{1,0:T(8,128)S(1)}, f32[8,128]{1,0:T(8,128)S(1)}, u32[]{:S(2)}, u32[]{:S(2)}) collective-permute-start(f32[8,128]{1,0:T(8,128)S(1)} %add.16), channel_id=1, source_target_pairs={{0,4},{1,5},{2,6},{3,7},{4,0},{5,1},{6,2},{7,3},{8,12},{9,13},{10,... | collective-permute-start | bytes 12296 | tf_op jit(solution)/shard_map/ppermute | solution.py:413
  101.2 3.6 %collective-permute-start.15 = (f32[8,128]{1,0:T(8,128)S(1)}, f32[8,128]{1,0:T(8,128)S(1)}, u32[]{:S(2)}, u32[]{:S(2)}) collective-permute-start(f32[8,128]{1,0:T(8,128)S(1)} %add.17), channel_id=1, source_target_pairs={{0,8},{1,9},{2,10},{3,11},{4,12},{5,13},{6,14},{7,15},{8,0},{9,1},... | collective-permute-start | bytes 12296 | tf_op jit(solution)/shard_map/ppermute | solution.py:413
  104.8 4.5 %collective-permute-start.16 = (f32[8,128]{1,0:T(8,128)S(1)}, f32[8,128]{1,0:T(8,128)S(1)}, u32[]{:S(2)}, u32[]{:S(2)}) collective-permute-start(f32[8,128]{1,0:T(8,128)S(1)} %add.18), channel_id=1, source_target_pairs={{0,16},{1,17},{2,18},{3,19},{4,20},{5,21},{6,22},{7,23},{8,24},{9,... | collective-permute-start | bytes 12296 | tf_op jit(solution)/shard_map/ppermute | solution.py:413
  104.8 11.0 %collective-permute-start.11 = (f32[4,64,512]{2,1,0:T(8,128)S(1)}, f32[4,64,512]{2,1,0:T(8,128)S(1)}, u32[]{:S(2)}, u32[]{:S(2)}) collective-permute-start(f32[4,64,512]{2,1,0:T(8,128)S(1)} %get-tuple-element.35), channel_id=1, source_target_pairs={{0,4},{1,5},{2,6},{3,7},{4,0},{5,1},{6,2},{7,3},{8,12},{9,13},{10,... | collective-permute-start | bytes 1572872 | tf_op jit(solution)/shard_map/ppermute | solution.py:413

commit v5 on v4

--- a/solution.py
+++ b/solution.py
@@ -98,13 +98,13 @@
         for c in range(self.chunks):
             ref[m, s * SUB : (s + 1) * SUB, c * LANE : (c + 1) * LANE] = values[c]
 
-    def gradient(self, x, above, rolled, rolled_next, mask):
+    def gradient(self, x, above, rolled, rolled_next, z_mask, mask):
         side = [pltpu.roll(v, LANE - 1, 1) for v in x]
         out = []
         for c in range(self.chunks):
             last = c + 1 == self.chunks
             y_next = side[c] if last else jnp.where(self.last_lane, side[c + 1], side[c])
-            d_z = above[c] - x[c]
+            d_z = (above[c] - x[c]) * z_mask
             d_x = jnp.where(self.last_sub, rolled_next[c], rolled[c]) - x[c]
             if mask is not None:
                 d_x = d_x * mask
@@ -118,7 +118,7 @@
         u_ref, bar_ref = (self.noisy, self.noisy) if first else (self.u, self.bar)
         plane = self.first_plane + m
         z_in = jnp.logical_and(plane >= 0, plane < self.all_planes - 1)
-        up = jnp.where(z_in, m + 1, m)
+        z_mask = jnp.where(z_in, 1.0, 0.0).astype(jnp.float32)
         zero = jnp.zeros((SUB, LANE), jnp.float32)
         tv_sum, quad_sum, step_sum = zero, zero, zero
         load, save, strips, chunks = self.load, self.save, self.strips, self.chunks
@@ -138,15 +138,15 @@
                 mask = self.cx_ref[0 if s == 0 else 1] if edge else None
                 bar_next = load(bar_ref, m, s + 1) if more else bar_now
                 bar_roll_next = row_up(bar_next) if more else bar_roll
-                above = load(bar_ref, up, s)
-                g_bar = self.gradient(bar_now, above, bar_roll, bar_roll_next, mask)
+                above = load(bar_ref, m + 1, s)
+                g_bar = self.gradient(bar_now, above, bar_roll, bar_roll_next, z_mask, mask)
                 w = load(self.weight, m, s)
                 g_u = g_bar
                 if own and not first:
                     u_next = load(u_ref, m, s + 1) if more else u_now
                     u_roll_next = row_up(u_next) if more else u_roll
-                    above = load(u_ref, up, s)
-                    g_u = self.gradient(u_now, above, u_roll, u_roll_next, mask)
+                    above = load(u_ref, m + 1, s)
+                    g_u = self.gradient(u_now, above, u_roll, u_roll_next, z_mask, mask)
                 if own:
                     for c in range(chunks):
                         a, b, d = g_u[c]

time: 117 us -> 98.8 us (0.84)
  Pallas kernels: 34.5 us -> 17.5 us
  starting transfers between devices: 49.1 us -> 47.2 us
    pallas_call x1, Pallas kernels: 21.1 us -> 9.82 us  [shards(): vmem_call(functools.partial(early, counts), [out_half, stats_shape] + sta...]
    pallas_call x1, Pallas kernels: 10.6 us -> 4.88 us  [shards(): vmem_call(functools.partial(late, counts), [out_half, stats_shape] + stat...]
    ppermute x17, starting transfers between devices: 49.1 us -> 47.2 us  [permute(): return lax.ppermute(value, both, pairs)]
  transfers between devices with their start and end apart: 17 -> 17, of which waited for: 10 -> 10; matrix products, arithmetic and copies ran while one was open for 1% -> 1% of each run, Pallas kernels for 18% -> 10%
where the time goes in v5:
time: 98.8 us; the launch traced here: 98.5 us
  starting transfers between devices  47.2 us (48%)
  waiting for transfers between devices  32.3 us (33%)
  Pallas kernels  17.5 us (18%)
    ppermute x17, starting transfers between devices, permute(): return lax.ppermute(value, both, pairs)  47.2 us
    ppermute x17, waiting for transfers between devices, permute(): return lax.ppermute(value, both, pairs)  32.3 us
    pallas_call x1, Pallas kernels, shards(): vmem_call(functools.partial(early, counts), [out_half, stats_shape] + sta...  9.82 us
    pallas_call x1, Pallas kernels, shards(): vmem_call(functools.partial(late, counts), [out_half, stats_shape] + stat...  4.88 us
  transfers between devices with their start and end apart: 17, of which 10 were waited for; matrix products, arithmetic and copies ran while one was open for 1% of the time, Pallas kernels for 10%

profile of v5, /device:TPU:0, one launch (start us, length us, event | category | flops | bytes accessed | tf_op | source)
XLA Modules:
  0.0 98.5 jit_solution(5028913799472838457)
XLA Ops:
  0.6 1.7 %shard_map.49 = (f32[204,512]{1,0:T(8,128)S(1)}, f32[204,512]{1,0:T(8,128)S(1)}, f32[136,512]{1,0:T(8,128)S(1)}, f32[544,512]{1,0:T(8,128)S(1)}, f32[2,2,8,512]{...) custom-call(f32[4,128,512]{2,1,0:T(8,128)} %noisy.1, f32[4,128,512]{2,1,0:T(8,128)} %weight.1), custom_call_target="tpu_custom_call" | custom-call | flops 1048576 | bytes 1048576 | tf_op jit(solution)/shard_map/pallas_call | solution.py:427
  2.4 1.3 %collective-permute-start.7 = (f32[544,512]{1,0:T(8,128)S(1)}, f32[544,512]{1,0:T(8,128)S(1)}, u32[]{:S(2)}, u32[]{:S(2)}) collective-permute-start(f32[544,512]{1,0:T(8,128)S(1)} %get-tuple-element.24.refs_0_), channel_id=1, source_target_pairs={{4,12},{5,13},{6,14},{7,15},{8,0},{9,1},{10,2},{11,3},{12,20},{13,... | collective-permute-start | bytes 3342344 | tf_op jit(solution)/shard_map/ppermute | solution.py:413
  3.7 5.3 %collective-permute-start = (f32[204,512]{1,0:T(8,128)S(1)}, f32[204,512]{1,0:T(8,128)S(1)}, u32[]{:S(2)}, u32[]{:S(2)}) collective-permute-start(f32[204,512]{1,0:T(8,128)S(1)} %get-tuple-element.20), channel_id=1, source_target_pairs={{0,4},{1,5},{2,6},{3,7},{4,0},{5,1},{6,2},{7,3},{8,12},{9,13},{10,... | collective-permute-start | bytes 1253384 | tf_op jit(solution)/shard_map/ppermute | solution.py:413
  9.1 1.9 %collective-permute-start.4 = (f32[136,512]{1,0:T(8,128)S(1)}, f32[136,512]{1,0:T(8,128)S(1)}, u32[]{:S(2)}, u32[]{:S(2)}) collective-permute-start(f32[136,512]{1,0:T(8,128)S(1)} %get-tuple-element.22), channel_id=1, source_target_pairs={{0,4},{1,5},{2,6},{3,7},{4,0},{5,1},{6,2},{7,3},{8,12},{9,13},{10,... | collective-permute-start | bytes 835592 | tf_op jit(solution)/shard_map/ppermute | solution.py:413
  11.0 8.6 %collective-permute-done.refs_2_ = f32[204,512]{1,0:T(8,128)S(1)} collective-permute-done((f32[204,512]{1,0:T(8,128)S(1)}, f32[204,512]{1,0:T(8,128)S(1)}, u32[]{:S(2)}, u32[]{:S(2)}) %collective-permute-start) | collective-permute-done | bytes 417824 | tf_op jit(solution)/shard_map/ppermute | solution.py:413
  19.6 3.4 %collective-permute-start.1 = (f32[204,512]{1,0:T(8,128)S(1)}, f32[204,512]{1,0:T(8,128)S(1)}, u32[]{:S(2)}, u32[]{:S(2)}) collective-permute-start(f32[204,512]{1,0:T(8,128)S(1)} %collective-permute-done.refs_2_), channel_id=1, source_target_pairs={{0,8},{1,9},{2,10},{3,11},{8,16},{9,17},{10,18},{11,19},{12,4},{13... | collective-permute-start | bytes 1253384 | tf_op jit(solution)/shard_map/ppermute | solution.py:413
  23.1 5.7 %collective-permute-done.2.refs_3_ = f32[204,512]{1,0:T(8,128)S(1)} collective-permute-done((f32[204,512]{1,0:T(8,128)S(1)}, f32[204,512]{1,0:T(8,128)S(1)}, u32[]{:S(2)}, u32[]{:S(2)}) %collective-permute-start.2) | collective-permute-done | bytes 417824 | tf_op jit(solution)/shard_map/ppermute | solution.py:413
  28.8 3.4 %collective-permute-start.3 = (f32[204,512]{1,0:T(8,128)S(1)}, f32[204,512]{1,0:T(8,128)S(1)}, u32[]{:S(2)}, u32[]{:S(2)}) collective-permute-start(f32[204,512]{1,0:T(8,128)S(1)} %collective-permute-done.2.refs_3_), channel_id=1, source_target_pairs={{0,8},{1,9},{2,10},{3,11},{8,16},{9,17},{10,18},{11,19},{12,4},{13... | collective-permute-start | bytes 1253384 | tf_op jit(solution)/shard_map/ppermute | solution.py:413
  32.2 1.4 %collective-permute-done.4.refs_4_ = f32[136,512]{1,0:T(8,128)S(1)} collective-permute-done((f32[136,512]{1,0:T(8,128)S(1)}, f32[136,512]{1,0:T(8,128)S(1)}, u32[]{:S(2)}, u32[]{:S(2)}) %collective-permute-start.4) | collective-permute-done | bytes 278560 | tf_op jit(solution)/shard_map/ppermute | solution.py:413
  33.6 3.4 %collective-permute-start.5 = (f32[136,512]{1,0:T(8,128)S(1)}, f32[136,512]{1,0:T(8,128)S(1)}, u32[]{:S(2)}, u32[]{:S(2)}) collective-permute-start(f32[136,512]{1,0:T(8,128)S(1)} %collective-permute-done.4.refs_4_), channel_id=1, source_target_pairs={{0,8},{1,9},{2,10},{3,11},{8,16},{9,17},{10,18},{11,19},{12,4},{13... | collective-permute-start | bytes 835592 | tf_op jit(solution)/shard_map/ppermute | solution.py:413
  37.0 0.7 collective-permute-start.9
  37.7 0.7 collective-permute-start.10
  38.4 10.4 %collective-permute-start.8 = (f32[2,2,8,512]{3,2,1,0:T(8,128)S(1)}, f32[2,2,8,512]{3,2,1,0:T(8,128)S(1)}, u32[]{:S(2)}, u32[]{:S(2)}) collective-permute-start(f32[2,2,8,512]{3,2,1,0:T(8,128)S(1)} %get-tuple-element.25), channel_id=1, source_target_pairs={{0,1},{1,2},{2,3},{5,4},{6,5},{7,6},{8,9},{9,10},{10,11},{13,12},{... | collective-permute-start | bytes 196616 | tf_op jit(solution)/shard_map/ppermute | solution.py:413
  48.8 0.9 collective-permute-done.8.refs_5_
  49.7 0.7 collective-permute-start.6
  50.3 9.8 %shard_map.50 = (f32[4,64,512]{2,1,0:T(8,128)S(1)}, f32[8,128]{1,0:T(8,128)S(1)}, f32[16,72,512]{2,1,0:T(8,128)S(1)}, f32[16,72,512]{2,1,0:T(8,128)S(1)}, f32[16...) custom-call(f32[544,512]{1,0:T(8,128)S(1)} %get-tuple-element.24.ref, ...), custom_call_target="tpu_custom_call" | custom-call | flops 104857600 | bytes 1048576 | tf_op jit(solution)/shard_map/pallas_call | solution.py:446
  60.2 4.9 %shard_map.51 = (f32[4,64,512]{2,1,0:T(8,128)S(1)}, f32[8,128]{1,0:T(8,128)S(1)}, f32[16,72,512]{2,1,0:T(8,128)S(1)}, f32[16,72,512]{2,1,0:T(8,128)S(1)}, f32[16...) custom-call(f32[204,512]{1,0:T(8,128)S(1)} %collective-permute-done., ...), custom_call_target="tpu_custom_call", output_to_operand_aliasing={{2}: (5, {}), {3}: (6, {}), {4}: (7, {}), {5}: (8, {}), {6}... | custom-call | flops 52428800 | bytes 1048576 | tf_op jit(solution)/shard_map/pallas_call | solution.py:455
  65.1 5.2 %collective-permute-start.12 = (f32[8,128]{1,0:T(8,128)S(1)}, f32[8,128]{1,0:T(8,128)S(1)}, u32[]{:S(2)}, u32[]{:S(2)}) collective-permute-start(f32[8,128]{1,0:T(8,128)S(1)} %get-tuple-element.36), channel_id=1, source_target_pairs={{0,1},{1,0},{2,3},{3,2},{4,5},{5,4},{6,7},{7,6},{8,9},{9,8},{10,11... | collective-permute-start | bytes 12296 | tf_op jit(solution)/shard_map/ppermute | solution.py:413
  70.3 0.8 collective-permute-done.12
  71.2 2.6 %collective-permute-start.13 = (f32[8,128]{1,0:T(8,128)S(1)}, f32[8,128]{1,0:T(8,128)S(1)}, u32[]{:S(2)}, u32[]{:S(2)}) collective-permute-start(f32[8,128]{1,0:T(8,128)S(1)} %add.15), channel_id=1, source_target_pairs={{0,2},{1,3},{2,0},{3,1},{4,6},{5,7},{6,4},{7,5},{8,10},{9,11},{10,... | collective-permute-start | bytes 12296 | tf_op jit(solution)/shard_map/ppermute | solution.py:413
  73.7 1.6 %collective-permute-done.13 = f32[8,128]{1,0:T(8,128)S(1)} collective-permute-done((f32[8,128]{1,0:T(8,128)S(1)}, f32[8,128]{1,0:T(8,128)S(1)}, u32[]{:S(2)}, u32[]{:S(2)}) %collective-permute-start.13) | collective-permute-done | bytes 4128 | tf_op jit(solution)/shard_map/ppermute | solution.py:413
  75.3 5.4 %collective-permute-start.14 = (f32[8,128]{1,0:T(8,128)S(1)}, f32[8,128]{1,0:T(8,128)S(1)}, u32[]{:S(2)}, u32[]{:S(2)}) collective-permute-start(f32[8,128]{1,0:T(8,128)S(1)} %add.16), channel_id=1, source_target_pairs={{0,4},{1,5},{2,6},{3,7},{4,0},{5,1},{6,2},{7,3},{8,12},{9,13},{10,... | collective-permute-start | bytes 12296 | tf_op jit(solution)/shard_map/ppermute | solution.py:413
  80.7 1.6 %collective-permute-done.14 = f32[8,128]{1,0:T(8,128)S(1)} collective-permute-done((f32[8,128]{1,0:T(8,128)S(1)}, f32[8,128]{1,0:T(8,128)S(1)}, u32[]{:S(2)}, u32[]{:S(2)}) %collective-permute-start.14) | collective-permute-done | bytes 4128 | tf_op jit(solution)/shard_map/ppermute | solution.py:413
  82.3 0.8 collective-permute-start.15
  83.1 2.8 %collective-permute-done.15 = f32[8,128]{1,0:T(8,128)S(1)} collective-permute-done((f32[8,128]{1,0:T(8,128)S(1)}, f32[8,128]{1,0:T(8,128)S(1)}, u32[]{:S(2)}, u32[]{:S(2)}) %collective-permute-start.15) | collective-permute-done | bytes 4128 | tf_op jit(solution)/shard_map/ppermute | solution.py:413
  85.9 1.0 %collective-permute-start.16 = (f32[8,128]{1,0:T(8,128)S(1)}, f32[8,128]{1,0:T(8,128)S(1)}, u32[]{:S(2)}, u32[]{:S(2)}) collective-permute-start(f32[8,128]{1,0:T(8,128)S(1)} %add.18), channel_id=1, source_target_pairs={{0,16},{1,17},{2,18},{3,19},{4,20},{5,21},{6,22},{7,23},{8,24},{9,... | collective-permute-start | bytes 12296 | tf_op jit(solution)/shard_map/ppermute | solution.py:413
  86.9 1.0 %collective-permute-start.11 = (f32[4,64,512]{2,1,0:T(8,128)S(1)}, f32[4,64,512]{2,1,0:T(8,128)S(1)}, u32[]{:S(2)}, u32[]{:S(2)}) collective-permute-start(f32[4,64,512]{2,1,0:T(8,128)S(1)} %get-tuple-element.35), channel_id=1, source_target_pairs={{0,4},{1,5},{2,6},{3,7},{4,0},{5,1},{6,2},{7,3},{8,12},{9,13},{10,... | collective-permute-start | bytes 1572872 | tf_op jit(solution)/shard_map/ppermute | solution.py:413
  87.9 2.5 %collective-permute-done.16 = f32[8,128]{1,0:T(8,128)S(1)} collective-permute-done((f32[8,128]{1,0:T(8,128)S(1)}, f32[8,128]{1,0:T(8,128)S(1)}, u32[]{:S(2)}, u32[]{:S(2)}) %collective-permute-start.16) | collective-permute-done | bytes 4128 | tf_op jit(solution)/shard_map/ppermute | solution.py:413
  90.4 0.1 add_reduce_fusion
  90.5 0.6 slice_sqrt_fusion
  91.1 6.3 %collective-permute-done.11.got = f32[4,64,512]{2,1,0:T(8,128)S(1)} collective-permute-done((f32[4,64,512]{2,1,0:T(8,128)S(1)}, f32[4,64,512]{2,1,0:T(8,128)S(1)}, u32[]{:S(2)}, u32[]{:S(2)}) %collective-permute-start.11) | collective-permute-done | bytes 524320 | tf_op jit(solution)/shard_map/ppermute | solution.py:413
  97.4 1.0 %shard_map.52 = f32[4,128,512]{2,1,0:T(8,128)} custom-call(f32[4,64,512]{2,1,0:T(8,128)S(1)} %get-tuple-element.34.keep, f32[4,64,512]{2,1,0:T(8,128)S(1)} %collective-permute-done.11.got), custom_call_target="tpu_custom_call" | custom-call | flops 1048576 | bytes 1048576 | tf_op jit(solution)/shard_map/pallas_call | solution.py:477
  (13 shorter events, 0.1 us)
Async XLA Ops:
  2.4 48.0 %collective-permute-start.7 = (f32[544,512]{1,0:T(8,128)S(1)}, f32[544,512]{1,0:T(8,128)S(1)}, u32[]{:S(2)}, u32[]{:S(2)}) collective-permute-start(f32[544,512]{1,0:T(8,128)S(1)} %get-tuple-element.24.refs_0_), channel_id=1, source_target_pairs={{4,12},{5,13},{6,14},{7,15},{8,0},{9,1},{10,2},{11,3},{12,20},{13,... | collective-permute-start | bytes 3342344 | tf_op jit(solution)/shard_map/ppermute | solution.py:413
  3.7 16.0 %collective-permute-start = (f32[204,512]{1,0:T(8,128)S(1)}, f32[204,512]{1,0:T(8,128)S(1)}, u32[]{:S(2)}, u32[]{:S(2)}) collective-permute-start(f32[204,512]{1,0:T(8,128)S(1)} %get-tuple-element.20), channel_id=1, source_target_pairs={{0,4},{1,5},{2,6},{3,7},{4,0},{5,1},{6,2},{7,3},{8,12},{9,13},{10,... | collective-permute-start | bytes 1253384 | tf_op jit(solution)/shard_map/ppermute | solution.py:413
  9.0 19.8 %collective-permute-start.2 = (f32[204,512]{1,0:T(8,128)S(1)}, f32[204,512]{1,0:T(8,128)S(1)}, u32[]{:S(2)}, u32[]{:S(2)}) collective-permute-start(f32[204,512]{1,0:T(8,128)S(1)} %get-tuple-element.21), channel_id=1, source_target_pairs={{0,4},{1,5},{2,6},{3,7},{4,0},{5,1},{6,2},{7,3},{8,12},{9,13},{10,... | collective-permute-start | bytes 1253384 | tf_op jit(solution)/shard_map/ppermute | solution.py:413
  9.1 24.6 %collective-permute-start.4 = (f32[136,512]{1,0:T(8,128)S(1)}, f32[136,512]{1,0:T(8,128)S(1)}, u32[]{:S(2)}, u32[]{:S(2)}) collective-permute-start(f32[136,512]{1,0:T(8,128)S(1)} %get-tuple-element.22), channel_id=1, source_target_pairs={{0,4},{1,5},{2,6},{3,7},{4,0},{5,1},{6,2},{7,3},{8,12},{9,13},{10,... | collective-permute-start | bytes 835592 | tf_op jit(solution)/shard_map/ppermute | solution.py:413
  19.6 40.6 %collective-permute-start.1 = (f32[204,512]{1,0:T(8,128)S(1)}, f32[204,512]{1,0:T(8,128)S(1)}, u32[]{:S(2)}, u32[]{:S(2)}) collective-permute-start(f32[204,512]{1,0:T(8,128)S(1)} %collective-permute-done.refs_2_), channel_id=1, source_target_pairs={{0,8},{1,9},{2,10},{3,11},{8,16},{9,17},{10,18},{11,19},{12,4},{13... | collective-permute-start | bytes 1253384 | tf_op jit(solution)/shard_map/ppermute | solution.py:413
  28.8 31.4 %collective-permute-start.3 = (f32[204,512]{1,0:T(8,128)S(1)}, f32[204,512]{1,0:T(8,128)S(1)}, u32[]{:S(2)}, u32[]{:S(2)}) collective-permute-start(f32[204,512]{1,0:T(8,128)S(1)} %collective-permute-done.2.refs_3_), channel_id=1, source_target_pairs={{0,8},{1,9},{2,10},{3,11},{8,16},{9,17},{10,18},{11,19},{12,4},{13... | collective-permute-start | bytes 1253384 | tf_op jit(solution)/shard_map/ppermute | solution.py:413
  33.6 26.6 %collective-permute-start.5 = (f32[136,512]{1,0:T(8,128)S(1)}, f32[136,512]{1,0:T(8,128)S(1)}, u32[]{:S(2)}, u32[]{:S(2)}) collective-permute-start(f32[136,512]{1,0:T(8,128)S(1)} %collective-permute-done.4.refs_4_), channel_id=1, source_target_pairs={{0,8},{1,9},{2,10},{3,11},{8,16},{9,17},{10,18},{11,19},{12,4},{13... | collective-permute-start | bytes 835592 | tf_op jit(solution)/shard_map/ppermute | solution.py:413
  37.0 0.7 collective-permute-start.9
  37.7 0.7 collective-permute-start.10
  38.4 11.3 %collective-permute-start.8 = (f32[2,2,8,512]{3,2,1,0:T(8,128)S(1)}, f32[2,2,8,512]{3,2,1,0:T(8,128)S(1)}, u32[]{:S(2)}, u32[]{:S(2)}) collective-permute-start(f32[2,2,8,512]{3,2,1,0:T(8,128)S(1)} %get-tuple-element.25), channel_id=1, source_target_pairs={{0,1},{1,2},{2,3},{5,4},{6,5},{7,6},{8,9},{9,10},{10,11},{13,12},{... | collective-permute-start | bytes 196616 | tf_op jit(solution)/shard_map/ppermute | solution.py:413
  49.7 10.5 %collective-permute-start.6 = (f32[2,2,8,512]{3,2,1,0:T(8,128)S(1)}, f32[2,2,8,512]{3,2,1,0:T(8,128)S(1)}, u32[]{:S(2)}, u32[]{:S(2)}) collective-permute-start(f32[2,2,8,512]{3,2,1,0:T(8,128)S(1)} %get-tuple-element.23), channel_id=1, source_target_pairs={{4,9},{5,10},{6,11},{9,4},{10,5},{11,6},{12,17},{13,18},{14,19},{1... | collective-permute-start | bytes 196616 | tf_op jit(solution)/shard_map/ppermute | solution.py:413
  65.1 6.1 %collective-permute-start.12 = (f32[8,128]{1,0:T(8,128)S(1)}, f32[8,128]{1,0:T(8,128)S(1)}, u32[]{:S(2)}, u32[]{:S(2)}) collective-permute-start(f32[8,128]{1,0:T(8,128)S(1)} %get-tuple-element.36), channel_id=1, source_target_pairs={{0,1},{1,0},{2,3},{3,2},{4,5},{5,4},{6,7},{7,6},{8,9},{9,8},{10,11... | collective-permute-start | bytes 12296 | tf_op jit(solution)/shard_map/ppermute | solution.py:413
  71.2 4.2 %collective-permute-start.13 = (f32[8,128]{1,0:T(8,128)S(1)}, f32[8,128]{1,0:T(8,128)S(1)}, u32[]{:S(2)}, u32[]{:S(2)}) collective-permute-start(f32[8,128]{1,0:T(8,128)S(1)} %add.15), channel_id=1, source_target_pairs={{0,2},{1,3},{2,0},{3,1},{4,6},{5,7},{6,4},{7,5},{8,10},{9,11},{10,... | collective-permute-start | bytes 12296 | tf_op jit(solution)/shard_map/ppermute | solution.py:413
  75.3 6.9 %collective-permute-start.14 = (f32[8,128]{1,0:T(8,128)S(1)}, f32[8,128]{1,0:T(8,128)S(1)}, u32[]{:S(2)}, u32[]{:S(2)}) collective-permute-start(f32[8,128]{1,0:T(8,128)S(1)} %add.16), channel_id=1, source_target_pairs={{0,4},{1,5},{2,6},{3,7},{4,0},{5,1},{6,2},{7,3},{8,12},{9,13},{10,... | collective-permute-start | bytes 12296 | tf_op jit(solution)/shard_map/ppermute | solution.py:413
  82.3 3.6 %collective-permute-start.15 = (f32[8,128]{1,0:T(8,128)S(1)}, f32[8,128]{1,0:T(8,128)S(1)}, u32[]{:S(2)}, u32[]{:S(2)}) collective-permute-start(f32[8,128]{1,0:T(8,128)S(1)} %add.17), channel_id=1, source_target_pairs={{0,8},{1,9},{2,10},{3,11},{4,12},{5,13},{6,14},{7,15},{8,0},{9,1},... | collective-permute-start | bytes 12296 | tf_op jit(solution)/shard_map/ppermute | solution.py:413
  85.9 4.5 %collective-permute-start.16 = (f32[8,128]{1,0:T(8,128)S(1)}, f32[8,128]{1,0:T(8,128)S(1)}, u32[]{:S(2)}, u32[]{:S(2)}) collective-permute-start(f32[8,128]{1,0:T(8,128)S(1)} %add.18), channel_id=1, source_target_pairs={{0,16},{1,17},{2,18},{3,19},{4,20},{5,21},{6,22},{7,23},{8,24},{9,... | collective-permute-start | bytes 12296 | tf_op jit(solution)/shard_map/ppermute | solution.py:413
  86.9 10.5 %collective-permute-start.11 = (f32[4,64,512]{2,1,0:T(8,128)S(1)}, f32[4,64,512]{2,1,0:T(8,128)S(1)}, u32[]{:S(2)}, u32[]{:S(2)}) collective-permute-start(f32[4,64,512]{2,1,0:T(8,128)S(1)} %get-tuple-element.35), channel_id=1, source_target_pairs={{0,4},{1,5},{2,6},{3,7},{4,0},{5,1},{6,2},{7,3},{8,12},{9,13},{10,... | collective-permute-start | bytes 1572872 | tf_op jit(solution)/shard_map/ppermute | solution.py:413
